TPU v7x, 512 devices: a 8x2x16 block of a 8x8x16 slice. The times are simulated.
512 devices in a mesh: groups: 2 (over y), inst: 16 (over z), tp: 8 (over x), rep: 2 (over core).
Axes of the slice: x: 8, y: 2, z: 16, core: 2. Of those that a mesh axis runs over, the one named last changes fastest.
The devices are a block of a 8x8x16 slice.
Arguments:
- queries: bfloat16 [32, 128, 8192], P(('groups', 'rep'), 'inst', 'tp'), parts along dimension 0, may hold values from -8 to 8, as said below
- tool_key_value: bfloat16 [32, 128, 2048], P(('groups', 'rep'), 'inst', 'tp'), parts along dimension 0, may hold values from -8 to 8, as said below
- cache: bfloat16 [32, 12288, 2048], P(('groups', 'rep'), 'inst', 'tp'), parts along dimension 0, may hold values from -6 to 6
- placed: int32 [32, 16], P(('groups', 'rep'), 'inst'), parts along dimension 0, may hold values 0 or 1
- blocks: int32 [32, 16], P(('groups', 'rep'), 'inst'), parts along dimension 0, may hold values from 1 to 6
- span_len: int32 [32], P(('groups', 'rep')), parts along dimension 0, may hold values from 32 to 128
- owner: int32 [32], P(('groups', 'rep')), parts along dimension 0, may hold values from 0 to 15, as said below
Outputs:
- attended: bfloat16 [32, 128, 8192], P(('groups', 'rep'), 'inst', 'tp'), parts along dimension 0
- owned: bfloat16 [32, 2, 128, 2048], P(('groups', 'inst'), 'rep', None, 'tp'), parts along dimension 0
There are 2 independent parts, one for each index of `groups`. A program takes and returns all parts, laid end to end along the dimension named above; each array names one. Nothing has to cross between parts.
Inputs may be any that keep to these rules, and one draw needn't show every extreme that they name: real-valued rotated queries. `tool_key_value`: real-valued rotated keys and values. `owner`: the 8 forks of one index of rep have different owners.
All inputs are finite; a program needn't handle non-finite values. No bound on the sum of `placed` on one device may be relied on, other than what follows from the above.
Results may differ from a plain program's by a relative error of at most 0.0022.
Values may be sent and summed in bfloat16 or wider, within the bound.
No kernel may reach another device: no remote copies, remote signals or barrier semaphores. Data moves between devices by JAX's collectives and lax.ppermute only.
A program may use at most 128 MiB of HBM per device.

v0:
```python
import math

import jax
import jax.numpy as jnp
from jax import lax
from jax.sharding import PartitionSpec as P

HEAD_DIM = 128
BLOCK = 128


def passed_along(shard, axis, by):
    size = lax.axis_size(axis)
    return lax.ppermute(shard, axis, [(i, (i + by) % size) for i in range(size)])


def copy_for_each(shard, axis):
    size = lax.axis_size(axis)
    return lax.all_to_all(
        jnp.broadcast_to(shard[None], (size, *shard.shape)), axis, 0, 0, tiled=True
    )


def joined_along(tiles, dim):
    tiles = jnp.moveaxis(tiles, 0, dim)
    dims = tiles.shape
    return tiles.reshape(*dims[:dim], dims[dim] * dims[dim + 1], *dims[dim + 2 :])


def gathered_copies(shard, axis, dim):
    tiles = copy_for_each(shard, axis)
    return joined_along(tiles, dim)


def block_partial(query_block, first_token, myself, stores):
    key_cache, value_cache, live_len, key_fresh, value_fresh = stores
    rows_here = query_block.shape[1]
    scaling = 1.0 / math.sqrt(HEAD_DIM)
    score_old = (
        jnp.einsum("fcjgd,fpjd->fcjgp", query_block, key_cache, preferred_element_type=jnp.float32)
        * scaling
    )
    score_new = (
        jnp.einsum("fcjgd,fujd->fcjgu", query_block, key_fresh, preferred_element_type=jnp.float32)
        * scaling
    )
    slots = jnp.arange(key_cache.shape[1], dtype=jnp.int32)
    mask_old = (slots[None, :] < live_len[:, None])[:, None, None, None, :]
    query_token = first_token + jnp.arange(rows_here, dtype=jnp.int32)
    key_token = myself * key_fresh.shape[1] + jnp.arange(key_fresh.shape[1], dtype=jnp.int32)
    mask_new = (key_token[None, :] <= query_token[:, None])[None, :, None, None, :]
    highest = jnp.maximum(
        jnp.max(jnp.where(mask_old, score_old, -jnp.inf), axis=-1),
        jnp.max(jnp.where(mask_new, score_new, -jnp.inf), axis=-1),
    )
    safe_max = jnp.where(highest > -jnp.inf, highest, 0.0)
    weight_old = jnp.where(mask_old, jnp.exp(score_old - safe_max[..., None]), 0.0)
    weight_new = jnp.where(mask_new, jnp.exp(score_new - safe_max[..., None]), 0.0)
    total = jnp.sum(weight_old, axis=-1) + jnp.sum(weight_new, axis=-1)
    numer = jnp.einsum(
        "fcjgp,fpjd->fcjgd",
        weight_old.astype(jnp.bfloat16),
        value_cache,
        preferred_element_type=jnp.float32,
    )
    numer = numer + jnp.einsum(
        "fcjgu,fujd->fcjgd",
        weight_new.astype(jnp.bfloat16),
        value_fresh,
        preferred_element_type=jnp.float32,
    )
    return (highest, total, numer)


def merge_parts(first, second):
    max_one, sum_one, acc_one = first
    max_two, sum_two, acc_two = second
    highest = jnp.maximum(max_one, max_two)
    safe_max = jnp.where(highest > -jnp.inf, highest, 0.0)
    scale_one = jnp.exp(max_one - safe_max)
    scale_two = jnp.exp(max_two - safe_max)
    return (
        highest,
        scale_one * sum_one + scale_two * sum_two,
        scale_one[..., None] * acc_one + scale_two[..., None] * acc_two,
    )


def body(queries, tool_key_value, cache, placed, blocks, span_len, owner):
    forks_here, tokens_here, width_kv = tool_key_value.shape
    kv_heads = width_kv // (2 * HEAD_DIM)
    query_group_size = queries.shape[2] // (kv_heads * HEAD_DIM)
    myself = lax.axis_index("inst")
    members = lax.axis_size("inst")
    query_block = queries.reshape(forks_here, tokens_here, kv_heads, query_group_size, HEAD_DIM)
    stored = cache.reshape(forks_here, cache.shape[1], kv_heads, 2, HEAD_DIM)
    fresh = tool_key_value.reshape(forks_here, tokens_here, kv_heads, 2, HEAD_DIM)
    live_len = placed[:, 0] * blocks[:, 0] * BLOCK
    stores = (
        stored[:, :, :, 0, :],
        stored[:, :, :, 1, :],
        live_len,
        fresh[:, :, :, 0, :],
        fresh[:, :, :, 1, :],
    )
    initial = block_partial(query_block, myself * tokens_here, myself, stores)

    def advance(turn_no, carry):
        moving, running = carry
        moving = passed_along(moving, "inst", 1)
        running = passed_along((running[0], running[1], running[2]), "inst", 1)
        anchor = (myself - turn_no) % members
        return (
            moving,
            merge_parts(running, block_partial(moving, anchor * tokens_here, myself, stores)),
        )

    _, running = lax.fori_loop(1, members, advance, (query_block, initial))
    running = passed_along((running[0], running[1], running[2]), "inst", 1)
    total = running[1]
    numer = running[2]
    token_ids = myself * tokens_here + jnp.arange(tokens_here, dtype=jnp.int32)
    valid = token_ids[None, :] < span_len[:, None]
    result = numer / total[..., None]
    result = jnp.where(valid[:, :, None, None, None], result, 0.0)
    attended = result.reshape(forks_here, tokens_here, queries.shape[2]).astype(jnp.bfloat16)
    kept = jnp.where(valid[:, :, None], tool_key_value, jnp.zeros((), jnp.bfloat16))
    whole = gathered_copies(kept, "inst", 1)
    chosen = (owner == myself).astype(jnp.bfloat16)
    owned = jnp.einsum("f,ftk->tk", chosen, whole, preferred_element_type=jnp.float32).astype(
        jnp.bfloat16
    )
    owned = owned.reshape(1, 1, members * tokens_here, width_kv)
    return (attended, owned)


def solution(mesh):
    return jax.shard_map(
        body,
        mesh=mesh,
        in_specs=(
            P(("groups", "rep"), "inst", "tp"),
            P(("groups", "rep"), "inst", "tp"),
            P(("groups", "rep"), "inst", "tp"),
            P(("groups", "rep"), "inst"),
            P(("groups", "rep"), "inst"),
            P(("groups", "rep")),
            P(("groups", "rep")),
        ),
        out_specs=(P(("groups", "rep"), "inst", "tp"), P(("groups", "inst"), "rep", None, "tp")),
        check_vma=False,
    )
```

profile of v0, /device:TPU:80, one launch (start us, length us, event | category | flops | bytes accessed | tf_op | source)
XLA Modules:
  0.0 387.9 jit_solution(4166383978048413307)
XLA Ops:
  3.7 43.7 %all-to-all-start = ((bf16[16,8,8,256]{3,2,1,0:T(8,128)(2,1)}), bf16[16,8,8,256]{3,2,1,0:T(8,128)(2,1)}, u32[]{:S(2)}, u32[]{:S(2)}) async-start(bf16[16,8,8,256]{3,2,1,0:T(8,128)(2,1)} %broadcast_in_dim.213), calls=%async_computation | async-start | bytes 1048576 | tf_op jit(solution)/shard_map/all_to_all | solution.py:19
  48.0 3.2 copy.23
  63.0 310.9 %while.21 = (s32[]{:T(128)}, bf16[8,8,1,8,128]{4,3,1,0,2:T(8,128)(2,1)}, f32[8,8,1,8]{3,1,0,2:T(8,128)}, f32[8,8,1,8]{3,1,0,2:T(8,128)}, f32[8,8,1,8,128]{4,3,1,...) while((s32[]{:T(128)}, ...), condition=%wide.region_9.10_spmd, body=%wide.region_4.9_spmd.sunk | while | flops 207273552 | bytes 11252614 | solution.py:118
  63.0 3.6 collective-permute-start
  66.7 3.4 collective-permute-start.1
  70.1 3.4 collective-permute-start.2
  73.5 4.6 %collective-permute-start.3 = (f32[8,8,1,8,128]{4,3,1,0,2:T(8,128)}, f32[8,8,1,8,128]{4,3,1,0,2:T(8,128)S(1)}, u32[]{:S(2)}, u32[]{:S(2)}) collective-permute-start(f32[8,8,1,8,128]{4,3,1,0,2:T(8,128)} %get-tuple-element.433), channel_id=1, source_target_pairs={{0,16},{16,32},{32,48},{48,64},{64,80},{80,96},{96,112},{112,128},... | collective-permute-start | bytes 786440 | tf_op jit(solution)/shard_map/while/body/eval_jaxpr/ppermute | solution.py:14
  86.0 3.4 collective-permute-start
  89.4 3.4 collective-permute-start.1
  92.8 3.4 collective-permute-start.2
  96.3 4.6 %collective-permute-start.3 = (f32[8,8,1,8,128]{4,3,1,0,2:T(8,128)}, f32[8,8,1,8,128]{4,3,1,0,2:T(8,128)S(1)}, u32[]{:S(2)}, u32[]{:S(2)}) collective-permute-start(f32[8,8,1,8,128]{4,3,1,0,2:T(8,128)} %get-tuple-element.433), channel_id=1, source_target_pairs={{0,16},{16,32},{32,48},{48,64},{64,80},{80,96},{96,112},{112,128},... | collective-permute-start | bytes 786440 | tf_op jit(solution)/shard_map/while/body/eval_jaxpr/ppermute | solution.py:14
  108.8 2.5 collective-permute-start
  111.3 2.5 collective-permute-start.1
  113.8 2.5 collective-permute-start.2
  116.3 3.7 collective-permute-start.3
  128.0 3.1 collective-permute-start
  131.1 2.5 collective-permute-start.1
  133.6 2.5 collective-permute-start.2
  136.1 3.7 collective-permute-start.3
  147.7 2.4 collective-permute-start
  150.1 2.6 collective-permute-start.1
  155.0 4.6 %collective-permute-start.3 = (f32[8,8,1,8,128]{4,3,1,0,2:T(8,128)}, f32[8,8,1,8,128]{4,3,1,0,2:T(8,128)S(1)}, u32[]{:S(2)}, u32[]{:S(2)}) collective-permute-start(f32[8,8,1,8,128]{4,3,1,0,2:T(8,128)} %get-tuple-element.433), channel_id=1, source_target_pairs={{0,16},{16,32},{32,48},{48,64},{64,80},{80,96},{96,112},{112,128},... | collective-permute-start | bytes 786440 | tf_op jit(solution)/shard_map/while/body/eval_jaxpr/ppermute | solution.py:14
  167.5 3.4 collective-permute-start
  170.9 3.4 collective-permute-start.1
  174.3 3.4 collective-permute-start.2
  177.7 4.6 %collective-permute-start.3 = (f32[8,8,1,8,128]{4,3,1,0,2:T(8,128)}, f32[8,8,1,8,128]{4,3,1,0,2:T(8,128)S(1)}, u32[]{:S(2)}, u32[]{:S(2)}) collective-permute-start(f32[8,8,1,8,128]{4,3,1,0,2:T(8,128)} %get-tuple-element.433), channel_id=1, source_target_pairs={{0,16},{16,32},{32,48},{48,64},{64,80},{80,96},{96,112},{112,128},... | collective-permute-start | bytes 786440 | tf_op jit(solution)/shard_map/while/body/eval_jaxpr/ppermute | solution.py:14
  190.3 2.5 collective-permute-start
  192.8 2.5 collective-permute-start.1
  195.4 2.5 collective-permute-start.2
  197.9 3.6 collective-permute-start.3
  209.4 3.1 collective-permute-start
  212.5 2.5 collective-permute-start.1
  215.1 2.5 collective-permute-start.2
  217.6 3.7 collective-permute-start.3
  229.2 3.0 collective-permute-start
  232.3 3.0 collective-permute-start.1
  237.2 3.8 collective-permute-start.3
  250.0 2.6 collective-permute-start
  252.6 3.4 collective-permute-start.1
  256.0 3.3 collective-permute-start.2
  259.2 4.8 %collective-permute-start.3 = (f32[8,8,1,8,128]{4,3,1,0,2:T(8,128)}, f32[8,8,1,8,128]{4,3,1,0,2:T(8,128)S(1)}, u32[]{:S(2)}, u32[]{:S(2)}) collective-permute-start(f32[8,8,1,8,128]{4,3,1,0,2:T(8,128)} %get-tuple-element.433), channel_id=1, source_target_pairs={{0,16},{16,32},{32,48},{48,64},{64,80},{80,96},{96,112},{112,128},... | collective-permute-start | bytes 786440 | tf_op jit(solution)/shard_map/while/body/eval_jaxpr/ppermute | solution.py:14
  272.0 3.4 collective-permute-start
  275.3 2.5 collective-permute-start.1
  277.9 2.3 collective-permute-start.2
  280.2 4.3 %collective-permute-start.3 = (f32[8,8,1,8,128]{4,3,1,0,2:T(8,128)}, f32[8,8,1,8,128]{4,3,1,0,2:T(8,128)S(1)}, u32[]{:S(2)}, u32[]{:S(2)}) collective-permute-start(f32[8,8,1,8,128]{4,3,1,0,2:T(8,128)} %get-tuple-element.433), channel_id=1, source_target_pairs={{0,16},{16,32},{32,48},{48,64},{64,80},{80,96},{96,112},{112,128},... | collective-permute-start | bytes 786440 | tf_op jit(solution)/shard_map/while/body/eval_jaxpr/ppermute | solution.py:14
  292.5 2.7 collective-permute-start
  295.1 2.9 collective-permute-start.1
  298.0 2.6 collective-permute-start.2
  300.6 4.1 %collective-permute-start.3 = (f32[8,8,1,8,128]{4,3,1,0,2:T(8,128)}, f32[8,8,1,8,128]{4,3,1,0,2:T(8,128)S(1)}, u32[]{:S(2)}, u32[]{:S(2)}) collective-permute-start(f32[8,8,1,8,128]{4,3,1,0,2:T(8,128)} %get-tuple-element.433), channel_id=1, source_target_pairs={{0,16},{16,32},{32,48},{48,64},{64,80},{80,96},{96,112},{112,128},... | collective-permute-start | bytes 786440 | tf_op jit(solution)/shard_map/while/body/eval_jaxpr/ppermute | solution.py:14
  312.6 2.4 collective-permute-start
  315.0 2.3 collective-permute-start.1
  317.3 2.6 collective-permute-start.2
  320.0 3.5 collective-permute-start.3
  331.5 2.6 collective-permute-start
  334.0 3.4 collective-permute-start.1
  337.4 3.3 collective-permute-start.2
  340.7 4.8 %collective-permute-start.3 = (f32[8,8,1,8,128]{4,3,1,0,2:T(8,128)}, f32[8,8,1,8,128]{4,3,1,0,2:T(8,128)S(1)}, u32[]{:S(2)}, u32[]{:S(2)}) collective-permute-start(f32[8,8,1,8,128]{4,3,1,0,2:T(8,128)} %get-tuple-element.433), channel_id=1, source_target_pairs={{0,16},{16,32},{32,48},{48,64},{64,80},{80,96},{96,112},{112,128},... | collective-permute-start | bytes 786440 | tf_op jit(solution)/shard_map/while/body/eval_jaxpr/ppermute | solution.py:14
  353.4 3.4 collective-permute-start
  356.9 2.7 collective-permute-start.1
  359.6 2.2 collective-permute-start.2
  361.9 4.1 %collective-permute-start.3 = (f32[8,8,1,8,128]{4,3,1,0,2:T(8,128)}, f32[8,8,1,8,128]{4,3,1,0,2:T(8,128)S(1)}, u32[]{:S(2)}, u32[]{:S(2)}) collective-permute-start(f32[8,8,1,8,128]{4,3,1,0,2:T(8,128)} %get-tuple-element.433), channel_id=1, source_target_pairs={{0,16},{16,32},{32,48},{48,64},{64,80},{80,96},{96,112},{112,128},... | collective-permute-start | bytes 786440 | tf_op jit(solution)/shard_map/while/body/eval_jaxpr/ppermute | solution.py:14
  373.9 2.8 collective-permute-start.4
  376.7 2.9 collective-permute-start.5
  379.6 4.5 %collective-permute-done.5 = f32[8,8,1,8]{3,1,0,2:T(8,128)S(1)} collective-permute-done((f32[8,8,1,8]{3,1,0,2:T(8,128)}, f32[8,8,1,8]{3,1,0,2:T(8,128)S(1)}, u32[]{:S(2)}, u32[]{:S(2)}) %collective-permute-start.5) | collective-permute-done | bytes 2080 | tf_op jit(solution)/shard_map/ppermute | solution.py:14
  (342 shorter events, 141.7 us)
Async XLA Ops:
  0.6 46.7 %copy-start.6 = (s32[8,1]{0,1:T(1,128)S(1)}, s32[8,1]{0,1:T(1,128)}, u32[]{:S(2)}) copy-start(s32[8,1]{0,1:T(1,128)} %param.12) | copy-start | bytes 100
  3.7 382.1 %all-to-all-start = ((bf16[16,8,8,256]{3,2,1,0:T(8,128)(2,1)}), bf16[16,8,8,256]{3,2,1,0:T(8,128)(2,1)}, u32[]{:S(2)}, u32[]{:S(2)}) async-start(bf16[16,8,8,256]{3,2,1,0:T(8,128)(2,1)} %broadcast_in_dim.213), calls=%async_computation | async-start | bytes 1048576 | tf_op jit(solution)/shard_map/all_to_all | solution.py:19
  63.0 15.9 %collective-permute-start = (bf16[8,8,1,8,128]{4,3,1,0,2:T(8,128)(2,1)}, bf16[8,8,1,8,128]{4,3,1,0,2:T(8,128)(2,1)S(1)}, u32[]{:S(2)}, u32[]{:S(2)}) collective-permute-start(bf16[8,8,1,8,128]{4,3,1,0,2:T(8,128)(2,1)} %get-tuple-element.430), channel_id=1, source_target_pairs={{0,16},{16,32},{32,48},{48,64},{64,80},{80,96},{96,112},{112,128},... | collective-permute-start | bytes 393224 | tf_op jit(solution)/shard_map/while/body/eval_jaxpr/ppermute | solution.py:14
  66.7 13.7 %collective-permute-start.1 = (f32[8,8,1,8]{3,1,0,2:T(8,128)}, f32[8,8,1,8]{3,1,0,2:T(8,128)}, u32[]{:S(2)}, u32[]{:S(2)}) collective-permute-start(f32[8,8,1,8]{3,1,0,2:T(8,128)} %get-tuple-element.431), channel_id=1, source_target_pairs={{0,16},{16,32},{32,48},{48,64},{64,80},{80,96},{96,112},{112,128},... | collective-permute-start | bytes 6152 | tf_op jit(solution)/shard_map/while/body/eval_jaxpr/ppermute | solution.py:14
  70.1 12.3 %collective-permute-start.2 = (f32[8,8,1,8]{3,1,0,2:T(8,128)}, f32[8,8,1,8]{3,1,0,2:T(8,128)}, u32[]{:S(2)}, u32[]{:S(2)}) collective-permute-start(f32[8,8,1,8]{3,1,0,2:T(8,128)} %get-tuple-element.432), channel_id=1, source_target_pairs={{0,16},{16,32},{32,48},{48,64},{64,80},{80,96},{96,112},{112,128},... | collective-permute-start | bytes 6152 | tf_op jit(solution)/shard_map/while/body/eval_jaxpr/ppermute | solution.py:14
  73.5 11.3 %collective-permute-start.3 = (f32[8,8,1,8,128]{4,3,1,0,2:T(8,128)}, f32[8,8,1,8,128]{4,3,1,0,2:T(8,128)S(1)}, u32[]{:S(2)}, u32[]{:S(2)}) collective-permute-start(f32[8,8,1,8,128]{4,3,1,0,2:T(8,128)} %get-tuple-element.433), channel_id=1, source_target_pairs={{0,16},{16,32},{32,48},{48,64},{64,80},{80,96},{96,112},{112,128},... | collective-permute-start | bytes 786440 | tf_op jit(solution)/shard_map/while/body/eval_jaxpr/ppermute | solution.py:14
  86.0 15.6 %collective-permute-start = (bf16[8,8,1,8,128]{4,3,1,0,2:T(8,128)(2,1)}, bf16[8,8,1,8,128]{4,3,1,0,2:T(8,128)(2,1)S(1)}, u32[]{:S(2)}, u32[]{:S(2)}) collective-permute-start(bf16[8,8,1,8,128]{4,3,1,0,2:T(8,128)(2,1)} %get-tuple-element.430), channel_id=1, source_target_pairs={{0,16},{16,32},{32,48},{48,64},{64,80},{80,96},{96,112},{112,128},... | collective-permute-start | bytes 393224 | tf_op jit(solution)/shard_map/while/body/eval_jaxpr/ppermute | solution.py:14
  89.4 13.7 %collective-permute-start.1 = (f32[8,8,1,8]{3,1,0,2:T(8,128)}, f32[8,8,1,8]{3,1,0,2:T(8,128)}, u32[]{:S(2)}, u32[]{:S(2)}) collective-permute-start(f32[8,8,1,8]{3,1,0,2:T(8,128)} %get-tuple-element.431), channel_id=1, source_target_pairs={{0,16},{16,32},{32,48},{48,64},{64,80},{80,96},{96,112},{112,128},... | collective-permute-start | bytes 6152 | tf_op jit(solution)/shard_map/while/body/eval_jaxpr/ppermute | solution.py:14
  92.8 12.3 %collective-permute-start.2 = (f32[8,8,1,8]{3,1,0,2:T(8,128)}, f32[8,8,1,8]{3,1,0,2:T(8,128)}, u32[]{:S(2)}, u32[]{:S(2)}) collective-permute-start(f32[8,8,1,8]{3,1,0,2:T(8,128)} %get-tuple-element.432), channel_id=1, source_target_pairs={{0,16},{16,32},{32,48},{48,64},{64,80},{80,96},{96,112},{112,128},... | collective-permute-start | bytes 6152 | tf_op jit(solution)/shard_map/while/body/eval_jaxpr/ppermute | solution.py:14
  96.3 11.3 %collective-permute-start.3 = (f32[8,8,1,8,128]{4,3,1,0,2:T(8,128)}, f32[8,8,1,8,128]{4,3,1,0,2:T(8,128)S(1)}, u32[]{:S(2)}, u32[]{:S(2)}) collective-permute-start(f32[8,8,1,8,128]{4,3,1,0,2:T(8,128)} %get-tuple-element.433), channel_id=1, source_target_pairs={{0,16},{16,32},{32,48},{48,64},{64,80},{80,96},{96,112},{112,128},... | collective-permute-start | bytes 786440 | tf_op jit(solution)/shard_map/while/body/eval_jaxpr/ppermute | solution.py:14
  108.8 12.0 %collective-permute-start = (bf16[8,8,1,8,128]{4,3,1,0,2:T(8,128)(2,1)}, bf16[8,8,1,8,128]{4,3,1,0,2:T(8,128)(2,1)S(1)}, u32[]{:S(2)}, u32[]{:S(2)}) collective-permute-start(bf16[8,8,1,8,128]{4,3,1,0,2:T(8,128)(2,1)} %get-tuple-element.430), channel_id=1, source_target_pairs={{0,16},{16,32},{32,48},{48,64},{64,80},{80,96},{96,112},{112,128},... | collective-permute-start | bytes 393224 | tf_op jit(solution)/shard_map/while/body/eval_jaxpr/ppermute | solution.py:14
  111.3 11.0 %collective-permute-start.1 = (f32[8,8,1,8]{3,1,0,2:T(8,128)}, f32[8,8,1,8]{3,1,0,2:T(8,128)}, u32[]{:S(2)}, u32[]{:S(2)}) collective-permute-start(f32[8,8,1,8]{3,1,0,2:T(8,128)} %get-tuple-element.431), channel_id=1, source_target_pairs={{0,16},{16,32},{32,48},{48,64},{64,80},{80,96},{96,112},{112,128},... | collective-permute-start | bytes 6152 | tf_op jit(solution)/shard_map/while/body/eval_jaxpr/ppermute | solution.py:14
  113.8 10.5 %collective-permute-start.2 = (f32[8,8,1,8]{3,1,0,2:T(8,128)}, f32[8,8,1,8]{3,1,0,2:T(8,128)}, u32[]{:S(2)}, u32[]{:S(2)}) collective-permute-start(f32[8,8,1,8]{3,1,0,2:T(8,128)} %get-tuple-element.432), channel_id=1, source_target_pairs={{0,16},{16,32},{32,48},{48,64},{64,80},{80,96},{96,112},{112,128},... | collective-permute-start | bytes 6152 | tf_op jit(solution)/shard_map/while/body/eval_jaxpr/ppermute | solution.py:14
  116.3 10.4 %collective-permute-start.3 = (f32[8,8,1,8,128]{4,3,1,0,2:T(8,128)}, f32[8,8,1,8,128]{4,3,1,0,2:T(8,128)S(1)}, u32[]{:S(2)}, u32[]{:S(2)}) collective-permute-start(f32[8,8,1,8,128]{4,3,1,0,2:T(8,128)} %get-tuple-element.433), channel_id=1, source_target_pairs={{0,16},{16,32},{32,48},{48,64},{64,80},{80,96},{96,112},{112,128},... | collective-permute-start | bytes 786440 | tf_op jit(solution)/shard_map/while/body/eval_jaxpr/ppermute | solution.py:14
  128.0 12.6 %collective-permute-start = (bf16[8,8,1,8,128]{4,3,1,0,2:T(8,128)(2,1)}, bf16[8,8,1,8,128]{4,3,1,0,2:T(8,128)(2,1)S(1)}, u32[]{:S(2)}, u32[]{:S(2)}) collective-permute-start(bf16[8,8,1,8,128]{4,3,1,0,2:T(8,128)(2,1)} %get-tuple-element.430), channel_id=1, source_target_pairs={{0,16},{16,32},{32,48},{48,64},{64,80},{80,96},{96,112},{112,128},... | collective-permute-start | bytes 393224 | tf_op jit(solution)/shard_map/while/body/eval_jaxpr/ppermute | solution.py:14
  131.1 11.0 %collective-permute-start.1 = (f32[8,8,1,8]{3,1,0,2:T(8,128)}, f32[8,8,1,8]{3,1,0,2:T(8,128)}, u32[]{:S(2)}, u32[]{:S(2)}) collective-permute-start(f32[8,8,1,8]{3,1,0,2:T(8,128)} %get-tuple-element.431), channel_id=1, source_target_pairs={{0,16},{16,32},{32,48},{48,64},{64,80},{80,96},{96,112},{112,128},... | collective-permute-start | bytes 6152 | tf_op jit(solution)/shard_map/while/body/eval_jaxpr/ppermute | solution.py:14
  133.6 10.5 %collective-permute-start.2 = (f32[8,8,1,8]{3,1,0,2:T(8,128)}, f32[8,8,1,8]{3,1,0,2:T(8,128)}, u32[]{:S(2)}, u32[]{:S(2)}) collective-permute-start(f32[8,8,1,8]{3,1,0,2:T(8,128)} %get-tuple-element.432), channel_id=1, source_target_pairs={{0,16},{16,32},{32,48},{48,64},{64,80},{80,96},{96,112},{112,128},... | collective-permute-start | bytes 6152 | tf_op jit(solution)/shard_map/while/body/eval_jaxpr/ppermute | solution.py:14
  136.1 10.3 %collective-permute-start.3 = (f32[8,8,1,8,128]{4,3,1,0,2:T(8,128)}, f32[8,8,1,8,128]{4,3,1,0,2:T(8,128)S(1)}, u32[]{:S(2)}, u32[]{:S(2)}) collective-permute-start(f32[8,8,1,8,128]{4,3,1,0,2:T(8,128)} %get-tuple-element.433), channel_id=1, source_target_pairs={{0,16},{16,32},{32,48},{48,64},{64,80},{80,96},{96,112},{112,128},... | collective-permute-start | bytes 786440 | tf_op jit(solution)/shard_map/while/body/eval_jaxpr/ppermute | solution.py:14
  147.7 12.6 %collective-permute-start = (bf16[8,8,1,8,128]{4,3,1,0,2:T(8,128)(2,1)}, bf16[8,8,1,8,128]{4,3,1,0,2:T(8,128)(2,1)S(1)}, u32[]{:S(2)}, u32[]{:S(2)}) collective-permute-start(bf16[8,8,1,8,128]{4,3,1,0,2:T(8,128)(2,1)} %get-tuple-element.430), channel_id=1, source_target_pairs={{0,16},{16,32},{32,48},{48,64},{64,80},{80,96},{96,112},{112,128},... | collective-permute-start | bytes 393224 | tf_op jit(solution)/shard_map/while/body/eval_jaxpr/ppermute | solution.py:14
  150.1 11.7 %collective-permute-start.1 = (f32[8,8,1,8]{3,1,0,2:T(8,128)}, f32[8,8,1,8]{3,1,0,2:T(8,128)}, u32[]{:S(2)}, u32[]{:S(2)}) collective-permute-start(f32[8,8,1,8]{3,1,0,2:T(8,128)} %get-tuple-element.431), channel_id=1, source_target_pairs={{0,16},{16,32},{32,48},{48,64},{64,80},{80,96},{96,112},{112,128},... | collective-permute-start | bytes 6152 | tf_op jit(solution)/shard_map/while/body/eval_jaxpr/ppermute | solution.py:14
  152.7 11.1 %collective-permute-start.2 = (f32[8,8,1,8]{3,1,0,2:T(8,128)}, f32[8,8,1,8]{3,1,0,2:T(8,128)}, u32[]{:S(2)}, u32[]{:S(2)}) collective-permute-start(f32[8,8,1,8]{3,1,0,2:T(8,128)} %get-tuple-element.432), channel_id=1, source_target_pairs={{0,16},{16,32},{32,48},{48,64},{64,80},{80,96},{96,112},{112,128},... | collective-permute-start | bytes 6152 | tf_op jit(solution)/shard_map/while/body/eval_jaxpr/ppermute | solution.py:14
  155.0 11.3 %collective-permute-start.3 = (f32[8,8,1,8,128]{4,3,1,0,2:T(8,128)}, f32[8,8,1,8,128]{4,3,1,0,2:T(8,128)S(1)}, u32[]{:S(2)}, u32[]{:S(2)}) collective-permute-start(f32[8,8,1,8,128]{4,3,1,0,2:T(8,128)} %get-tuple-element.433), channel_id=1, source_target_pairs={{0,16},{16,32},{32,48},{48,64},{64,80},{80,96},{96,112},{112,128},... | collective-permute-start | bytes 786440 | tf_op jit(solution)/shard_map/while/body/eval_jaxpr/ppermute | solution.py:14
  167.5 15.6 %collective-permute-start = (bf16[8,8,1,8,128]{4,3,1,0,2:T(8,128)(2,1)}, bf16[8,8,1,8,128]{4,3,1,0,2:T(8,128)(2,1)S(1)}, u32[]{:S(2)}, u32[]{:S(2)}) collective-permute-start(bf16[8,8,1,8,128]{4,3,1,0,2:T(8,128)(2,1)} %get-tuple-element.430), channel_id=1, source_target_pairs={{0,16},{16,32},{32,48},{48,64},{64,80},{80,96},{96,112},{112,128},... | collective-permute-start | bytes 393224 | tf_op jit(solution)/shard_map/while/body/eval_jaxpr/ppermute | solution.py:14
  170.9 13.7 %collective-permute-start.1 = (f32[8,8,1,8]{3,1,0,2:T(8,128)}, f32[8,8,1,8]{3,1,0,2:T(8,128)}, u32[]{:S(2)}, u32[]{:S(2)}) collective-permute-start(f32[8,8,1,8]{3,1,0,2:T(8,128)} %get-tuple-element.431), channel_id=1, source_target_pairs={{0,16},{16,32},{32,48},{48,64},{64,80},{80,96},{96,112},{112,128},... | collective-permute-start | bytes 6152 | tf_op jit(solution)/shard_map/while/body/eval_jaxpr/ppermute | solution.py:14
  174.3 12.3 %collective-permute-start.2 = (f32[8,8,1,8]{3,1,0,2:T(8,128)}, f32[8,8,1,8]{3,1,0,2:T(8,128)}, u32[]{:S(2)}, u32[]{:S(2)}) collective-permute-start(f32[8,8,1,8]{3,1,0,2:T(8,128)} %get-tuple-element.432), channel_id=1, source_target_pairs={{0,16},{16,32},{32,48},{48,64},{64,80},{80,96},{96,112},{112,128},... | collective-permute-start | bytes 6152 | tf_op jit(solution)/shard_map/while/body/eval_jaxpr/ppermute | solution.py:14
  177.7 11.3 %collective-permute-start.3 = (f32[8,8,1,8,128]{4,3,1,0,2:T(8,128)}, f32[8,8,1,8,128]{4,3,1,0,2:T(8,128)S(1)}, u32[]{:S(2)}, u32[]{:S(2)}) collective-permute-start(f32[8,8,1,8,128]{4,3,1,0,2:T(8,128)} %get-tuple-element.433), channel_id=1, source_target_pairs={{0,16},{16,32},{32,48},{48,64},{64,80},{80,96},{96,112},{112,128},... | collective-permute-start | bytes 786440 | tf_op jit(solution)/shard_map/while/body/eval_jaxpr/ppermute | solution.py:14
  190.3 12.0 %collective-permute-start = (bf16[8,8,1,8,128]{4,3,1,0,2:T(8,128)(2,1)}, bf16[8,8,1,8,128]{4,3,1,0,2:T(8,128)(2,1)S(1)}, u32[]{:S(2)}, u32[]{:S(2)}) collective-permute-start(bf16[8,8,1,8,128]{4,3,1,0,2:T(8,128)(2,1)} %get-tuple-element.430), channel_id=1, source_target_pairs={{0,16},{16,32},{32,48},{48,64},{64,80},{80,96},{96,112},{112,128},... | collective-permute-start | bytes 393224 | tf_op jit(solution)/shard_map/while/body/eval_jaxpr/ppermute | solution.py:14
  192.8 10.9 %collective-permute-start.1 = (f32[8,8,1,8]{3,1,0,2:T(8,128)}, f32[8,8,1,8]{3,1,0,2:T(8,128)}, u32[]{:S(2)}, u32[]{:S(2)}) collective-permute-start(f32[8,8,1,8]{3,1,0,2:T(8,128)} %get-tuple-element.431), channel_id=1, source_target_pairs={{0,16},{16,32},{32,48},{48,64},{64,80},{80,96},{96,112},{112,128},... | collective-permute-start | bytes 6152 | tf_op jit(solution)/shard_map/while/body/eval_jaxpr/ppermute | solution.py:14
  195.4 10.4 %collective-permute-start.2 = (f32[8,8,1,8]{3,1,0,2:T(8,128)}, f32[8,8,1,8]{3,1,0,2:T(8,128)}, u32[]{:S(2)}, u32[]{:S(2)}) collective-permute-start(f32[8,8,1,8]{3,1,0,2:T(8,128)} %get-tuple-element.432), channel_id=1, source_target_pairs={{0,16},{16,32},{32,48},{48,64},{64,80},{80,96},{96,112},{112,128},... | collective-permute-start | bytes 6152 | tf_op jit(solution)/shard_map/while/body/eval_jaxpr/ppermute | solution.py:14
  197.9 10.3 %collective-permute-start.3 = (f32[8,8,1,8,128]{4,3,1,0,2:T(8,128)}, f32[8,8,1,8,128]{4,3,1,0,2:T(8,128)S(1)}, u32[]{:S(2)}, u32[]{:S(2)}) collective-permute-start(f32[8,8,1,8,128]{4,3,1,0,2:T(8,128)} %get-tuple-element.433), channel_id=1, source_target_pairs={{0,16},{16,32},{32,48},{48,64},{64,80},{80,96},{96,112},{112,128},... | collective-permute-start | bytes 786440 | tf_op jit(solution)/shard_map/while/body/eval_jaxpr/ppermute | solution.py:14
  209.4 12.6 %collective-permute-start = (bf16[8,8,1,8,128]{4,3,1,0,2:T(8,128)(2,1)}, bf16[8,8,1,8,128]{4,3,1,0,2:T(8,128)(2,1)S(1)}, u32[]{:S(2)}, u32[]{:S(2)}) collective-permute-start(bf16[8,8,1,8,128]{4,3,1,0,2:T(8,128)(2,1)} %get-tuple-element.430), channel_id=1, source_target_pairs={{0,16},{16,32},{32,48},{48,64},{64,80},{80,96},{96,112},{112,128},... | collective-permute-start | bytes 393224 | tf_op jit(solution)/shard_map/while/body/eval_jaxpr/ppermute | solution.py:14
  212.5 11.0 %collective-permute-start.1 = (f32[8,8,1,8]{3,1,0,2:T(8,128)}, f32[8,8,1,8]{3,1,0,2:T(8,128)}, u32[]{:S(2)}, u32[]{:S(2)}) collective-permute-start(f32[8,8,1,8]{3,1,0,2:T(8,128)} %get-tuple-element.431), channel_id=1, source_target_pairs={{0,16},{16,32},{32,48},{48,64},{64,80},{80,96},{96,112},{112,128},... | collective-permute-start | bytes 6152 | tf_op jit(solution)/shard_map/while/body/eval_jaxpr/ppermute | solution.py:14
  215.1 10.5 %collective-permute-start.2 = (f32[8,8,1,8]{3,1,0,2:T(8,128)}, f32[8,8,1,8]{3,1,0,2:T(8,128)}, u32[]{:S(2)}, u32[]{:S(2)}) collective-permute-start(f32[8,8,1,8]{3,1,0,2:T(8,128)} %get-tuple-element.432), channel_id=1, source_target_pairs={{0,16},{16,32},{32,48},{48,64},{64,80},{80,96},{96,112},{112,128},... | collective-permute-start | bytes 6152 | tf_op jit(solution)/shard_map/while/body/eval_jaxpr/ppermute | solution.py:14
  217.6 10.3 %collective-permute-start.3 = (f32[8,8,1,8,128]{4,3,1,0,2:T(8,128)}, f32[8,8,1,8,128]{4,3,1,0,2:T(8,128)S(1)}, u32[]{:S(2)}, u32[]{:S(2)}) collective-permute-start(f32[8,8,1,8,128]{4,3,1,0,2:T(8,128)} %get-tuple-element.433), channel_id=1, source_target_pairs={{0,16},{16,32},{32,48},{48,64},{64,80},{80,96},{96,112},{112,128},... | collective-permute-start | bytes 786440 | tf_op jit(solution)/shard_map/while/body/eval_jaxpr/ppermute | solution.py:14
  229.2 12.6 %collective-permute-start = (bf16[8,8,1,8,128]{4,3,1,0,2:T(8,128)(2,1)}, bf16[8,8,1,8,128]{4,3,1,0,2:T(8,128)(2,1)S(1)}, u32[]{:S(2)}, u32[]{:S(2)}) collective-permute-start(bf16[8,8,1,8,128]{4,3,1,0,2:T(8,128)(2,1)} %get-tuple-element.430), channel_id=1, source_target_pairs={{0,16},{16,32},{32,48},{48,64},{64,80},{80,96},{96,112},{112,128},... | collective-permute-start | bytes 393224 | tf_op jit(solution)/shard_map/while/body/eval_jaxpr/ppermute | solution.py:14
  232.3 11.1 %collective-permute-start.1 = (f32[8,8,1,8]{3,1,0,2:T(8,128)}, f32[8,8,1,8]{3,1,0,2:T(8,128)}, u32[]{:S(2)}, u32[]{:S(2)}) collective-permute-start(f32[8,8,1,8]{3,1,0,2:T(8,128)} %get-tuple-element.431), channel_id=1, source_target_pairs={{0,16},{16,32},{32,48},{48,64},{64,80},{80,96},{96,112},{112,128},... | collective-permute-start | bytes 6152 | tf_op jit(solution)/shard_map/while/body/eval_jaxpr/ppermute | solution.py:14
  235.3 10.1 %collective-permute-start.2 = (f32[8,8,1,8]{3,1,0,2:T(8,128)}, f32[8,8,1,8]{3,1,0,2:T(8,128)}, u32[]{:S(2)}, u32[]{:S(2)}) collective-permute-start(f32[8,8,1,8]{3,1,0,2:T(8,128)} %get-tuple-element.432), channel_id=1, source_target_pairs={{0,16},{16,32},{32,48},{48,64},{64,80},{80,96},{96,112},{112,128},... | collective-permute-start | bytes 6152 | tf_op jit(solution)/shard_map/while/body/eval_jaxpr/ppermute | solution.py:14
  237.2 11.5 %collective-permute-start.3 = (f32[8,8,1,8,128]{4,3,1,0,2:T(8,128)}, f32[8,8,1,8,128]{4,3,1,0,2:T(8,128)S(1)}, u32[]{:S(2)}, u32[]{:S(2)}) collective-permute-start(f32[8,8,1,8,128]{4,3,1,0,2:T(8,128)} %get-tuple-element.433), channel_id=1, source_target_pairs={{0,16},{16,32},{32,48},{48,64},{64,80},{80,96},{96,112},{112,128},... | collective-permute-start | bytes 786440 | tf_op jit(solution)/shard_map/while/body/eval_jaxpr/ppermute | solution.py:14
  250.0 14.8 %collective-permute-start = (bf16[8,8,1,8,128]{4,3,1,0,2:T(8,128)(2,1)}, bf16[8,8,1,8,128]{4,3,1,0,2:T(8,128)(2,1)S(1)}, u32[]{:S(2)}, u32[]{:S(2)}) collective-permute-start(bf16[8,8,1,8,128]{4,3,1,0,2:T(8,128)(2,1)} %get-tuple-element.430), channel_id=1, source_target_pairs={{0,16},{16,32},{32,48},{48,64},{64,80},{80,96},{96,112},{112,128},... | collective-permute-start | bytes 393224 | tf_op jit(solution)/shard_map/while/body/eval_jaxpr/ppermute | solution.py:14
  252.6 13.7 %collective-permute-start.1 = (f32[8,8,1,8]{3,1,0,2:T(8,128)}, f32[8,8,1,8]{3,1,0,2:T(8,128)}, u32[]{:S(2)}, u32[]{:S(2)}) collective-permute-start(f32[8,8,1,8]{3,1,0,2:T(8,128)} %get-tuple-element.431), channel_id=1, source_target_pairs={{0,16},{16,32},{32,48},{48,64},{64,80},{80,96},{96,112},{112,128},... | collective-permute-start | bytes 6152 | tf_op jit(solution)/shard_map/while/body/eval_jaxpr/ppermute | solution.py:14
  256.0 12.3 %collective-permute-start.2 = (f32[8,8,1,8]{3,1,0,2:T(8,128)}, f32[8,8,1,8]{3,1,0,2:T(8,128)}, u32[]{:S(2)}, u32[]{:S(2)}) collective-permute-start(f32[8,8,1,8]{3,1,0,2:T(8,128)} %get-tuple-element.432), channel_id=1, source_target_pairs={{0,16},{16,32},{32,48},{48,64},{64,80},{80,96},{96,112},{112,128},... | collective-permute-start | bytes 6152 | tf_op jit(solution)/shard_map/while/body/eval_jaxpr/ppermute | solution.py:14
  259.2 11.5 %collective-permute-start.3 = (f32[8,8,1,8,128]{4,3,1,0,2:T(8,128)}, f32[8,8,1,8,128]{4,3,1,0,2:T(8,128)S(1)}, u32[]{:S(2)}, u32[]{:S(2)}) collective-permute-start(f32[8,8,1,8,128]{4,3,1,0,2:T(8,128)} %get-tuple-element.433), channel_id=1, source_target_pairs={{0,16},{16,32},{32,48},{48,64},{64,80},{80,96},{96,112},{112,128},... | collective-permute-start | bytes 786440 | tf_op jit(solution)/shard_map/while/body/eval_jaxpr/ppermute | solution.py:14
  272.0 13.4 %collective-permute-start = (bf16[8,8,1,8,128]{4,3,1,0,2:T(8,128)(2,1)}, bf16[8,8,1,8,128]{4,3,1,0,2:T(8,128)(2,1)S(1)}, u32[]{:S(2)}, u32[]{:S(2)}) collective-permute-start(bf16[8,8,1,8,128]{4,3,1,0,2:T(8,128)(2,1)} %get-tuple-element.430), channel_id=1, source_target_pairs={{0,16},{16,32},{32,48},{48,64},{64,80},{80,96},{96,112},{112,128},... | collective-permute-start | bytes 393224 | tf_op jit(solution)/shard_map/while/body/eval_jaxpr/ppermute | solution.py:14
  275.3 11.4 %collective-permute-start.1 = (f32[8,8,1,8]{3,1,0,2:T(8,128)}, f32[8,8,1,8]{3,1,0,2:T(8,128)}, u32[]{:S(2)}, u32[]{:S(2)}) collective-permute-start(f32[8,8,1,8]{3,1,0,2:T(8,128)} %get-tuple-element.431), channel_id=1, source_target_pairs={{0,16},{16,32},{32,48},{48,64},{64,80},{80,96},{96,112},{112,128},... | collective-permute-start | bytes 6152 | tf_op jit(solution)/shard_map/while/body/eval_jaxpr/ppermute | solution.py:14
  277.9 10.9 %collective-permute-start.2 = (f32[8,8,1,8]{3,1,0,2:T(8,128)}, f32[8,8,1,8]{3,1,0,2:T(8,128)}, u32[]{:S(2)}, u32[]{:S(2)}) collective-permute-start(f32[8,8,1,8]{3,1,0,2:T(8,128)} %get-tuple-element.432), channel_id=1, source_target_pairs={{0,16},{16,32},{32,48},{48,64},{64,80},{80,96},{96,112},{112,128},... | collective-permute-start | bytes 6152 | tf_op jit(solution)/shard_map/while/body/eval_jaxpr/ppermute | solution.py:14
  280.2 11.0 %collective-permute-start.3 = (f32[8,8,1,8,128]{4,3,1,0,2:T(8,128)}, f32[8,8,1,8,128]{4,3,1,0,2:T(8,128)S(1)}, u32[]{:S(2)}, u32[]{:S(2)}) collective-permute-start(f32[8,8,1,8,128]{4,3,1,0,2:T(8,128)} %get-tuple-element.433), channel_id=1, source_target_pairs={{0,16},{16,32},{32,48},{48,64},{64,80},{80,96},{96,112},{112,128},... | collective-permute-start | bytes 786440 | tf_op jit(solution)/shard_map/while/body/eval_jaxpr/ppermute | solution.py:14
  292.5 13.0 %collective-permute-start = (bf16[8,8,1,8,128]{4,3,1,0,2:T(8,128)(2,1)}, bf16[8,8,1,8,128]{4,3,1,0,2:T(8,128)(2,1)S(1)}, u32[]{:S(2)}, u32[]{:S(2)}) collective-permute-start(bf16[8,8,1,8,128]{4,3,1,0,2:T(8,128)(2,1)} %get-tuple-element.430), channel_id=1, source_target_pairs={{0,16},{16,32},{32,48},{48,64},{64,80},{80,96},{96,112},{112,128},... | collective-permute-start | bytes 393224 | tf_op jit(solution)/shard_map/while/body/eval_jaxpr/ppermute | solution.py:14
  295.1 11.8 %collective-permute-start.1 = (f32[8,8,1,8]{3,1,0,2:T(8,128)}, f32[8,8,1,8]{3,1,0,2:T(8,128)}, u32[]{:S(2)}, u32[]{:S(2)}) collective-permute-start(f32[8,8,1,8]{3,1,0,2:T(8,128)} %get-tuple-element.431), channel_id=1, source_target_pairs={{0,16},{16,32},{32,48},{48,64},{64,80},{80,96},{96,112},{112,128},... | collective-permute-start | bytes 6152 | tf_op jit(solution)/shard_map/while/body/eval_jaxpr/ppermute | solution.py:14
  298.0 11.0 %collective-permute-start.2 = (f32[8,8,1,8]{3,1,0,2:T(8,128)}, f32[8,8,1,8]{3,1,0,2:T(8,128)}, u32[]{:S(2)}, u32[]{:S(2)}) collective-permute-start(f32[8,8,1,8]{3,1,0,2:T(8,128)} %get-tuple-element.432), channel_id=1, source_target_pairs={{0,16},{16,32},{32,48},{48,64},{64,80},{80,96},{96,112},{112,128},... | collective-permute-start | bytes 6152 | tf_op jit(solution)/shard_map/while/body/eval_jaxpr/ppermute | solution.py:14
  300.6 10.7 %collective-permute-start.3 = (f32[8,8,1,8,128]{4,3,1,0,2:T(8,128)}, f32[8,8,1,8,128]{4,3,1,0,2:T(8,128)S(1)}, u32[]{:S(2)}, u32[]{:S(2)}) collective-permute-start(f32[8,8,1,8,128]{4,3,1,0,2:T(8,128)} %get-tuple-element.433), channel_id=1, source_target_pairs={{0,16},{16,32},{32,48},{48,64},{64,80},{80,96},{96,112},{112,128},... | collective-permute-start | bytes 786440 | tf_op jit(solution)/shard_map/while/body/eval_jaxpr/ppermute | solution.py:14
  312.6 11.7 %collective-permute-start = (bf16[8,8,1,8,128]{4,3,1,0,2:T(8,128)(2,1)}, bf16[8,8,1,8,128]{4,3,1,0,2:T(8,128)(2,1)S(1)}, u32[]{:S(2)}, u32[]{:S(2)}) collective-permute-start(bf16[8,8,1,8,128]{4,3,1,0,2:T(8,128)(2,1)} %get-tuple-element.430), channel_id=1, source_target_pairs={{0,16},{16,32},{32,48},{48,64},{64,80},{80,96},{96,112},{112,128},... | collective-permute-start | bytes 393224 | tf_op jit(solution)/shard_map/while/body/eval_jaxpr/ppermute | solution.py:14
  315.0 10.7 %collective-permute-start.1 = (f32[8,8,1,8]{3,1,0,2:T(8,128)}, f32[8,8,1,8]{3,1,0,2:T(8,128)}, u32[]{:S(2)}, u32[]{:S(2)}) collective-permute-start(f32[8,8,1,8]{3,1,0,2:T(8,128)} %get-tuple-element.431), channel_id=1, source_target_pairs={{0,16},{16,32},{32,48},{48,64},{64,80},{80,96},{96,112},{112,128},... | collective-permute-start | bytes 6152 | tf_op jit(solution)/shard_map/while/body/eval_jaxpr/ppermute | solution.py:14
  317.3 10.5 %collective-permute-start.2 = (f32[8,8,1,8]{3,1,0,2:T(8,128)}, f32[8,8,1,8]{3,1,0,2:T(8,128)}, u32[]{:S(2)}, u32[]{:S(2)}) collective-permute-start(f32[8,8,1,8]{3,1,0,2:T(8,128)} %get-tuple-element.432), channel_id=1, source_target_pairs={{0,16},{16,32},{32,48},{48,64},{64,80},{80,96},{96,112},{112,128},... | collective-permute-start | bytes 6152 | tf_op jit(solution)/shard_map/while/body/eval_jaxpr/ppermute | solution.py:14
  320.0 10.2 %collective-permute-start.3 = (f32[8,8,1,8,128]{4,3,1,0,2:T(8,128)}, f32[8,8,1,8,128]{4,3,1,0,2:T(8,128)S(1)}, u32[]{:S(2)}, u32[]{:S(2)}) collective-permute-start(f32[8,8,1,8,128]{4,3,1,0,2:T(8,128)} %get-tuple-element.433), channel_id=1, source_target_pairs={{0,16},{16,32},{32,48},{48,64},{64,80},{80,96},{96,112},{112,128},... | collective-permute-start | bytes 786440 | tf_op jit(solution)/shard_map/while/body/eval_jaxpr/ppermute | solution.py:14
  331.5 14.8 %collective-permute-start = (bf16[8,8,1,8,128]{4,3,1,0,2:T(8,128)(2,1)}, bf16[8,8,1,8,128]{4,3,1,0,2:T(8,128)(2,1)S(1)}, u32[]{:S(2)}, u32[]{:S(2)}) collective-permute-start(bf16[8,8,1,8,128]{4,3,1,0,2:T(8,128)(2,1)} %get-tuple-element.430), channel_id=1, source_target_pairs={{0,16},{16,32},{32,48},{48,64},{64,80},{80,96},{96,112},{112,128},... | collective-permute-start | bytes 393224 | tf_op jit(solution)/shard_map/while/body/eval_jaxpr/ppermute | solution.py:14
  334.0 13.7 %collective-permute-start.1 = (f32[8,8,1,8]{3,1,0,2:T(8,128)}, f32[8,8,1,8]{3,1,0,2:T(8,128)}, u32[]{:S(2)}, u32[]{:S(2)}) collective-permute-start(f32[8,8,1,8]{3,1,0,2:T(8,128)} %get-tuple-element.431), channel_id=1, source_target_pairs={{0,16},{16,32},{32,48},{48,64},{64,80},{80,96},{96,112},{112,128},... | collective-permute-start | bytes 6152 | tf_op jit(solution)/shard_map/while/body/eval_jaxpr/ppermute | solution.py:14
  337.4 12.3 %collective-permute-start.2 = (f32[8,8,1,8]{3,1,0,2:T(8,128)}, f32[8,8,1,8]{3,1,0,2:T(8,128)}, u32[]{:S(2)}, u32[]{:S(2)}) collective-permute-start(f32[8,8,1,8]{3,1,0,2:T(8,128)} %get-tuple-element.432), channel_id=1, source_target_pairs={{0,16},{16,32},{32,48},{48,64},{64,80},{80,96},{96,112},{112,128},... | collective-permute-start | bytes 6152 | tf_op jit(solution)/shard_map/while/body/eval_jaxpr/ppermute | solution.py:14
  340.7 11.5 %collective-permute-start.3 = (f32[8,8,1,8,128]{4,3,1,0,2:T(8,128)}, f32[8,8,1,8,128]{4,3,1,0,2:T(8,128)S(1)}, u32[]{:S(2)}, u32[]{:S(2)}) collective-permute-start(f32[8,8,1,8,128]{4,3,1,0,2:T(8,128)} %get-tuple-element.433), channel_id=1, source_target_pairs={{0,16},{16,32},{32,48},{48,64},{64,80},{80,96},{96,112},{112,128},... | collective-permute-start | bytes 786440 | tf_op jit(solution)/shard_map/while/body/eval_jaxpr/ppermute | solution.py:14
  353.4 13.4 %collective-permute-start = (bf16[8,8,1,8,128]{4,3,1,0,2:T(8,128)(2,1)}, bf16[8,8,1,8,128]{4,3,1,0,2:T(8,128)(2,1)S(1)}, u32[]{:S(2)}, u32[]{:S(2)}) collective-permute-start(bf16[8,8,1,8,128]{4,3,1,0,2:T(8,128)(2,1)} %get-tuple-element.430), channel_id=1, source_target_pairs={{0,16},{16,32},{32,48},{48,64},{64,80},{80,96},{96,112},{112,128},... | collective-permute-start | bytes 393224 | tf_op jit(solution)/shard_map/while/body/eval_jaxpr/ppermute | solution.py:14
  356.9 11.4 %collective-permute-start.1 = (f32[8,8,1,8]{3,1,0,2:T(8,128)}, f32[8,8,1,8]{3,1,0,2:T(8,128)}, u32[]{:S(2)}, u32[]{:S(2)}) collective-permute-start(f32[8,8,1,8]{3,1,0,2:T(8,128)} %get-tuple-element.431), channel_id=1, source_target_pairs={{0,16},{16,32},{32,48},{48,64},{64,80},{80,96},{96,112},{112,128},... | collective-permute-start | bytes 6152 | tf_op jit(solution)/shard_map/while/body/eval_jaxpr/ppermute | solution.py:14
  359.6 10.6 %collective-permute-start.2 = (f32[8,8,1,8]{3,1,0,2:T(8,128)}, f32[8,8,1,8]{3,1,0,2:T(8,128)}, u32[]{:S(2)}, u32[]{:S(2)}) collective-permute-start(f32[8,8,1,8]{3,1,0,2:T(8,128)} %get-tuple-element.432), channel_id=1, source_target_pairs={{0,16},{16,32},{32,48},{48,64},{64,80},{80,96},{96,112},{112,128},... | collective-permute-start | bytes 6152 | tf_op jit(solution)/shard_map/while/body/eval_jaxpr/ppermute | solution.py:14
  361.9 10.8 %collective-permute-start.3 = (f32[8,8,1,8,128]{4,3,1,0,2:T(8,128)}, f32[8,8,1,8,128]{4,3,1,0,2:T(8,128)S(1)}, u32[]{:S(2)}, u32[]{:S(2)}) collective-permute-start(f32[8,8,1,8,128]{4,3,1,0,2:T(8,128)} %get-tuple-element.433), channel_id=1, source_target_pairs={{0,16},{16,32},{32,48},{48,64},{64,80},{80,96},{96,112},{112,128},... | collective-permute-start | bytes 786440 | tf_op jit(solution)/shard_map/while/body/eval_jaxpr/ppermute | solution.py:14
  373.9 10.2 %collective-permute-start.4 = (f32[8,8,1,8,128]{4,3,1,0,2:T(8,128)}, f32[8,8,1,8,128]{4,3,1,0,2:T(8,128)S(1)}, u32[]{:S(2)}, u32[]{:S(2)}) collective-permute-start(f32[8,8,1,8,128]{4,3,1,0,2:T(8,128)} %get-tuple-element.274), channel_id=1, source_target_pairs={{0,16},{16,32},{32,48},{48,64},{64,80},{80,96},{96,112},{112,128},... | collective-permute-start | bytes 786440 | tf_op jit(solution)/shard_map/ppermute | solution.py:14
  376.7 7.4 %collective-permute-start.5 = (f32[8,8,1,8]{3,1,0,2:T(8,128)}, f32[8,8,1,8]{3,1,0,2:T(8,128)S(1)}, u32[]{:S(2)}, u32[]{:S(2)}) collective-permute-start(f32[8,8,1,8]{3,1,0,2:T(8,128)} %get-tuple-element.275), channel_id=1, source_target_pairs={{0,16},{16,32},{32,48},{48,64},{64,80},{80,96},{96,112},{112,128},... | collective-permute-start | bytes 6152 | tf_op jit(solution)/shard_map/ppermute | solution.py:14
  (21 other events, 139.4 us)
where the time goes:
time: 392 us; the launch traced here: 388 us
  starting transfers between devices  240 us (61%)
  other arithmetic  66.8 us (17%)
  matrix products  48.3 us (12%)
  local copies, waits for them, and re-layouts  24.5 us (6%)
  waiting for transfers between devices  5.67 us (1%)
    ppermute x62, starting transfers between devices, passed_along(): lax.ppermute(shard, axis, [(i, (i + by) % size) for i in range(size)])  196 us
    all_to_all x1, starting transfers between devices, copy_for_each(): lax.all_to_all(jnp.broadcast_to(shard[None], (size, *shard.shape)), axis,...  43.7 us
    mul x15, other arithmetic, merge_parts(): scale_one[..., None] * acc_one + scale_two[..., None] * acc_two  21.2 us
    mul x15, other arithmetic, merge_parts(): scale_two[..., None] * acc_two  20.7 us
    dot_general x16, matrix products, block_partial(): jnp.einsum('fcjgp,fpjd->fcjgd', weight_old.astype(jnp.bfloat16), value_ca...  20.3 us
    dot_general x16, matrix products, block_partial(): jnp.einsum('fcjgd,fpjd->fcjgp', query_block, key_cache, preferred_element...  11.6 us
    dot_general x16, matrix products, block_partial(): jnp.einsum('fcjgd,fujd->fcjgu', query_block, key_fresh, preferred_element...  11.2 us
    lt x17, other arithmetic, block_partial(): mask_old = (slots[None, :] < live_len[:, None])[:, None, None, None, :]  10.2 us
  transfers between devices with their start and end apart: 63, of which 2 were waited for; matrix products, arithmetic and copies ran while one was open for 35% of the time, Pallas kernels for 0%

commit v1 on v0

v1 whole, which is shorter than its diff:
```python
import functools
import math

import jax
import jax.numpy as jnp
from jax import lax
from jax.experimental import pallas as pl
from jax.experimental.pallas import tpu as pltpu
from jax.sharding import PartitionSpec as P

HEAD_DIM = 128
BLOCK = 128
STEP = 256
META = 8
CODE = 16
NEVER = -1e30
FLOOR = -2000.0
NT = (((1,), (1,)), ((), ()))
TN = (((0,), (0,)), ((), ()))


def passed_along(x, by):
    size = lax.axis_size("inst")
    return lax.ppermute(x, "inst", [(i, (i + by) % size) for i in range(size)])


def meta_rows(rows, one, two, three):
    row = lax.broadcasted_iota(jnp.int32, (rows, one.shape[1]), 0)
    return jnp.where(row == 0, one, jnp.where(row == 1, two, three))


def whole(x):
    return jnp.floor(x + 0.5)


def coded(level, mean, out, sl):
    power = jnp.ceil(jnp.log2(jnp.maximum(jnp.max(jnp.abs(mean), axis=0, keepdims=True), 1e-30)))
    steps = whole(mean * jnp.exp2(15.0 - power))
    out[:HEAD_DIM, sl] = jnp.clip(steps, -32767.0, 32767.0).astype(jnp.int32).astype(jnp.int16)
    eighths = whole(level * 8.0)
    rest = whole((level - eighths * 0.125) * 2.0**18)
    out[HEAD_DIM:, sl] = meta_rows(CODE, eighths, rest, power).astype(jnp.int32).astype(jnp.int16)


def code_part(top, total, numer, out, sl):
    held = jnp.maximum(total, 1e-30)
    coded(jnp.maximum(top + jnp.log2(held), FLOOR), numer * (1.0 / held), out, sl)


def decoded(msg, sl):
    x = msg[:, sl].astype(jnp.int32).astype(jnp.float32)
    level = x[HEAD_DIM : HEAD_DIM + 1] * 0.125 + x[HEAD_DIM + 1 : HEAD_DIM + 2] * 2.0**-18
    return level, x[:HEAD_DIM] * jnp.exp2(x[HEAD_DIM + 2 : HEAD_DIM + 3] - 15.0)


def joined(parts):
    top = functools.reduce(jnp.maximum, [p[0] for p in parts])
    total, numer = 0.0, 0.0
    for t, l, n in parts:
        by = jnp.exp2(t - top)
        total = total + by * l
        numer = numer + by * n
    return top, total, numer


def held_part(ref, sl):
    return ref[HEAD_DIM : HEAD_DIM + 1, sl], ref[HEAD_DIM + 1 : HEAD_DIM + 2, sl], ref[:HEAD_DIM, sl]


def sent_part(msg, sl):
    level, mean = decoded(msg, sl)
    return level, 1.0, mean


def part_kernel(offsets, codes, members, tokens, rows, info, *refs):
    n = len(offsets)
    q_refs, fresh_ref, kv_ref = refs[:n], refs[n], refs[n + 1]
    out_refs, s_ref, o_ref = refs[n + 2 : 2 * n + 2], refs[2 * n + 2], refs[2 * n + 3]
    forks = kv_ref.shape[0]
    cap = kv_ref.shape[1]
    lanes = n * rows
    g = pl.program_id(0)
    me = info[0]
    unit = math.log2(math.e) / math.sqrt(HEAD_DIM)

    lane = lax.broadcasted_iota(jnp.int32, (1, lanes), 1)
    first = jnp.zeros((1, lanes), jnp.int32)
    for b, off in enumerate(offsets):
        here = lax.rem(me + (off + members), members) * tokens
        first = jnp.where((lane >= b * rows) & (lane < (b + 1) * rows), here, first)
    q_token = first + lax.rem(lane, tokens)
    u = lax.broadcasted_iota(jnp.int32, (2 * tokens, lanes), 0)
    seen = (u < tokens) & (me * tokens + u <= q_token)

    def one(j, steps):
        q = jnp.concatenate([r[j, :rows] for r in q_refs], axis=0)
        fresh = fresh_ref[j]
        live = info[1 + g * forks + j]
        s_new = lax.dot_general(fresh, q, NT, preferred_element_type=jnp.float32)
        s_new = jnp.where(seen, s_new, -jnp.inf)
        top = jnp.max(s_new, axis=0, keepdims=True)
        for c in range(steps):
            at = c * STEP
            s = lax.dot_general(
                kv_ref[j, at : at + STEP, :HEAD_DIM], q, NT, preferred_element_type=jnp.float32
            )
            if c == steps - 1:
                tail = jnp.where(at + BLOCK < live, s[BLOCK:], -jnp.inf)
                s_ref[at : at + BLOCK] = s[:BLOCK]
                s_ref[at + BLOCK : at + STEP] = tail
                top = jnp.maximum(top, jnp.max(s[:BLOCK], axis=0, keepdims=True))
                top = jnp.maximum(top, jnp.max(tail, axis=0, keepdims=True))
            else:
                s_ref[at : at + STEP] = s
                top = jnp.maximum(top, jnp.max(s, axis=0, keepdims=True))
        top = jnp.maximum(top, NEVER)
        w = jnp.exp2((s_new - top) * unit)
        total = jnp.sum(w, axis=0, keepdims=True)
        w = jnp.concatenate([w[tokens:], w[:tokens]], axis=0)
        numer = lax.dot_general(fresh, w.astype(jnp.bfloat16), TN, preferred_element_type=jnp.float32)
        for c in range(steps):
            at = c * STEP
            w = jnp.exp2((s_ref[at : at + STEP] - top) * unit)
            total = total + jnp.sum(w, axis=0, keepdims=True)
            numer = numer + lax.dot_general(
                kv_ref[j, at : at + STEP, HEAD_DIM:],
                w.astype(jnp.bfloat16),
                TN,
                preferred_element_type=jnp.float32,
            )
        o_ref[j, :HEAD_DIM] = numer
        row = lax.broadcasted_iota(jnp.int32, (META, lanes), 0)
        o_ref[j, HEAD_DIM:] = jnp.where(row == 0, top * unit, total)

    def fork(j, carry):
        live = info[1 + g * forks + j]
        for steps in range(cap // STEP + 1):
            pl.when((live > (steps - 1) * STEP) & (live <= steps * STEP))(
                functools.partial(one, j, steps)
            )
        return carry

    lax.fori_loop(0, forks, fork, 0)
    for b in range(n):
        o = jnp.concatenate([o_ref[j, :, b * rows : (b + 1) * rows] for j in range(forks)], axis=1)
        if codes[b]:
            code_part(o[HEAD_DIM : HEAD_DIM + 1], o[HEAD_DIM + 1 : HEAD_DIM + 2], o[:HEAD_DIM], out_refs[b], slice(None))
        else:
            out_refs[b][...] = o


def parts_of(blocks_q, offsets, codes, info, cache, fresh, members, tokens):
    n = len(offsets)
    forks, carried, _ = blocks_q[0].shape
    rows = carried - 2 * tokens
    both = 128 // rows
    cap, width = cache.shape[1:]
    keys = cap + tokens
    lanes = n * rows
    heights = [HEAD_DIM + (CODE if c else META) for c in codes]
    return pl.pallas_call(
        functools.partial(part_kernel, offsets, codes, members, tokens, rows),
        grid_spec=pltpu.PrefetchScalarGridSpec(
            num_scalar_prefetch=1,
            grid=(forks // both,),
            in_specs=[pl.BlockSpec((both, carried, HEAD_DIM), lambda g, i: (g, 0, 0))] * n
            + [
                pl.BlockSpec((both, 2 * tokens, HEAD_DIM), lambda g, i: (g, rows // (2 * tokens), 0)),
                pl.BlockSpec((both, cap, width), lambda g, i: (g, 0, 0)),
            ],
            out_specs=[pl.BlockSpec((h, both * rows), lambda g, i: (0, g)) for h in heights],
            scratch_shapes=[
                pltpu.VMEM((cap, lanes), jnp.float32),
                pltpu.VMEM((both, HEAD_DIM + META, lanes), jnp.float32),
            ],
        ),
        out_shape=[
            jax.ShapeDtypeStruct((h, forks * rows), jnp.int16 if c else jnp.float32)
            for h, c in zip(heights, codes)
        ],
        compiler_params=pltpu.CompilerParams(vmem_limit_bytes=8 * 2**20),
        cost_estimate=pl.CostEstimate(
            flops=4 * forks * lanes * keys * HEAD_DIM,
            transcendentals=forks * lanes * keys,
            bytes_accessed=2 * forks * keys * width,
        ),
        name="parts",
    )(info, *blocks_q, fresh, cache)


def merge_kernel(*refs):
    n = len(refs) // 3
    for k in range(n):
        msg, part, out = refs[2 * k], refs[2 * k + 1], refs[2 * n + k]
        for at in range(0, msg.shape[1], 128):
            sl = slice(at, at + 128)
            top, total, numer = joined([sent_part(msg, sl), held_part(part, sl)])
            code_part(top, total, numer, out, sl)


def merge(*pairs):
    return pl.pallas_call(
        merge_kernel,
        out_shape=[jax.ShapeDtypeStruct(pairs[2 * k].shape, jnp.int16) for k in range(len(pairs) // 2)],
        compiler_params=pltpu.CompilerParams(vmem_limit_bytes=8 * 2**20),
        name="merge",
    )(*pairs)


def finish_kernel(tokens, rows, info, span, own, right, left, out):
    me = info[0]
    forks = own.shape[1] // rows
    both = 128 // rows
    spot = lax.rem(lax.broadcasted_iota(jnp.int32, (rows, HEAD_DIM), 0), tokens) + me * tokens
    for g in range(forks // both):
        sl = slice(g * 128, (g + 1) * 128)
        _, total, numer = joined([held_part(own, sl), sent_part(right, sl), sent_part(left, sl)])
        turned = (numer / total).T
        for j in range(both):
            f = g * both + j
            value = turned[j * rows : (j + 1) * rows]
            out[f] = jnp.where(spot < span[f], value, 0.0).astype(jnp.bfloat16)


def finish(info, span, own, right, left, tokens, rows):
    forks = own.shape[1] // rows
    smem = pl.BlockSpec(memory_space=pltpu.SMEM)
    vmem = pl.BlockSpec(memory_space=pltpu.VMEM)
    return pl.pallas_call(
        functools.partial(finish_kernel, tokens, rows),
        in_specs=[smem, smem, vmem, vmem, vmem],
        out_specs=vmem,
        out_shape=jax.ShapeDtypeStruct((forks, rows, HEAD_DIM), jnp.bfloat16),
        compiler_params=pltpu.CompilerParams(vmem_limit_bytes=8 * 2**20),
        name="finish",
    )(info, span, own, right, left)


def own_kernel(offsets, tokens, info, span, owner, *refs):
    members = len(offsets)
    out = refs[members]
    me = info[0]
    forks = refs[0].shape[0]
    row = lax.rem(lax.broadcasted_iota(jnp.int32, (2 * tokens, HEAD_DIM), 0), tokens)
    for off, ref in zip(offsets, refs):
        first = lax.rem(me + (off + members), members) * tokens
        picked = jnp.zeros((2 * tokens, HEAD_DIM), jnp.float32)
        for f in range(forks):
            mine = (owner[f] == me) & (row + first < span[f])
            picked = jnp.where(mine, ref[f].astype(jnp.float32), picked)
        at = pl.ds(pl.multiple_of(first, tokens), tokens)
        out[at, :HEAD_DIM] = picked[:tokens]
        out[at, HEAD_DIM:] = picked[tokens:]


def own_kv(info, span, owner, q, tokens, width):
    offsets = tuple(q)
    forks, carried, _ = q[0].shape
    smem = pl.BlockSpec(memory_space=pltpu.SMEM)
    at = carried // (2 * tokens) - 1
    tokens_all = len(offsets) * tokens
    return pl.pallas_call(
        functools.partial(own_kernel, offsets, tokens),
        grid=(1,),
        in_specs=[smem] * 3
        + [pl.BlockSpec((forks, 2 * tokens, HEAD_DIM), lambda g: (0, at, 0))] * len(offsets),
        out_specs=pl.BlockSpec((tokens_all, width), lambda g: (0, 0)),
        out_shape=jax.ShapeDtypeStruct((tokens_all, width), jnp.float32),
        compiler_params=pltpu.CompilerParams(vmem_limit_bytes=8 * 2**20),
        name="own_kv",
    )(info, span, owner, *[q[o] for o in offsets]).astype(jnp.bfloat16)


def body(queries, tool_key_value, cache, placed, blocks, span_len, owner):
    forks, tokens, width = tool_key_value.shape
    heads = queries.shape[2] // HEAD_DIM
    rows = heads * tokens
    me = lax.axis_index("inst")
    members = lax.axis_size("inst")
    half = members // 2
    live = placed[:, 0] * blocks[:, 0] * BLOCK
    info = jnp.concatenate([me.astype(jnp.int32)[None], live])
    own_q = queries.reshape(forks, tokens, heads, HEAD_DIM).transpose(0, 2, 1, 3)
    own_kv_rows = tool_key_value.reshape(forks, tokens, 2, HEAD_DIM).transpose(0, 2, 1, 3)
    own_q = jnp.concatenate(
        [own_q.reshape(forks, rows, HEAD_DIM), own_kv_rows.reshape(forks, 2 * tokens, HEAD_DIM)], axis=1
    )

    q = {0: own_q}
    for k in range(1, half + 1):
        q[-k] = passed_along(q[1 - k], 1)
        if k < half:
            q[k] = passed_along(q[k - 1], -1)
    part = {}
    for offsets in CALLS(half):
        codes = tuple(o in (-half, half - 1) for o in offsets)
        got = parts_of([q[o] for o in offsets], offsets, codes, info, cache, own_q, members, tokens)
        part.update(zip(offsets, got))

    left, right = part[-half], part[half - 1]
    for k in range(half - 1, 0, -1):
        left = passed_along(left, -1)
        right = passed_along(right, 1)
        if k > 1:
            left, right = merge(left, part[-k], right, part[k - 1])
        else:
            (left,) = merge(left, part[-1])
    left = passed_along(left, -1)
    owned = own_kv(info, span_len, owner, q, tokens, width).reshape(1, 1, members * tokens, width)
    attended = finish(info, span_len, part[0], right, left, tokens, rows)
    attended = attended.reshape(forks, heads, tokens, HEAD_DIM).transpose(0, 2, 1, 3)
    return attended.reshape(forks, tokens, heads * HEAD_DIM), owned


def CALLS(half):
    order = [0]
    for k in range(1, half + 1):
        order += [-k, k] if k < half else [-k]
    calls = [tuple(order[i : i + 4]) for i in range(0, len(order) - 4, 4)]
    return calls + [tuple(order[-4:-1]), tuple(order[-1:])]


def solution(mesh):
    return jax.shard_map(
        body,
        mesh=mesh,
        in_specs=(
            P(("groups", "rep"), "inst", "tp"),
            P(("groups", "rep"), "inst", "tp"),
            P(("groups", "rep"), "inst", "tp"),
            P(("groups", "rep"), "inst"),
            P(("groups", "rep"), "inst"),
            P(("groups", "rep")),
            P(("groups", "rep")),
        ),
        out_specs=(P(("groups", "rep"), "inst", "tp"), P(("groups", "inst"), "rep", None, "tp")),
        check_vma=False,
    )
```

time: 392 us -> 207 us (0.53)
  starting transfers between devices: 240 us -> 139 us
  other arithmetic: 66.8 us -> 2.33 us
  matrix products: 48.3 us -> 0 us
  Pallas kernels: 0 us -> 31.9 us
  waiting for transfers between devices: 5.67 us -> 28.8 us
  local copies, waits for them, and re-layouts: 24.5 us -> 1.91 us
    ppermute x62 -> x30, starting transfers between devices: 196 us -> 139 us  [passed_along(): return lax.ppermute(x, 'inst', [(i, (i + by) % size) for i in range(size)])]
    dot_general x65 -> x0, matrix products: 48.3 us -> none  [the longest x16 20.3 us: block_partial(): jnp.einsum('fcjgp,fpjd->fcjgd', weight_old.astype(jnp.bfloat16), value_ca...]
    all_to_all x1 -> x0, starting transfers between devices: 43.7 us -> none  [copy_for_each(): lax.all_to_all(jnp.broadcast_to(shard[None], (size, *shard.shape)), axis,...]
    mul x30 -> x1, other arithmetic: 41.9 us -> 0.68 us  [body(): live = placed[:, 0] * blocks[:, 0] * BLOCK]
    pallas_call x0 -> x14, Pallas kernels: none -> 31.9 us  [the longest x5 27.6 us: parts_of(): pl.pallas_call(functools.partial(part_kernel, offsets, codes, members, to...]
    ppermute x62 -> x30, waiting for transfers between devices: 5.67 us -> 28.8 us  [passed_along(): return lax.ppermute(x, 'inst', [(i, (i + by) % size) for i in range(size)])]
    lt x18 -> x0, other arithmetic: 10.9 us -> none  [the longest x17 10.2 us: block_partial(): mask_old = (slots[None, :] < live_len[:, None])[:, None, None, None, :]]
    while x45 -> x0, local copies, waits for them, and re-layouts: 9.88 us -> none
  transfers between devices with their start and end apart: 63 -> 30, of which waited for: 2 -> 15; matrix products, arithmetic and copies ran while one was open for 35% -> 1% of each run, Pallas kernels for 0% -> 14%
where the time goes in v1:
time: 207 us; the launch traced here: 205 us
  starting transfers between devices  139 us (67%)
  Pallas kernels  31.9 us (15%)
  waiting for transfers between devices  28.8 us (14%)
  other arithmetic  2.33 us (1%)
    ppermute x30, starting transfers between devices, passed_along(): return lax.ppermute(x, 'inst', [(i, (i + by) % size) for i in range(size)])  139 us
    ppermute x30, waiting for transfers between devices, passed_along(): return lax.ppermute(x, 'inst', [(i, (i + by) % size) for i in range(size)])  28.8 us
    pallas_call x5, Pallas kernels, parts_of(): pl.pallas_call(functools.partial(part_kernel, offsets, codes, members, to...  27.6 us
  transfers between devices with their start and end apart: 30, of which 15 were waited for; matrix products, arithmetic and copies ran while one was open for 1% of the time, Pallas kernels for 14%

profile of v1, /device:TPU:80, one launch (start us, length us, event | category | flops | bytes accessed | tf_op | source)
XLA Modules:
  0.0 205.1 jit_solution(1399749665668363324)
XLA Ops:
  0.6 0.9 pad_maximum_fusion.refs_0_.refs_4_.refs_1_.refs_3_
  1.6 6.0 %collective-permute-start = (bf16[8,80,128]{2,1,0:T(8,128)(2,1)S(1)}, bf16[8,80,128]{2,1,0:T(8,128)(2,1)S(1)}, u32[]{:S(2)}, u32[]{:S(2)}) collective-permute-start(bf16[8,80,128]{2,1,0:T(8,128)(2,1)S(1)} %pad_maximum_fusion.refs_0_.refs_4_.refs_1_.refs_3_), channel_id=1, source_target_pairs={{0,16},{16,32},{32,48},{48,64},{64,80},{80,96},{96,112},{112,128},... | collective-permute-start | bytes 491528 | tf_op jit(solution)/shard_map/ppermute | solution.py:24
  7.6 39.9 %collective-permute-start.1 = (bf16[8,80,128]{2,1,0:T(8,128)(2,1)S(1)}, bf16[8,80,128]{2,1,0:T(8,128)(2,1)S(1)}, u32[]{:S(2)}, u32[]{:S(2)}) collective-permute-start(bf16[8,80,128]{2,1,0:T(8,128)(2,1)S(1)} %pad_maximum_fusion.refs_0_.refs_4_.refs_1_.refs_3_), channel_id=1, source_target_pairs={{0,240},{16,0},{32,16},{48,32},{64,48},{80,64},{96,80},{112,96},{1... | collective-permute-start | bytes 491528 | tf_op jit(solution)/shard_map/ppermute | solution.py:24
  47.6 2.3 %collective-permute-done.refs_1_ = bf16[8,80,128]{2,1,0:T(8,128)(2,1)S(1)} collective-permute-done((bf16[8,80,128]{2,1,0:T(8,128)(2,1)S(1)}, bf16[8,80,128]{2,1,0:T(8,128)(2,1)S(1)}, u32[]{:S(2)}, u32[]{:S(2)}) %collective-permute-start) | collective-permute-done | bytes 163872 | tf_op jit(solution)/shard_map/ppermute | solution.py:24
  49.9 1.9 collective-permute-start.2
  51.8 5.2 %collective-permute-start.10 = (bf16[8,80,128]{2,1,0:T(8,128)(2,1)S(1)}, bf16[8,80,128]{2,1,0:T(8,128)(2,1)S(1)}, u32[]{:S(2)}, u32[]{:S(2)}) collective-permute-start(bf16[8,80,128]{2,1,0:T(8,128)(2,1)S(1)} %collective-permute-done.1.refs_2_), channel_id=1, source_target_pairs={{0,240},{16,0},{32,16},{48,32},{64,48},{80,64},{96,80},{112,96},{1... | collective-permute-start | bytes 491528 | tf_op jit(solution)/shard_map/ppermute | solution.py:24
  57.0 1.4 collective-permute-done.2.refs_3_
  58.4 1.9 collective-permute-start.3
  60.4 5.2 %collective-permute-start.11 = (bf16[8,80,128]{2,1,0:T(8,128)(2,1)S(1)}, bf16[8,80,128]{2,1,0:T(8,128)(2,1)S(1)}, u32[]{:S(2)}, u32[]{:S(2)}) collective-permute-start(bf16[8,80,128]{2,1,0:T(8,128)(2,1)S(1)} %collective-permute-done.10.refs_0_.refs_4_), channel_id=1, source_target_pairs={{0,240},{16,0},{32,16},{48,32},{64,48},{80,64},{96,80},{112,96},{1... | collective-permute-start | bytes 491528 | tf_op jit(solution)/shard_map/ppermute | solution.py:24
  65.5 1.3 collective-permute-done.3.refs_1_.refs_5_
  66.9 1.9 collective-permute-start.4
  68.8 5.2 %collective-permute-start.12 = (bf16[8,80,128]{2,1,0:T(8,128)(2,1)S(1)}, bf16[8,80,128]{2,1,0:T(8,128)(2,1)S(1)}, u32[]{:S(2)}, u32[]{:S(2)}) collective-permute-start(bf16[8,80,128]{2,1,0:T(8,128)(2,1)S(1)} %collective-permute-done.11.refs_2_.refs_6_), channel_id=1, source_target_pairs={{0,240},{16,0},{32,16},{48,32},{64,48},{80,64},{96,80},{112,96},{1... | collective-permute-start | bytes 491528 | tf_op jit(solution)/shard_map/ppermute | solution.py:24
  74.0 1.3 collective-permute-done.4.refs_3_.refs_7_
  75.3 1.9 collective-permute-start.5
  77.3 5.2 %collective-permute-start.13 = (bf16[8,80,128]{2,1,0:T(8,128)(2,1)S(1)}, bf16[8,80,128]{2,1,0:T(8,128)(2,1)S(1)}, u32[]{:S(2)}, u32[]{:S(2)}) collective-permute-start(bf16[8,80,128]{2,1,0:T(8,128)(2,1)S(1)} %collective-permute-done.12.refs_0_.refs_8_), channel_id=1, source_target_pairs={{0,240},{16,0},{32,16},{48,32},{64,48},{80,64},{96,80},{112,96},{1... | collective-permute-start | bytes 491528 | tf_op jit(solution)/shard_map/ppermute | solution.py:24
  82.4 1.3 collective-permute-done.5.refs_1_.refs_9_
  83.7 1.9 collective-permute-start.6
  85.7 5.2 %collective-permute-start.14 = (bf16[8,80,128]{2,1,0:T(8,128)(2,1)S(1)}, bf16[8,80,128]{2,1,0:T(8,128)(2,1)S(1)}, u32[]{:S(2)}, u32[]{:S(2)}) collective-permute-start(bf16[8,80,128]{2,1,0:T(8,128)(2,1)S(1)} %collective-permute-done.13.refs_2_.refs_10_), channel_id=1, source_target_pairs={{0,240},{16,0},{32,16},{48,32},{64,48},{80,64},{96,80},{112,96},{1... | collective-permute-start | bytes 491528 | tf_op jit(solution)/shard_map/ppermute | solution.py:24
  90.9 1.7 collective-permute-done.6.refs_3_.refs_11_
  92.6 1.9 collective-permute-start.7
  94.5 5.4 %collective-permute-start.15 = (bf16[8,80,128]{2,1,0:T(8,128)(2,1)S(1)}, bf16[8,80,128]{2,1,0:T(8,128)(2,1)S(1)}, u32[]{:S(2)}, u32[]{:S(2)}) collective-permute-start(bf16[8,80,128]{2,1,0:T(8,128)(2,1)S(1)} %collective-permute-done.14.refs_0_.refs_12_), channel_id=1, source_target_pairs={{0,240},{16,0},{32,16},{48,32},{64,48},{80,64},{96,80},{112,96},{1... | collective-permute-start | bytes 491528 | tf_op jit(solution)/shard_map/ppermute | solution.py:24
  100.0 0.7 multiply_bitcast_fusion
  100.7 1.9 collective-permute-done.7.refs_1_.refs_13_
  102.6 1.9 collective-permute-start.8
  104.5 0.1 pad_add_fusion.info
  104.6 1.9 copy-done
  106.5 5.8 %parts.7 = (f32[136,512]{1,0:T(8,128)S(1)}, f32[136,512]{1,0:T(8,128)S(1)}, s16[144,512]{1,0:T(8,128)(2,1)S(1)}) custom-call(s32[9]{0:T(128)S(1)} %pad_add_fusion.info, bf16[8,80,128]{2,1,0:T(8,128)(2,1)S(1)} %collective-permute-done.14.refs_0_.refs_12_, bf16[8,80,128]{2,1,0:T(8,128)(2,1)S(1)} %collective-permute-done.7.refs_1_.refs_13_, ...), custom_call_target="tpu_custom_call" | custom-call | flops 610271232 | bytes 3178496 | tf_op jit(solution)/shard_map/parts/pallas_call | solution.py:161
  112.3 2.2 %collective-permute-start.16 = (s16[144,512]{1,0:T(8,128)(2,1)S(1)}, s16[144,512]{1,0:T(8,128)(2,1)S(1)}, u32[]{:S(2)}, u32[]{:S(2)}) collective-permute-start(s16[144,512]{1,0:T(8,128)(2,1)S(1)} %get-tuple-element.31), channel_id=1, source_target_pairs={{0,16},{16,32},{32,48},{48,64},{64,80},{80,96},{96,112},{112,128},... | collective-permute-start | bytes 442376 | tf_op jit(solution)/shard_map/ppermute | solution.py:24
  114.5 4.6 %parts.6 = s16[144,512]{1,0:T(8,128)(2,1)S(1)} custom-call(s32[9]{0:T(128)S(1)} %pad_add_fusion.info, bf16[8,80,128]{2,1,0:T(8,128)(2,1)S(1)} %collective-permute-done.8.refs_0_.refs_15_, bf16[8,80,128]{2,1,0:T(8,128)(2,1)S(1)} %pad_maximum_fusion.refs_0_.refs_4_.refs_1_.refs_3_, bf16[8,768,256]{2,1,0:T(8,128)(2,1)S(1)} %copy-done), custom_call_target="tpu_custom_call" | custom-call | flops 203423744 | bytes 3178496 | tf_op jit(solution)/shard_map/parts/pallas_call | solution.py:161
  119.1 4.9 %collective-permute-start.9 = (s16[144,512]{1,0:T(8,128)(2,1)S(1)}, s16[144,512]{1,0:T(8,128)(2,1)S(1)}, u32[]{:S(2)}, u32[]{:S(2)}) collective-permute-start(s16[144,512]{1,0:T(8,128)(2,1)S(1)} %parts.6), channel_id=1, source_target_pairs={{0,240},{16,0},{32,16},{48,32},{64,48},{80,64},{96,80},{112,96},{1... | collective-permute-start | bytes 442376 | tf_op jit(solution)/shard_map/ppermute | solution.py:24
  124.1 2.6 %collective-permute-done.9.refs_0_ = s16[144,512]{1,0:T(8,128)(2,1)S(1)} collective-permute-done((s16[144,512]{1,0:T(8,128)(2,1)S(1)}, s16[144,512]{1,0:T(8,128)(2,1)S(1)}, u32[]{:S(2)}, u32[]{:S(2)}) %collective-permute-start.9) | collective-permute-done | bytes 147488 | tf_op jit(solution)/shard_map/ppermute | solution.py:24
  126.7 0.3 merge.7
  127.0 5.6 %collective-permute-start.17 = (s16[144,512]{1,0:T(8,128)(2,1)S(1)}, s16[144,512]{1,0:T(8,128)(2,1)S(1)}, u32[]{:S(2)}, u32[]{:S(2)}) collective-permute-start(s16[144,512]{1,0:T(8,128)(2,1)S(1)} %get-tuple-element.33), channel_id=1, source_target_pairs={{0,240},{16,0},{32,16},{48,32},{64,48},{80,64},{96,80},{112,96},{1... | collective-permute-start | bytes 442376 | tf_op jit(solution)/shard_map/ppermute | solution.py:24
  132.7 2.0 collective-permute-start.18
  134.6 5.8 %parts.8 = (f32[136,512]{1,0:T(8,128)S(1)}, f32[136,512]{1,0:T(8,128)S(1)}, f32[136,512]{1,0:T(8,128)S(1)}, f32[136,512]{1,0:T(8,128)S(1)}) custom-call(s32[9]{0:T(128)S(1)} %pad_add_fusion.info, bf16[8,80,128]{2,1,0:T(8,128)(2,1)S(1)} %collective-permute-done.12.refs_0_.refs_8_, bf16[8,80,128]{2,1,0:T(8,128)(2,1)S(1)} %collective-permute-done.5.refs_1_.refs_9_, ...), custom_call_target="tpu_custom_call" | custom-call | flops 813694976 | bytes 3178496 | tf_op jit(solution)/shard_map/parts/pallas_call | solution.py:161
  140.4 0.5 collective-permute-done.18.refs_2_
  140.9 0.3 merge.8
  141.3 4.1 %collective-permute-start.19 = (s16[144,512]{1,0:T(8,128)(2,1)S(1)}, s16[144,512]{1,0:T(8,128)(2,1)S(1)}, u32[]{:S(2)}, u32[]{:S(2)}) collective-permute-start(s16[144,512]{1,0:T(8,128)(2,1)S(1)} %get-tuple-element.37), channel_id=1, source_target_pairs={{0,240},{16,0},{32,16},{48,32},{64,48},{80,64},{96,80},{112,96},{1... | collective-permute-start | bytes 442376 | tf_op jit(solution)/shard_map/ppermute | solution.py:24
  145.4 2.0 collective-permute-start.20
  147.4 2.1 %collective-permute-done.19.refs_0_ = s16[144,512]{1,0:T(8,128)(2,1)S(1)} collective-permute-done((s16[144,512]{1,0:T(8,128)(2,1)S(1)}, s16[144,512]{1,0:T(8,128)(2,1)S(1)}, u32[]{:S(2)}, u32[]{:S(2)}) %collective-permute-start.19) | collective-permute-done | bytes 147488 | tf_op jit(solution)/shard_map/ppermute | solution.py:24
  149.4 4.3 %collective-permute-done.20.refs_2_ = s16[144,512]{1,0:T(8,128)(2,1)S(1)} collective-permute-done((s16[144,512]{1,0:T(8,128)(2,1)S(1)}, s16[144,512]{1,0:T(8,128)(2,1)S(1)}, u32[]{:S(2)}, u32[]{:S(2)}) %collective-permute-start.20) | collective-permute-done | bytes 147488 | tf_op jit(solution)/shard_map/ppermute | solution.py:24
  153.7 0.3 merge.9
  154.0 2.0 collective-permute-start.21
  156.0 4.0 %collective-permute-start.22 = (s16[144,512]{1,0:T(8,128)(2,1)S(1)}, s16[144,512]{1,0:T(8,128)(2,1)S(1)}, u32[]{:S(2)}, u32[]{:S(2)}) collective-permute-start(s16[144,512]{1,0:T(8,128)(2,1)S(1)} %get-tuple-element.43), channel_id=1, source_target_pairs={{0,16},{16,32},{32,48},{48,64},{64,80},{80,96},{96,112},{112,128},... | collective-permute-start | bytes 442376 | tf_op jit(solution)/shard_map/ppermute | solution.py:24
  159.9 5.8 %parts.9 = (f32[136,512]{1,0:T(8,128)S(1)}, f32[136,512]{1,0:T(8,128)S(1)}, f32[136,512]{1,0:T(8,128)S(1)}, f32[136,512]{1,0:T(8,128)S(1)}) custom-call(s32[9]{0:T(128)S(1)} %pad_add_fusion.info, bf16[8,80,128]{2,1,0:T(8,128)(2,1)S(1)} %collective-permute-done.10.refs_0_.refs_4_, bf16[8,80,128]{2,1,0:T(8,128)(2,1)S(1)} %collective-permute-done.3.refs_1_.refs_5_, ...), custom_call_target="tpu_custom_call" | custom-call | flops 813694976 | bytes 3178496 | tf_op jit(solution)/shard_map/parts/pallas_call | solution.py:161
  165.7 0.3 merge.10
  166.1 2.6 %collective-permute-start.23 = (s16[144,512]{1,0:T(8,128)(2,1)S(1)}, s16[144,512]{1,0:T(8,128)(2,1)S(1)}, u32[]{:S(2)}, u32[]{:S(2)}) collective-permute-start(s16[144,512]{1,0:T(8,128)(2,1)S(1)} %get-tuple-element.45), channel_id=1, source_target_pairs={{0,240},{16,0},{32,16},{48,32},{64,48},{80,64},{96,80},{112,96},{1... | collective-permute-start | bytes 442376 | tf_op jit(solution)/shard_map/ppermute | solution.py:24
  168.7 3.3 %collective-permute-start.24 = (s16[144,512]{1,0:T(8,128)(2,1)S(1)}, s16[144,512]{1,0:T(8,128)(2,1)S(1)}, u32[]{:S(2)}, u32[]{:S(2)}) collective-permute-start(s16[144,512]{1,0:T(8,128)(2,1)S(1)} %get-tuple-element.47), channel_id=1, source_target_pairs={{0,16},{16,32},{32,48},{48,64},{64,80},{80,96},{96,112},{112,128},... | collective-permute-start | bytes 442376 | tf_op jit(solution)/shard_map/ppermute | solution.py:24
  172.0 1.7 collective-permute-done.23.refs_0_
  173.7 3.3 %collective-permute-done.24.refs_2_ = s16[144,512]{1,0:T(8,128)(2,1)S(1)} collective-permute-done((s16[144,512]{1,0:T(8,128)(2,1)S(1)}, s16[144,512]{1,0:T(8,128)(2,1)S(1)}, u32[]{:S(2)}, u32[]{:S(2)}) %collective-permute-start.24) | collective-permute-done | bytes 147488 | tf_op jit(solution)/shard_map/ppermute | solution.py:24
  177.0 0.3 merge.11
  177.3 2.0 collective-permute-start.25
  179.3 4.0 %collective-permute-start.26 = (s16[144,512]{1,0:T(8,128)(2,1)S(1)}, s16[144,512]{1,0:T(8,128)(2,1)S(1)}, u32[]{:S(2)}, u32[]{:S(2)}) collective-permute-start(s16[144,512]{1,0:T(8,128)(2,1)S(1)} %get-tuple-element.51), channel_id=1, source_target_pairs={{0,16},{16,32},{32,48},{48,64},{64,80},{80,96},{96,112},{112,128},... | collective-permute-start | bytes 442376 | tf_op jit(solution)/shard_map/ppermute | solution.py:24
  183.3 5.8 %parts.5 = (f32[136,512]{1,0:T(8,128)S(1)}, f32[136,512]{1,0:T(8,128)S(1)}, f32[136,512]{1,0:T(8,128)S(1)}, f32[136,512]{1,0:T(8,128)S(1)}) custom-call(s32[9]{0:T(128)S(1)} %pad_add_fusion.info, bf16[8,80,128]{2,1,0:T(8,128)(2,1)S(1)} %pad_maximum_fusion.refs_0_.refs_4_.refs_1_.refs_3_, bf16[8,80,128]{2,1,0:T(8,128)(2,1)S(1)} %collective-permute-done.refs_1_, ...), custom_call_target="tpu_custom_call" | custom-call | flops 813694976 | bytes 3178496 | tf_op jit(solution)/shard_map/parts/pallas_call | solution.py:161
  189.1 0.3 merge.12
  189.4 2.6 %collective-permute-start.28 = (s16[144,512]{1,0:T(8,128)(2,1)S(1)}, s16[144,512]{1,0:T(8,128)(2,1)S(1)}, u32[]{:S(2)}, u32[]{:S(2)}) collective-permute-start(s16[144,512]{1,0:T(8,128)(2,1)S(1)} %get-tuple-element.54), channel_id=1, source_target_pairs={{0,240},{16,0},{32,16},{48,32},{64,48},{80,64},{96,80},{112,96},{1... | collective-permute-start | bytes 442376 | tf_op jit(solution)/shard_map/ppermute | solution.py:24
  192.1 0.7 own_kv.1
  192.8 3.3 %collective-permute-start.27 = (s16[144,512]{1,0:T(8,128)(2,1)S(1)}, s16[144,512]{1,0:T(8,128)(2,1)S(1)}, u32[]{:S(2)}, u32[]{:S(2)}) collective-permute-start(s16[144,512]{1,0:T(8,128)(2,1)S(1)} %get-tuple-element.53), channel_id=1, source_target_pairs={{0,16},{16,32},{32,48},{48,64},{64,80},{80,96},{96,112},{112,128},... | collective-permute-start | bytes 442376 | tf_op jit(solution)/shard_map/ppermute | solution.py:24
  196.1 0.4 collective-permute-done.28.refs_0_
  196.4 0.2 merge.13
  196.6 3.9 %collective-permute-start.29 = (s16[144,512]{1,0:T(8,128)(2,1)S(1)}, s16[144,512]{1,0:T(8,128)(2,1)S(1)}, u32[]{:S(2)}, u32[]{:S(2)}) collective-permute-start(s16[144,512]{1,0:T(8,128)(2,1)S(1)} %merge.13), channel_id=1, source_target_pairs={{0,240},{16,0},{32,16},{48,32},{64,48},{80,64},{96,80},{112,96},{1... | collective-permute-start | bytes 442376 | tf_op jit(solution)/shard_map/ppermute | solution.py:24
  200.5 0.6 convert_bitcast_fusion
  201.1 2.6 %collective-permute-done.29.left = s16[144,512]{1,0:T(8,128)(2,1)S(1)} collective-permute-done((s16[144,512]{1,0:T(8,128)(2,1)S(1)}, s16[144,512]{1,0:T(8,128)(2,1)S(1)}, u32[]{:S(2)}, u32[]{:S(2)}) %collective-permute-start.29) | collective-permute-done | bytes 147488 | tf_op jit(solution)/shard_map/ppermute | solution.py:24
  203.7 1.4 finish.1
  (22 shorter events, 0.1 us)
Async XLA Ops:
  1.6 48.3 %collective-permute-start = (bf16[8,80,128]{2,1,0:T(8,128)(2,1)S(1)}, bf16[8,80,128]{2,1,0:T(8,128)(2,1)S(1)}, u32[]{:S(2)}, u32[]{:S(2)}) collective-permute-start(bf16[8,80,128]{2,1,0:T(8,128)(2,1)S(1)} %pad_maximum_fusion.refs_0_.refs_4_.refs_1_.refs_3_), channel_id=1, source_target_pairs={{0,16},{16,32},{32,48},{48,64},{64,80},{80,96},{96,112},{112,128},... | collective-permute-start | bytes 491528 | tf_op jit(solution)/shard_map/ppermute | solution.py:24
  7.6 44.2 %collective-permute-start.1 = (bf16[8,80,128]{2,1,0:T(8,128)(2,1)S(1)}, bf16[8,80,128]{2,1,0:T(8,128)(2,1)S(1)}, u32[]{:S(2)}, u32[]{:S(2)}) collective-permute-start(bf16[8,80,128]{2,1,0:T(8,128)(2,1)S(1)} %pad_maximum_fusion.refs_0_.refs_4_.refs_1_.refs_3_), channel_id=1, source_target_pairs={{0,240},{16,0},{32,16},{48,32},{64,48},{80,64},{96,80},{112,96},{1... | collective-permute-start | bytes 491528 | tf_op jit(solution)/shard_map/ppermute | solution.py:24
  49.9 8.6 %collective-permute-start.2 = (bf16[8,80,128]{2,1,0:T(8,128)(2,1)S(1)}, bf16[8,80,128]{2,1,0:T(8,128)(2,1)S(1)}, u32[]{:S(2)}, u32[]{:S(2)}) collective-permute-start(bf16[8,80,128]{2,1,0:T(8,128)(2,1)S(1)} %collective-permute-done.refs_1_), channel_id=1, source_target_pairs={{0,16},{16,32},{32,48},{48,64},{64,80},{80,96},{96,112},{112,128},... | collective-permute-start | bytes 491528 | tf_op jit(solution)/shard_map/ppermute | solution.py:24
  51.8 8.5 %collective-permute-start.10 = (bf16[8,80,128]{2,1,0:T(8,128)(2,1)S(1)}, bf16[8,80,128]{2,1,0:T(8,128)(2,1)S(1)}, u32[]{:S(2)}, u32[]{:S(2)}) collective-permute-start(bf16[8,80,128]{2,1,0:T(8,128)(2,1)S(1)} %collective-permute-done.1.refs_2_), channel_id=1, source_target_pairs={{0,240},{16,0},{32,16},{48,32},{64,48},{80,64},{96,80},{112,96},{1... | collective-permute-start | bytes 491528 | tf_op jit(solution)/shard_map/ppermute | solution.py:24
  58.4 8.4 %collective-permute-start.3 = (bf16[8,80,128]{2,1,0:T(8,128)(2,1)S(1)}, bf16[8,80,128]{2,1,0:T(8,128)(2,1)S(1)}, u32[]{:S(2)}, u32[]{:S(2)}) collective-permute-start(bf16[8,80,128]{2,1,0:T(8,128)(2,1)S(1)} %collective-permute-done.2.refs_3_), channel_id=1, source_target_pairs={{0,16},{16,32},{32,48},{48,64},{64,80},{80,96},{96,112},{112,128},... | collective-permute-start | bytes 491528 | tf_op jit(solution)/shard_map/ppermute | solution.py:24
  60.4 8.4 %collective-permute-start.11 = (bf16[8,80,128]{2,1,0:T(8,128)(2,1)S(1)}, bf16[8,80,128]{2,1,0:T(8,128)(2,1)S(1)}, u32[]{:S(2)}, u32[]{:S(2)}) collective-permute-start(bf16[8,80,128]{2,1,0:T(8,128)(2,1)S(1)} %collective-permute-done.10.refs_0_.refs_4_), channel_id=1, source_target_pairs={{0,240},{16,0},{32,16},{48,32},{64,48},{80,64},{96,80},{112,96},{1... | collective-permute-start | bytes 491528 | tf_op jit(solution)/shard_map/ppermute | solution.py:24
  66.9 8.4 %collective-permute-start.4 = (bf16[8,80,128]{2,1,0:T(8,128)(2,1)S(1)}, bf16[8,80,128]{2,1,0:T(8,128)(2,1)S(1)}, u32[]{:S(2)}, u32[]{:S(2)}) collective-permute-start(bf16[8,80,128]{2,1,0:T(8,128)(2,1)S(1)} %collective-permute-done.3.refs_1_.refs_5_), channel_id=1, source_target_pairs={{0,16},{16,32},{32,48},{48,64},{64,80},{80,96},{96,112},{112,128},... | collective-permute-start | bytes 491528 | tf_op jit(solution)/shard_map/ppermute | solution.py:24
  68.8 8.4 %collective-permute-start.12 = (bf16[8,80,128]{2,1,0:T(8,128)(2,1)S(1)}, bf16[8,80,128]{2,1,0:T(8,128)(2,1)S(1)}, u32[]{:S(2)}, u32[]{:S(2)}) collective-permute-start(bf16[8,80,128]{2,1,0:T(8,128)(2,1)S(1)} %collective-permute-done.11.refs_2_.refs_6_), channel_id=1, source_target_pairs={{0,240},{16,0},{32,16},{48,32},{64,48},{80,64},{96,80},{112,96},{1... | collective-permute-start | bytes 491528 | tf_op jit(solution)/shard_map/ppermute | solution.py:24
  75.3 8.4 %collective-permute-start.5 = (bf16[8,80,128]{2,1,0:T(8,128)(2,1)S(1)}, bf16[8,80,128]{2,1,0:T(8,128)(2,1)S(1)}, u32[]{:S(2)}, u32[]{:S(2)}) collective-permute-start(bf16[8,80,128]{2,1,0:T(8,128)(2,1)S(1)} %collective-permute-done.4.refs_3_.refs_7_), channel_id=1, source_target_pairs={{0,16},{16,32},{32,48},{48,64},{64,80},{80,96},{96,112},{112,128},... | collective-permute-start | bytes 491528 | tf_op jit(solution)/shard_map/ppermute | solution.py:24
  77.3 8.4 %collective-permute-start.13 = (bf16[8,80,128]{2,1,0:T(8,128)(2,1)S(1)}, bf16[8,80,128]{2,1,0:T(8,128)(2,1)S(1)}, u32[]{:S(2)}, u32[]{:S(2)}) collective-permute-start(bf16[8,80,128]{2,1,0:T(8,128)(2,1)S(1)} %collective-permute-done.12.refs_0_.refs_8_), channel_id=1, source_target_pairs={{0,240},{16,0},{32,16},{48,32},{64,48},{80,64},{96,80},{112,96},{1... | collective-permute-start | bytes 491528 | tf_op jit(solution)/shard_map/ppermute | solution.py:24
  83.7 8.9 %collective-permute-start.6 = (bf16[8,80,128]{2,1,0:T(8,128)(2,1)S(1)}, bf16[8,80,128]{2,1,0:T(8,128)(2,1)S(1)}, u32[]{:S(2)}, u32[]{:S(2)}) collective-permute-start(bf16[8,80,128]{2,1,0:T(8,128)(2,1)S(1)} %collective-permute-done.5.refs_1_.refs_9_), channel_id=1, source_target_pairs={{0,16},{16,32},{32,48},{48,64},{64,80},{80,96},{96,112},{112,128},... | collective-permute-start | bytes 491528 | tf_op jit(solution)/shard_map/ppermute | solution.py:24
  85.7 8.8 %collective-permute-start.14 = (bf16[8,80,128]{2,1,0:T(8,128)(2,1)S(1)}, bf16[8,80,128]{2,1,0:T(8,128)(2,1)S(1)}, u32[]{:S(2)}, u32[]{:S(2)}) collective-permute-start(bf16[8,80,128]{2,1,0:T(8,128)(2,1)S(1)} %collective-permute-done.13.refs_2_.refs_10_), channel_id=1, source_target_pairs={{0,240},{16,0},{32,16},{48,32},{64,48},{80,64},{96,80},{112,96},{1... | collective-permute-start | bytes 491528 | tf_op jit(solution)/shard_map/ppermute | solution.py:24
  92.6 10.0 %collective-permute-start.7 = (bf16[8,80,128]{2,1,0:T(8,128)(2,1)S(1)}, bf16[8,80,128]{2,1,0:T(8,128)(2,1)S(1)}, u32[]{:S(2)}, u32[]{:S(2)}) collective-permute-start(bf16[8,80,128]{2,1,0:T(8,128)(2,1)S(1)} %collective-permute-done.6.refs_3_.refs_11_), channel_id=1, source_target_pairs={{0,16},{16,32},{32,48},{48,64},{64,80},{80,96},{96,112},{112,128},... | collective-permute-start | bytes 491528 | tf_op jit(solution)/shard_map/ppermute | solution.py:24
  94.5 10.1 %collective-permute-start.15 = (bf16[8,80,128]{2,1,0:T(8,128)(2,1)S(1)}, bf16[8,80,128]{2,1,0:T(8,128)(2,1)S(1)}, u32[]{:S(2)}, u32[]{:S(2)}) collective-permute-start(bf16[8,80,128]{2,1,0:T(8,128)(2,1)S(1)} %collective-permute-done.14.refs_0_.refs_12_), channel_id=1, source_target_pairs={{0,240},{16,0},{32,16},{48,32},{64,48},{80,64},{96,80},{112,96},{1... | collective-permute-start | bytes 491528 | tf_op jit(solution)/shard_map/ppermute | solution.py:24
  102.6 11.9 %collective-permute-start.8 = (bf16[8,80,128]{2,1,0:T(8,128)(2,1)S(1)}, bf16[8,80,128]{2,1,0:T(8,128)(2,1)S(1)}, u32[]{:S(2)}, u32[]{:S(2)}) collective-permute-start(bf16[8,80,128]{2,1,0:T(8,128)(2,1)S(1)} %collective-permute-done.7.refs_1_.refs_13_), channel_id=1, source_target_pairs={{0,16},{16,32},{32,48},{48,64},{64,80},{80,96},{96,112},{112,128},... | collective-permute-start | bytes 491528 | tf_op jit(solution)/shard_map/ppermute | solution.py:24
  104.6 1.9 copy-start
  112.3 22.3 %copy-start.1 = (bf16[8,768,256]{2,1,0:T(8,128)(2,1)S(1)}, bf16[8,768,256]{2,1,0:T(8,128)(2,1)}, u32[]{:S(2)}) copy-start(bf16[8,768,256]{2,1,0:T(8,128)(2,1)} %refs_5_.5) | copy-start | bytes 9437188
  112.3 11.7 %collective-permute-start.16 = (s16[144,512]{1,0:T(8,128)(2,1)S(1)}, s16[144,512]{1,0:T(8,128)(2,1)S(1)}, u32[]{:S(2)}, u32[]{:S(2)}) collective-permute-start(s16[144,512]{1,0:T(8,128)(2,1)S(1)} %get-tuple-element.31), channel_id=1, source_target_pairs={{0,16},{16,32},{32,48},{48,64},{64,80},{80,96},{96,112},{112,128},... | collective-permute-start | bytes 442376 | tf_op jit(solution)/shard_map/ppermute | solution.py:24
  119.1 7.6 %collective-permute-start.9 = (s16[144,512]{1,0:T(8,128)(2,1)S(1)}, s16[144,512]{1,0:T(8,128)(2,1)S(1)}, u32[]{:S(2)}, u32[]{:S(2)}) collective-permute-start(s16[144,512]{1,0:T(8,128)(2,1)S(1)} %parts.6), channel_id=1, source_target_pairs={{0,240},{16,0},{32,16},{48,32},{64,48},{80,64},{96,80},{112,96},{1... | collective-permute-start | bytes 442376 | tf_op jit(solution)/shard_map/ppermute | solution.py:24
  127.0 13.4 %collective-permute-start.17 = (s16[144,512]{1,0:T(8,128)(2,1)S(1)}, s16[144,512]{1,0:T(8,128)(2,1)S(1)}, u32[]{:S(2)}, u32[]{:S(2)}) collective-permute-start(s16[144,512]{1,0:T(8,128)(2,1)S(1)} %get-tuple-element.33), channel_id=1, source_target_pairs={{0,240},{16,0},{32,16},{48,32},{64,48},{80,64},{96,80},{112,96},{1... | collective-permute-start | bytes 442376 | tf_op jit(solution)/shard_map/ppermute | solution.py:24
  132.7 8.3 %collective-permute-start.18 = (s16[144,512]{1,0:T(8,128)(2,1)S(1)}, s16[144,512]{1,0:T(8,128)(2,1)S(1)}, u32[]{:S(2)}, u32[]{:S(2)}) collective-permute-start(s16[144,512]{1,0:T(8,128)(2,1)S(1)} %get-tuple-element.35), channel_id=1, source_target_pairs={{0,16},{16,32},{32,48},{48,64},{64,80},{80,96},{96,112},{112,128},... | collective-permute-start | bytes 442376 | tf_op jit(solution)/shard_map/ppermute | solution.py:24
  141.3 8.2 %collective-permute-start.19 = (s16[144,512]{1,0:T(8,128)(2,1)S(1)}, s16[144,512]{1,0:T(8,128)(2,1)S(1)}, u32[]{:S(2)}, u32[]{:S(2)}) collective-permute-start(s16[144,512]{1,0:T(8,128)(2,1)S(1)} %get-tuple-element.37), channel_id=1, source_target_pairs={{0,240},{16,0},{32,16},{48,32},{64,48},{80,64},{96,80},{112,96},{1... | collective-permute-start | bytes 442376 | tf_op jit(solution)/shard_map/ppermute | solution.py:24
  145.4 8.3 %collective-permute-start.20 = (s16[144,512]{1,0:T(8,128)(2,1)S(1)}, s16[144,512]{1,0:T(8,128)(2,1)S(1)}, u32[]{:S(2)}, u32[]{:S(2)}) collective-permute-start(s16[144,512]{1,0:T(8,128)(2,1)S(1)} %get-tuple-element.39), channel_id=1, source_target_pairs={{0,16},{16,32},{32,48},{48,64},{64,80},{80,96},{96,112},{112,128},... | collective-permute-start | bytes 442376 | tf_op jit(solution)/shard_map/ppermute | solution.py:24
  154.0 11.7 %collective-permute-start.21 = (s16[144,512]{1,0:T(8,128)(2,1)S(1)}, s16[144,512]{1,0:T(8,128)(2,1)S(1)}, u32[]{:S(2)}, u32[]{:S(2)}) collective-permute-start(s16[144,512]{1,0:T(8,128)(2,1)S(1)} %get-tuple-element.41), channel_id=1, source_target_pairs={{0,240},{16,0},{32,16},{48,32},{64,48},{80,64},{96,80},{112,96},{1... | collective-permute-start | bytes 442376 | tf_op jit(solution)/shard_map/ppermute | solution.py:24
  156.0 9.7 %collective-permute-start.22 = (s16[144,512]{1,0:T(8,128)(2,1)S(1)}, s16[144,512]{1,0:T(8,128)(2,1)S(1)}, u32[]{:S(2)}, u32[]{:S(2)}) collective-permute-start(s16[144,512]{1,0:T(8,128)(2,1)S(1)} %get-tuple-element.43), channel_id=1, source_target_pairs={{0,16},{16,32},{32,48},{48,64},{64,80},{80,96},{96,112},{112,128},... | collective-permute-start | bytes 442376 | tf_op jit(solution)/shard_map/ppermute | solution.py:24
  165.7 26.3 %copy-start.2 = (s32[8]{0:T(128)S(1)}, s32[8]{0:T(128)}, u32[]{:S(2)}) copy-start(s32[8]{0:T(128)} %span.3) | copy-start | bytes 100
  165.7 26.3 %copy-start.3 = (s32[8]{0:T(128)S(1)}, s32[8]{0:T(128)}, u32[]{:S(2)}) copy-start(s32[8]{0:T(128)} %owner.1) | copy-start | bytes 100
  166.1 7.6 %collective-permute-start.23 = (s16[144,512]{1,0:T(8,128)(2,1)S(1)}, s16[144,512]{1,0:T(8,128)(2,1)S(1)}, u32[]{:S(2)}, u32[]{:S(2)}) collective-permute-start(s16[144,512]{1,0:T(8,128)(2,1)S(1)} %get-tuple-element.45), channel_id=1, source_target_pairs={{0,240},{16,0},{32,16},{48,32},{64,48},{80,64},{96,80},{112,96},{1... | collective-permute-start | bytes 442376 | tf_op jit(solution)/shard_map/ppermute | solution.py:24
  168.7 8.3 %collective-permute-start.24 = (s16[144,512]{1,0:T(8,128)(2,1)S(1)}, s16[144,512]{1,0:T(8,128)(2,1)S(1)}, u32[]{:S(2)}, u32[]{:S(2)}) collective-permute-start(s16[144,512]{1,0:T(8,128)(2,1)S(1)} %get-tuple-element.47), channel_id=1, source_target_pairs={{0,16},{16,32},{32,48},{48,64},{64,80},{80,96},{96,112},{112,128},... | collective-permute-start | bytes 442376 | tf_op jit(solution)/shard_map/ppermute | solution.py:24
  177.3 11.7 %collective-permute-start.25 = (s16[144,512]{1,0:T(8,128)(2,1)S(1)}, s16[144,512]{1,0:T(8,128)(2,1)S(1)}, u32[]{:S(2)}, u32[]{:S(2)}) collective-permute-start(s16[144,512]{1,0:T(8,128)(2,1)S(1)} %get-tuple-element.49), channel_id=1, source_target_pairs={{0,240},{16,0},{32,16},{48,32},{64,48},{80,64},{96,80},{112,96},{1... | collective-permute-start | bytes 442376 | tf_op jit(solution)/shard_map/ppermute | solution.py:24
  179.3 9.7 %collective-permute-start.26 = (s16[144,512]{1,0:T(8,128)(2,1)S(1)}, s16[144,512]{1,0:T(8,128)(2,1)S(1)}, u32[]{:S(2)}, u32[]{:S(2)}) collective-permute-start(s16[144,512]{1,0:T(8,128)(2,1)S(1)} %get-tuple-element.51), channel_id=1, source_target_pairs={{0,16},{16,32},{32,48},{48,64},{64,80},{80,96},{96,112},{112,128},... | collective-permute-start | bytes 442376 | tf_op jit(solution)/shard_map/ppermute | solution.py:24
  189.4 7.1 %collective-permute-start.28 = (s16[144,512]{1,0:T(8,128)(2,1)S(1)}, s16[144,512]{1,0:T(8,128)(2,1)S(1)}, u32[]{:S(2)}, u32[]{:S(2)}) collective-permute-start(s16[144,512]{1,0:T(8,128)(2,1)S(1)} %get-tuple-element.54), channel_id=1, source_target_pairs={{0,240},{16,0},{32,16},{48,32},{64,48},{80,64},{96,80},{112,96},{1... | collective-permute-start | bytes 442376 | tf_op jit(solution)/shard_map/ppermute | solution.py:24
  192.8 8.3 %collective-permute-start.27 = (s16[144,512]{1,0:T(8,128)(2,1)S(1)}, s16[144,512]{1,0:T(8,128)(2,1)S(1)}, u32[]{:S(2)}, u32[]{:S(2)}) collective-permute-start(s16[144,512]{1,0:T(8,128)(2,1)S(1)} %get-tuple-element.53), channel_id=1, source_target_pairs={{0,16},{16,32},{32,48},{48,64},{64,80},{80,96},{96,112},{112,128},... | collective-permute-start | bytes 442376 | tf_op jit(solution)/shard_map/ppermute | solution.py:24
  196.6 7.1 %collective-permute-start.29 = (s16[144,512]{1,0:T(8,128)(2,1)S(1)}, s16[144,512]{1,0:T(8,128)(2,1)S(1)}, u32[]{:S(2)}, u32[]{:S(2)}) collective-permute-start(s16[144,512]{1,0:T(8,128)(2,1)S(1)} %merge.13), channel_id=1, source_target_pairs={{0,240},{16,0},{32,16},{48,32},{64,48},{80,64},{96,80},{112,96},{1... | collective-permute-start | bytes 442376 | tf_op jit(solution)/shard_map/ppermute | solution.py:24

commit v2 on v1

--- a/solution.py
+++ b/solution.py
@@ -14,6 +14,7 @@
 META = 8
 CODE = 16
 NEVER = -1e30
+WIDE = 4096.0
 FLOOR = -2000.0
 NT = (((1,), (1,)), ((), ()))
 TN = (((0,), (0,)), ((), ()))
@@ -93,7 +94,7 @@
     seen = (u < tokens) & (me * tokens + u <= q_token)
 
     def one(j, steps):
-        q = jnp.concatenate([r[j, :rows] for r in q_refs], axis=0)
+        q = jnp.concatenate([r[j] for r in q_refs], axis=0)
         fresh = fresh_ref[j]
         live = info[1 + g * forks + j]
         s_new = lax.dot_general(fresh, q, NT, preferred_element_type=jnp.float32)
@@ -149,9 +150,9 @@
             out_refs[b][...] = o
 
 
-def parts_of(blocks_q, offsets, codes, info, cache, fresh, members, tokens):
+def parts_of(blocks_q, offsets, codes, info, cache, fresh, tokens):
     n = len(offsets)
-    forks, carried, _ = blocks_q[0].shape
+    members, forks, carried, _ = blocks_q.shape
     rows = carried - 2 * tokens
     both = 128 // rows
     cap, width = cache.shape[1:]
@@ -163,9 +164,15 @@
         grid_spec=pltpu.PrefetchScalarGridSpec(
             num_scalar_prefetch=1,
             grid=(forks // both,),
-            in_specs=[pl.BlockSpec((both, carried, HEAD_DIM), lambda g, i: (g, 0, 0))] * n
+            in_specs=[
+                pl.BlockSpec(
+                    (None, both, rows, HEAD_DIM),
+                    lambda g, i, off=off: (lax.rem(i[0] + (off + members), members), g, 0, 0),
+                )
+                for off in offsets
+            ]
             + [
-                pl.BlockSpec((both, 2 * tokens, HEAD_DIM), lambda g, i: (g, rows // (2 * tokens), 0)),
+                pl.BlockSpec((both, 2 * tokens, HEAD_DIM), lambda g, i: (g, 0, 0)),
                 pl.BlockSpec((both, cap, width), lambda g, i: (g, 0, 0)),
             ],
             out_specs=[pl.BlockSpec((h, both * rows), lambda g, i: (0, g)) for h in heights],
@@ -185,7 +192,7 @@
             bytes_accessed=2 * forks * keys * width,
         ),
         name="parts",
-    )(info, *blocks_q, fresh, cache)
+    )(info, *[blocks_q] * n, fresh, cache)
 
 
 def merge_kernel(*refs):
@@ -236,39 +243,33 @@
     )(info, span, own, right, left)
 
 
-def own_kernel(offsets, tokens, info, span, owner, *refs):
-    members = len(offsets)
-    out = refs[members]
+def own_kernel(tokens, info, span, owner, rows_ref, out):
+    members, forks = rows_ref.shape[:2]
     me = info[0]
-    forks = refs[0].shape[0]
     row = lax.rem(lax.broadcasted_iota(jnp.int32, (2 * tokens, HEAD_DIM), 0), tokens)
-    for off, ref in zip(offsets, refs):
-        first = lax.rem(me + (off + members), members) * tokens
+    for i in range(members):
         picked = jnp.zeros((2 * tokens, HEAD_DIM), jnp.float32)
         for f in range(forks):
-            mine = (owner[f] == me) & (row + first < span[f])
-            picked = jnp.where(mine, ref[f].astype(jnp.float32), picked)
-        at = pl.ds(pl.multiple_of(first, tokens), tokens)
-        out[at, :HEAD_DIM] = picked[:tokens]
-        out[at, HEAD_DIM:] = picked[tokens:]
+            mine = (owner[f] == me) & (row + i * tokens < span[f])
+            picked = jnp.where(mine, rows_ref[i, f].astype(jnp.float32), picked)
+        out[i * tokens : (i + 1) * tokens, :HEAD_DIM] = picked[:tokens]
+        out[i * tokens : (i + 1) * tokens, HEAD_DIM:] = picked[tokens:]
 
 
 def own_kv(info, span, owner, q, tokens, width):
-    offsets = tuple(q)
-    forks, carried, _ = q[0].shape
+    members, forks, carried, _ = q.shape
     smem = pl.BlockSpec(memory_space=pltpu.SMEM)
     at = carried // (2 * tokens) - 1
-    tokens_all = len(offsets) * tokens
     return pl.pallas_call(
-        functools.partial(own_kernel, offsets, tokens),
+        functools.partial(own_kernel, tokens),
         grid=(1,),
         in_specs=[smem] * 3
-        + [pl.BlockSpec((forks, 2 * tokens, HEAD_DIM), lambda g: (0, at, 0))] * len(offsets),
-        out_specs=pl.BlockSpec((tokens_all, width), lambda g: (0, 0)),
-        out_shape=jax.ShapeDtypeStruct((tokens_all, width), jnp.float32),
+        + [pl.BlockSpec((members, forks, 2 * tokens, HEAD_DIM), lambda g: (0, 0, at, 0))],
+        out_specs=pl.BlockSpec((members * tokens, width), lambda g: (0, 0)),
+        out_shape=jax.ShapeDtypeStruct((members * tokens, width), jnp.float32),
         compiler_params=pltpu.CompilerParams(vmem_limit_bytes=8 * 2**20),
         name="own_kv",
-    )(info, span, owner, *[q[o] for o in offsets]).astype(jnp.bfloat16)
+    )(info, span, owner, q).astype(jnp.bfloat16)
 
 
 def body(queries, tool_key_value, cache, placed, blocks, span_len, owner):
@@ -281,30 +282,25 @@
     live = placed[:, 0] * blocks[:, 0] * BLOCK
     info = jnp.concatenate([me.astype(jnp.int32)[None], live])
     own_q = queries.reshape(forks, tokens, heads, HEAD_DIM).transpose(0, 2, 1, 3)
-    own_kv_rows = tool_key_value.reshape(forks, tokens, 2, HEAD_DIM).transpose(0, 2, 1, 3)
-    own_q = jnp.concatenate(
-        [own_q.reshape(forks, rows, HEAD_DIM), own_kv_rows.reshape(forks, 2 * tokens, HEAD_DIM)], axis=1
-    )
-
-    q = {0: own_q}
-    for k in range(1, half + 1):
-        q[-k] = passed_along(q[1 - k], 1)
-        if k < half:
-            q[k] = passed_along(q[k - 1], -1)
+    fresh = tool_key_value.reshape(forks, tokens, 2, HEAD_DIM).transpose(0, 2, 1, 3)
+    own_q, fresh = own_q.reshape(forks, rows, HEAD_DIM), fresh.reshape(forks, 2 * tokens, HEAD_DIM)
+    sent = jnp.concatenate([own_q, fresh], axis=1).astype(jnp.float32) * WIDE
+    q = lax.all_gather(sent.astype(jnp.float16), "inst", axis=0)
+    q = (q.astype(jnp.float32) * (1.0 / WIDE)).astype(jnp.bfloat16)
+
     part = {}
     for offsets in CALLS(half):
         codes = tuple(o in (-half, half - 1) for o in offsets)
-        got = parts_of([q[o] for o in offsets], offsets, codes, info, cache, own_q, members, tokens)
+        got = parts_of(q, offsets, codes, info, cache, fresh, tokens)
         part.update(zip(offsets, got))
 
     left, right = part[-half], part[half - 1]
     for k in range(half - 1, 0, -1):
         left = passed_along(left, -1)
         right = passed_along(right, 1)
+        (left,) = merge(left, part[-k])
         if k > 1:
-            left, right = merge(left, part[-k], right, part[k - 1])
-        else:
-            (left,) = merge(left, part[-1])
+            (right,) = merge(right, part[k - 1])
     left = passed_along(left, -1)
     owned = own_kv(info, span_len, owner, q, tokens, width).reshape(1, 1, members * tokens, width)
     attended = finish(info, span_len, part[0], right, left, tokens, rows)
@@ -313,11 +309,10 @@
 
 
 def CALLS(half):
-    order = [0]
-    for k in range(1, half + 1):
-        order += [-k, k] if k < half else [-k]
-    calls = [tuple(order[i : i + 4]) for i in range(0, len(order) - 4, 4)]
-    return calls + [tuple(order[-4:-1]), tuple(order[-1:])]
+    order = []
+    for k in range(half, 0, -1):
+        order += [-k, k - 1]
+    return [tuple(order[:2])] + [tuple(order[i : i + 4]) for i in range(2, len(order), 4)]
 
 
 def solution(mesh):

time: 207 us -> 182 us (0.88)
  starting transfers between devices: 139 us -> 50.7 us
  blocking collectives: 0 us -> 87.7 us
  waiting for transfers between devices: 28.8 us -> 7.76 us
    ppermute x30 -> x15, starting transfers between devices: 139 us -> 50.7 us  [passed_along(): return lax.ppermute(x, 'inst', [(i, (i + by) % size) for i in range(size)])]
    all_gather x0 -> x1, blocking collectives: none -> 87.7 us  [body(): q = lax.all_gather(sent.astype(jnp.float16), 'inst', axis=0)]
    ppermute x30 -> x15, waiting for transfers between devices: 28.8 us -> 7.76 us  [passed_along(): return lax.ppermute(x, 'inst', [(i, (i + by) % size) for i in range(size)])]
  transfers between devices with their start and end apart: 30 -> 15, of which waited for: 15 -> 5; matrix products, arithmetic and copies ran while one was open for 1% -> 0% of each run, Pallas kernels for 14% -> 13%
where the time goes in v2:
time: 182 us; the launch traced here: 181 us
  blocking collectives  87.7 us (48%)
  starting transfers between devices  50.7 us (28%)
  Pallas kernels  30.3 us (17%)
  waiting for transfers between devices  7.76 us (4%)
  other arithmetic  2.41 us (1%)
    all_gather x1, blocking collectives, body(): q = lax.all_gather(sent.astype(jnp.float16), 'inst', axis=0)  87.7 us
    ppermute x15, starting transfers between devices, passed_along(): return lax.ppermute(x, 'inst', [(i, (i + by) % size) for i in range(size)])  50.7 us
    pallas_call x5, Pallas kernels, parts_of(): pl.pallas_call(functools.partial(part_kernel, offsets, codes, members, to...  26 us
    ppermute x15, waiting for transfers between devices, passed_along(): return lax.ppermute(x, 'inst', [(i, (i + by) % size) for i in range(size)])  7.76 us
  transfers between devices with their start and end apart: 15, of which 5 were waited for; matrix products, arithmetic and copies ran while one was open for 0% of the time, Pallas kernels for 13%

profile of v2, /device:TPU:80, one launch (start us, length us, event | category | flops | bytes accessed | tf_op | source)
XLA Modules:
  0.0 181.0 jit_solution(15236658394522134575)
XLA Ops:
  0.6 1.0 multiply_convert_fusion.1
  1.6 87.7 %all-gather.1 = f16[16,8,80,128]{3,2,1,0:T(8,128)(2,1)S(1)} all-gather(f16[1,8,80,128]{3,2,1,0:T(8,128)(2,1)S(1)} %multiply_convert_fusion.1), channel_id=1, replica_groups=mesh['groups'=2,'inst'=16,'tp'=8,'rep'=2] {'inst'}, dimensions={0}, use_global_device_ids=true | all-gather | bytes 2785280 | tf_op jit(solution)/shard_map/all_gather | solution.py:288
  89.3 0.0 copy-start.4
  89.3 0.7 multiply_convert_fusion.refs_0_.refs_1_.refs_2_.refs_3_.rows_ref
  90.1 0.0 copy-done.4
  90.1 0.0 copy-done.5
  90.1 0.1 pad_add_fusion.info
  90.2 1.1 copy-done
  91.3 0.0 copy-done.1
  91.3 4.7 %parts.6 = (s16[144,512]{1,0:T(8,128)(2,1)S(1)}, s16[144,512]{1,0:T(8,128)(2,1)S(1)}) custom-call(s32[9]{0:T(128)S(1)} %pad_add_fusion.info, bf16[16,8,80,128]{3,2,1,0:T(8,128)(2,1)S(1)} %multiply_convert_fusion.refs_0_.refs_1_.refs_2_.refs_3_.rows_ref, bf16[16,8,80,128]{3,2,1,0:T(8,128)(2,1)S(1)} %multiply_convert_fusion.refs_0_.refs_1_.refs_2_.refs_3_.rows_ref, ...), custom_call_target="tpu_custom_call" | custom-call | flops 406847488 | bytes 3178496 | tf_op jit(solution)/shard_map/parts/pallas_call | solution.py:162
  96.0 2.0 %collective-permute-start.7 = (s16[144,512]{1,0:T(8,128)(2,1)S(1)}, s16[144,512]{1,0:T(8,128)(2,1)S(1)}, u32[]{:S(2)}, u32[]{:S(2)}) collective-permute-start(s16[144,512]{1,0:T(8,128)(2,1)S(1)} %get-tuple-element.26), channel_id=1, source_target_pairs={{0,240},{16,0},{32,16},{48,32},{64,48},{80,64},{96,80},{112,96},{1... | collective-permute-start | bytes 442376 | tf_op jit(solution)/shard_map/ppermute | solution.py:25
  97.9 4.0 %collective-permute-start = (s16[144,512]{1,0:T(8,128)(2,1)S(1)}, s16[144,512]{1,0:T(8,128)(2,1)S(1)}, u32[]{:S(2)}, u32[]{:S(2)}) collective-permute-start(s16[144,512]{1,0:T(8,128)(2,1)S(1)} %get-tuple-element.19), channel_id=1, source_target_pairs={{0,16},{16,32},{32,48},{48,64},{64,80},{80,96},{96,112},{112,128},... | collective-permute-start | bytes 442376 | tf_op jit(solution)/shard_map/ppermute | solution.py:25
  101.9 5.6 %parts.7 = (f32[136,512]{1,0:T(8,128)S(1)}, f32[136,512]{1,0:T(8,128)S(1)}, f32[136,512]{1,0:T(8,128)S(1)}, f32[136,512]{1,0:T(8,128)S(1)}) custom-call(s32[9]{0:T(128)S(1)} %pad_add_fusion.info, bf16[16,8,80,128]{3,2,1,0:T(8,128)(2,1)S(1)} %multiply_convert_fusion.refs_0_.refs_1_.refs_2_.refs_3_.rows_ref, ...), custom_call_target="tpu_custom_call" | custom-call | flops 813694976 | bytes 3178496 | tf_op jit(solution)/shard_map/parts/pallas_call | solution.py:162
  107.5 0.0 collective-permute-done.7.refs_0_
  107.5 0.2 merge.19
  107.7 3.4 %collective-permute-start.8 = (s16[144,512]{1,0:T(8,128)(2,1)S(1)}, s16[144,512]{1,0:T(8,128)(2,1)S(1)}, u32[]{:S(2)}, u32[]{:S(2)}) collective-permute-start(s16[144,512]{1,0:T(8,128)(2,1)S(1)} %merge.19), channel_id=1, source_target_pairs={{0,240},{16,0},{32,16},{48,32},{64,48},{80,64},{96,80},{112,96},{1... | collective-permute-start | bytes 442376 | tf_op jit(solution)/shard_map/ppermute | solution.py:25
  111.1 0.0 collective-permute-done.refs_0_
  111.1 0.2 merge.13
  111.3 2.5 %collective-permute-start.1 = (s16[144,512]{1,0:T(8,128)(2,1)S(1)}, s16[144,512]{1,0:T(8,128)(2,1)S(1)}, u32[]{:S(2)}, u32[]{:S(2)}) collective-permute-start(s16[144,512]{1,0:T(8,128)(2,1)S(1)} %merge.13), channel_id=1, source_target_pairs={{0,16},{16,32},{32,48},{48,64},{64,80},{80,96},{96,112},{112,128},... | collective-permute-start | bytes 442376 | tf_op jit(solution)/shard_map/ppermute | solution.py:25
  113.8 2.5 %collective-permute-done.8.refs_0_ = s16[144,512]{1,0:T(8,128)(2,1)S(1)} collective-permute-done((s16[144,512]{1,0:T(8,128)(2,1)S(1)}, s16[144,512]{1,0:T(8,128)(2,1)S(1)}, u32[]{:S(2)}, u32[]{:S(2)}) %collective-permute-start.8) | collective-permute-done | bytes 147488 | tf_op jit(solution)/shard_map/ppermute | solution.py:25
  116.3 0.2 merge.20
  116.5 3.1 %collective-permute-start.9 = (s16[144,512]{1,0:T(8,128)(2,1)S(1)}, s16[144,512]{1,0:T(8,128)(2,1)S(1)}, u32[]{:S(2)}, u32[]{:S(2)}) collective-permute-start(s16[144,512]{1,0:T(8,128)(2,1)S(1)} %merge.20), channel_id=1, source_target_pairs={{0,240},{16,0},{32,16},{48,32},{64,48},{80,64},{96,80},{112,96},{1... | collective-permute-start | bytes 442376 | tf_op jit(solution)/shard_map/ppermute | solution.py:25
  119.6 5.6 %parts.8 = (f32[136,512]{1,0:T(8,128)S(1)}, f32[136,512]{1,0:T(8,128)S(1)}, f32[136,512]{1,0:T(8,128)S(1)}, f32[136,512]{1,0:T(8,128)S(1)}) custom-call(s32[9]{0:T(128)S(1)} %pad_add_fusion.info, bf16[16,8,80,128]{3,2,1,0:T(8,128)(2,1)S(1)} %multiply_convert_fusion.refs_0_.refs_1_.refs_2_.refs_3_.rows_ref, ...), custom_call_target="tpu_custom_call" | custom-call | flops 813694976 | bytes 3178496 | tf_op jit(solution)/shard_map/parts/pallas_call | solution.py:162
  125.1 0.0 collective-permute-done.1.refs_0_
  125.2 0.2 merge.14
  125.3 3.1 %collective-permute-start.2 = (s16[144,512]{1,0:T(8,128)(2,1)S(1)}, s16[144,512]{1,0:T(8,128)(2,1)S(1)}, u32[]{:S(2)}, u32[]{:S(2)}) collective-permute-start(s16[144,512]{1,0:T(8,128)(2,1)S(1)} %merge.14), channel_id=1, source_target_pairs={{0,16},{16,32},{32,48},{48,64},{64,80},{80,96},{96,112},{112,128},... | collective-permute-start | bytes 442376 | tf_op jit(solution)/shard_map/ppermute | solution.py:25
  128.4 0.0 collective-permute-done.9.refs_0_
  128.4 0.2 merge.21
  128.6 4.1 %collective-permute-start.10 = (s16[144,512]{1,0:T(8,128)(2,1)S(1)}, s16[144,512]{1,0:T(8,128)(2,1)S(1)}, u32[]{:S(2)}, u32[]{:S(2)}) collective-permute-start(s16[144,512]{1,0:T(8,128)(2,1)S(1)} %merge.21), channel_id=1, source_target_pairs={{0,240},{16,0},{32,16},{48,32},{64,48},{80,64},{96,80},{112,96},{1... | collective-permute-start | bytes 442376 | tf_op jit(solution)/shard_map/ppermute | solution.py:25
  132.6 2.2 %collective-permute-done.2.refs_0_ = s16[144,512]{1,0:T(8,128)(2,1)S(1)} collective-permute-done((s16[144,512]{1,0:T(8,128)(2,1)S(1)}, s16[144,512]{1,0:T(8,128)(2,1)S(1)}, u32[]{:S(2)}, u32[]{:S(2)}) %collective-permute-start.2) | collective-permute-done | bytes 147488 | tf_op jit(solution)/shard_map/ppermute | solution.py:25
  134.9 0.2 merge.15
  135.0 2.0 %collective-permute-start.3 = (s16[144,512]{1,0:T(8,128)(2,1)S(1)}, s16[144,512]{1,0:T(8,128)(2,1)S(1)}, u32[]{:S(2)}, u32[]{:S(2)}) collective-permute-start(s16[144,512]{1,0:T(8,128)(2,1)S(1)} %merge.15), channel_id=1, source_target_pairs={{0,16},{16,32},{32,48},{48,64},{64,80},{80,96},{96,112},{112,128},... | collective-permute-start | bytes 442376 | tf_op jit(solution)/shard_map/ppermute | solution.py:25
  137.0 0.0 collective-permute-done.10.refs_0_
  137.0 0.2 merge.22
  137.2 0.0 copy-start.2
  137.2 0.0 copy-start.3
  137.2 5.4 %collective-permute-start.11 = (s16[144,512]{1,0:T(8,128)(2,1)S(1)}, s16[144,512]{1,0:T(8,128)(2,1)S(1)}, u32[]{:S(2)}, u32[]{:S(2)}) collective-permute-start(s16[144,512]{1,0:T(8,128)(2,1)S(1)} %merge.22), channel_id=1, source_target_pairs={{0,240},{16,0},{32,16},{48,32},{64,48},{80,64},{96,80},{112,96},{1... | collective-permute-start | bytes 442376 | tf_op jit(solution)/shard_map/ppermute | solution.py:25
  142.6 5.6 %parts.9 = (f32[136,512]{1,0:T(8,128)S(1)}, f32[136,512]{1,0:T(8,128)S(1)}, f32[136,512]{1,0:T(8,128)S(1)}, f32[136,512]{1,0:T(8,128)S(1)}) custom-call(s32[9]{0:T(128)S(1)} %pad_add_fusion.info, bf16[16,8,80,128]{3,2,1,0:T(8,128)(2,1)S(1)} %multiply_convert_fusion.refs_0_.refs_1_.refs_2_.refs_3_.rows_ref, ...), custom_call_target="tpu_custom_call" | custom-call | flops 813694976 | bytes 3178496 | tf_op jit(solution)/shard_map/parts/pallas_call | solution.py:162
  148.2 0.0 collective-permute-done.3.refs_0_
  148.2 0.2 merge.16
  148.4 2.0 %collective-permute-start.4 = (s16[144,512]{1,0:T(8,128)(2,1)S(1)}, s16[144,512]{1,0:T(8,128)(2,1)S(1)}, u32[]{:S(2)}, u32[]{:S(2)}) collective-permute-start(s16[144,512]{1,0:T(8,128)(2,1)S(1)} %merge.16), channel_id=1, source_target_pairs={{0,16},{16,32},{32,48},{48,64},{64,80},{80,96},{96,112},{112,128},... | collective-permute-start | bytes 442376 | tf_op jit(solution)/shard_map/ppermute | solution.py:25
  150.4 0.0 collective-permute-done.11.refs_0_
  150.4 0.2 merge.23
  150.6 5.2 %collective-permute-start.12 = (s16[144,512]{1,0:T(8,128)(2,1)S(1)}, s16[144,512]{1,0:T(8,128)(2,1)S(1)}, u32[]{:S(2)}, u32[]{:S(2)}) collective-permute-start(s16[144,512]{1,0:T(8,128)(2,1)S(1)} %merge.23), channel_id=1, source_target_pairs={{0,240},{16,0},{32,16},{48,32},{64,48},{80,64},{96,80},{112,96},{1... | collective-permute-start | bytes 442376 | tf_op jit(solution)/shard_map/ppermute | solution.py:25
  155.7 1.0 collective-permute-done.4.refs_0_
  156.7 0.2 merge.17
  156.9 2.0 %collective-permute-start.5 = (s16[144,512]{1,0:T(8,128)(2,1)S(1)}, s16[144,512]{1,0:T(8,128)(2,1)S(1)}, u32[]{:S(2)}, u32[]{:S(2)}) collective-permute-start(s16[144,512]{1,0:T(8,128)(2,1)S(1)} %merge.17), channel_id=1, source_target_pairs={{0,16},{16,32},{32,48},{48,64},{64,80},{80,96},{96,112},{112,128},... | collective-permute-start | bytes 442376 | tf_op jit(solution)/shard_map/ppermute | solution.py:25
  158.8 0.0 collective-permute-done.12.refs_0_
  158.8 0.2 merge.24
  159.0 5.2 %collective-permute-start.13 = (s16[144,512]{1,0:T(8,128)(2,1)S(1)}, s16[144,512]{1,0:T(8,128)(2,1)S(1)}, u32[]{:S(2)}, u32[]{:S(2)}) collective-permute-start(s16[144,512]{1,0:T(8,128)(2,1)S(1)} %merge.24), channel_id=1, source_target_pairs={{0,240},{16,0},{32,16},{48,32},{64,48},{80,64},{96,80},{112,96},{1... | collective-permute-start | bytes 442376 | tf_op jit(solution)/shard_map/ppermute | solution.py:25
  164.2 0.0 copy-done.2
  164.2 0.0 copy-done.3
  164.2 0.7 own_kv.1
  164.9 4.5 %parts.5 = (f32[136,512]{1,0:T(8,128)S(1)}, f32[136,512]{1,0:T(8,128)S(1)}) custom-call(s32[9]{0:T(128)S(1)} %pad_add_fusion.info, bf16[16,8,80,128]{3,2,1,0:T(8,128)(2,1)S(1)} %multiply_convert_fusion.refs_0_.refs_1_.refs_2_.refs_3_.rows_ref, bf16[16,8,80,128]{3,2,1,0:T(8,128)(2,1)S(1)} %multiply_convert_fusion.refs_0_.refs_1_.refs_2_.refs_3_.rows_ref, ...), custom_call_target="tpu_custom_call" | custom-call | flops 406847488 | bytes 3178496 | tf_op jit(solution)/shard_map/parts/pallas_call | solution.py:162
  169.4 0.0 collective-permute-done.5.refs_0_
  169.5 0.2 merge.18
  169.6 2.0 %collective-permute-start.6 = (s16[144,512]{1,0:T(8,128)(2,1)S(1)}, s16[144,512]{1,0:T(8,128)(2,1)S(1)}, u32[]{:S(2)}, u32[]{:S(2)}) collective-permute-start(s16[144,512]{1,0:T(8,128)(2,1)S(1)} %merge.18), channel_id=1, source_target_pairs={{0,16},{16,32},{32,48},{48,64},{64,80},{80,96},{96,112},{112,128},... | collective-permute-start | bytes 442376 | tf_op jit(solution)/shard_map/ppermute | solution.py:25
  171.6 0.0 collective-permute-done.13.refs_0_
  171.6 0.2 merge.25
  171.8 5.2 %collective-permute-start.14 = (s16[144,512]{1,0:T(8,128)(2,1)S(1)}, s16[144,512]{1,0:T(8,128)(2,1)S(1)}, u32[]{:S(2)}, u32[]{:S(2)}) collective-permute-start(s16[144,512]{1,0:T(8,128)(2,1)S(1)} %merge.25), channel_id=1, source_target_pairs={{0,240},{16,0},{32,16},{48,32},{64,48},{80,64},{96,80},{112,96},{1... | collective-permute-start | bytes 442376 | tf_op jit(solution)/shard_map/ppermute | solution.py:25
  176.9 0.6 convert_bitcast_fusion
  177.6 0.3 collective-permute-done.6.right
  177.9 1.7 collective-permute-done.14.left
  179.6 1.4 finish.1
  (4 shorter events, 0.0 us)
Async XLA Ops:
  89.3 0.7 copy-start.4
  89.3 0.7 copy-start.5
  89.3 1.9 %copy-start = (bf16[8,768,256]{2,1,0:T(8,128)(2,1)S(1)}, bf16[8,768,256]{2,1,0:T(8,128)(2,1)}, u32[]{:S(2)}) copy-start(bf16[8,768,256]{2,1,0:T(8,128)(2,1)} %refs_5_.5) | copy-start | bytes 9437188
  89.3 1.9 %copy-start.1 = (bf16[8,8,256]{2,1,0:T(8,128)(2,1)S(1)}, bf16[8,8,256]{2,1,0:T(8,128)(2,1)}, u32[]{:S(2)}) copy-start(bf16[8,8,256]{2,1,0:T(8,128)(2,1)} %param.8) | copy-start | bytes 98308
  96.0 11.5 %collective-permute-start.7 = (s16[144,512]{1,0:T(8,128)(2,1)S(1)}, s16[144,512]{1,0:T(8,128)(2,1)S(1)}, u32[]{:S(2)}, u32[]{:S(2)}) collective-permute-start(s16[144,512]{1,0:T(8,128)(2,1)S(1)} %get-tuple-element.26), channel_id=1, source_target_pairs={{0,240},{16,0},{32,16},{48,32},{64,48},{80,64},{96,80},{112,96},{1... | collective-permute-start | bytes 442376 | tf_op jit(solution)/shard_map/ppermute | solution.py:25
  97.9 13.2 %collective-permute-start = (s16[144,512]{1,0:T(8,128)(2,1)S(1)}, s16[144,512]{1,0:T(8,128)(2,1)S(1)}, u32[]{:S(2)}, u32[]{:S(2)}) collective-permute-start(s16[144,512]{1,0:T(8,128)(2,1)S(1)} %get-tuple-element.19), channel_id=1, source_target_pairs={{0,16},{16,32},{32,48},{48,64},{64,80},{80,96},{96,112},{112,128},... | collective-permute-start | bytes 442376 | tf_op jit(solution)/shard_map/ppermute | solution.py:25
  107.7 8.6 %collective-permute-start.8 = (s16[144,512]{1,0:T(8,128)(2,1)S(1)}, s16[144,512]{1,0:T(8,128)(2,1)S(1)}, u32[]{:S(2)}, u32[]{:S(2)}) collective-permute-start(s16[144,512]{1,0:T(8,128)(2,1)S(1)} %merge.19), channel_id=1, source_target_pairs={{0,240},{16,0},{32,16},{48,32},{64,48},{80,64},{96,80},{112,96},{1... | collective-permute-start | bytes 442376 | tf_op jit(solution)/shard_map/ppermute | solution.py:25
  111.3 13.9 %collective-permute-start.1 = (s16[144,512]{1,0:T(8,128)(2,1)S(1)}, s16[144,512]{1,0:T(8,128)(2,1)S(1)}, u32[]{:S(2)}, u32[]{:S(2)}) collective-permute-start(s16[144,512]{1,0:T(8,128)(2,1)S(1)} %merge.13), channel_id=1, source_target_pairs={{0,16},{16,32},{32,48},{48,64},{64,80},{80,96},{96,112},{112,128},... | collective-permute-start | bytes 442376 | tf_op jit(solution)/shard_map/ppermute | solution.py:25
  116.5 11.9 %collective-permute-start.9 = (s16[144,512]{1,0:T(8,128)(2,1)S(1)}, s16[144,512]{1,0:T(8,128)(2,1)S(1)}, u32[]{:S(2)}, u32[]{:S(2)}) collective-permute-start(s16[144,512]{1,0:T(8,128)(2,1)S(1)} %merge.20), channel_id=1, source_target_pairs={{0,240},{16,0},{32,16},{48,32},{64,48},{80,64},{96,80},{112,96},{1... | collective-permute-start | bytes 442376 | tf_op jit(solution)/shard_map/ppermute | solution.py:25
  125.3 9.5 %collective-permute-start.2 = (s16[144,512]{1,0:T(8,128)(2,1)S(1)}, s16[144,512]{1,0:T(8,128)(2,1)S(1)}, u32[]{:S(2)}, u32[]{:S(2)}) collective-permute-start(s16[144,512]{1,0:T(8,128)(2,1)S(1)} %merge.14), channel_id=1, source_target_pairs={{0,16},{16,32},{32,48},{48,64},{64,80},{80,96},{96,112},{112,128},... | collective-permute-start | bytes 442376 | tf_op jit(solution)/shard_map/ppermute | solution.py:25
  128.6 8.4 %collective-permute-start.10 = (s16[144,512]{1,0:T(8,128)(2,1)S(1)}, s16[144,512]{1,0:T(8,128)(2,1)S(1)}, u32[]{:S(2)}, u32[]{:S(2)}) collective-permute-start(s16[144,512]{1,0:T(8,128)(2,1)S(1)} %merge.21), channel_id=1, source_target_pairs={{0,240},{16,0},{32,16},{48,32},{64,48},{80,64},{96,80},{112,96},{1... | collective-permute-start | bytes 442376 | tf_op jit(solution)/shard_map/ppermute | solution.py:25
  135.0 13.2 %collective-permute-start.3 = (s16[144,512]{1,0:T(8,128)(2,1)S(1)}, s16[144,512]{1,0:T(8,128)(2,1)S(1)}, u32[]{:S(2)}, u32[]{:S(2)}) collective-permute-start(s16[144,512]{1,0:T(8,128)(2,1)S(1)} %merge.15), channel_id=1, source_target_pairs={{0,16},{16,32},{32,48},{48,64},{64,80},{80,96},{96,112},{112,128},... | collective-permute-start | bytes 442376 | tf_op jit(solution)/shard_map/ppermute | solution.py:25
  137.2 27.0 %copy-start.2 = (s32[8]{0:T(128)S(1)}, s32[8]{0:T(128)}, u32[]{:S(2)}) copy-start(s32[8]{0:T(128)} %span.3) | copy-start | bytes 100
  137.2 27.0 %copy-start.3 = (s32[8]{0:T(128)S(1)}, s32[8]{0:T(128)}, u32[]{:S(2)}) copy-start(s32[8]{0:T(128)} %owner.1) | copy-start | bytes 100
  137.2 13.2 %collective-permute-start.11 = (s16[144,512]{1,0:T(8,128)(2,1)S(1)}, s16[144,512]{1,0:T(8,128)(2,1)S(1)}, u32[]{:S(2)}, u32[]{:S(2)}) collective-permute-start(s16[144,512]{1,0:T(8,128)(2,1)S(1)} %merge.22), channel_id=1, source_target_pairs={{0,240},{16,0},{32,16},{48,32},{64,48},{80,64},{96,80},{112,96},{1... | collective-permute-start | bytes 442376 | tf_op jit(solution)/shard_map/ppermute | solution.py:25
  148.4 8.3 %collective-permute-start.4 = (s16[144,512]{1,0:T(8,128)(2,1)S(1)}, s16[144,512]{1,0:T(8,128)(2,1)S(1)}, u32[]{:S(2)}, u32[]{:S(2)}) collective-permute-start(s16[144,512]{1,0:T(8,128)(2,1)S(1)} %merge.16), channel_id=1, source_target_pairs={{0,16},{16,32},{32,48},{48,64},{64,80},{80,96},{96,112},{112,128},... | collective-permute-start | bytes 442376 | tf_op jit(solution)/shard_map/ppermute | solution.py:25
  150.6 8.3 %collective-permute-start.12 = (s16[144,512]{1,0:T(8,128)(2,1)S(1)}, s16[144,512]{1,0:T(8,128)(2,1)S(1)}, u32[]{:S(2)}, u32[]{:S(2)}) collective-permute-start(s16[144,512]{1,0:T(8,128)(2,1)S(1)} %merge.23), channel_id=1, source_target_pairs={{0,240},{16,0},{32,16},{48,32},{64,48},{80,64},{96,80},{112,96},{1... | collective-permute-start | bytes 442376 | tf_op jit(solution)/shard_map/ppermute | solution.py:25
  156.9 12.6 %collective-permute-start.5 = (s16[144,512]{1,0:T(8,128)(2,1)S(1)}, s16[144,512]{1,0:T(8,128)(2,1)S(1)}, u32[]{:S(2)}, u32[]{:S(2)}) collective-permute-start(s16[144,512]{1,0:T(8,128)(2,1)S(1)} %merge.17), channel_id=1, source_target_pairs={{0,16},{16,32},{32,48},{48,64},{64,80},{80,96},{96,112},{112,128},... | collective-permute-start | bytes 442376 | tf_op jit(solution)/shard_map/ppermute | solution.py:25
  159.0 12.6 %collective-permute-start.13 = (s16[144,512]{1,0:T(8,128)(2,1)S(1)}, s16[144,512]{1,0:T(8,128)(2,1)S(1)}, u32[]{:S(2)}, u32[]{:S(2)}) collective-permute-start(s16[144,512]{1,0:T(8,128)(2,1)S(1)} %merge.24), channel_id=1, source_target_pairs={{0,240},{16,0},{32,16},{48,32},{64,48},{80,64},{96,80},{112,96},{1... | collective-permute-start | bytes 442376 | tf_op jit(solution)/shard_map/ppermute | solution.py:25
  169.6 8.3 %collective-permute-start.6 = (s16[144,512]{1,0:T(8,128)(2,1)S(1)}, s16[144,512]{1,0:T(8,128)(2,1)S(1)}, u32[]{:S(2)}, u32[]{:S(2)}) collective-permute-start(s16[144,512]{1,0:T(8,128)(2,1)S(1)} %merge.18), channel_id=1, source_target_pairs={{0,16},{16,32},{32,48},{48,64},{64,80},{80,96},{96,112},{112,128},... | collective-permute-start | bytes 442376 | tf_op jit(solution)/shard_map/ppermute | solution.py:25
  171.8 7.8 %collective-permute-start.14 = (s16[144,512]{1,0:T(8,128)(2,1)S(1)}, s16[144,512]{1,0:T(8,128)(2,1)S(1)}, u32[]{:S(2)}, u32[]{:S(2)}) collective-permute-start(s16[144,512]{1,0:T(8,128)(2,1)S(1)} %merge.25), channel_id=1, source_target_pairs={{0,240},{16,0},{32,16},{48,32},{64,48},{80,64},{96,80},{112,96},{1... | collective-permute-start | bytes 442376 | tf_op jit(solution)/shard_map/ppermute | solution.py:25

commit v3 on v2

v3 whole, which is shorter than its diff:
```python
import functools
import math

import jax
import jax.numpy as jnp
from jax import lax
from jax.experimental import pallas as pl
from jax.experimental.pallas import tpu as pltpu
from jax.sharding import PartitionSpec as P

HEAD_DIM = 128
BLOCK = 128
STEP = 256
META = 8
CODE = 8
NEVER = -1e30
WIDE = 4096.0
FLOOR = -2000.0
NT = (((1,), (1,)), ((), ()))
TN = (((0,), (0,)), ((), ()))


def passed_along(x, by):
    size = lax.axis_size("inst")
    return lax.ppermute(x, "inst", [(i, (i + by) % size) for i in range(size)])


def meta_rows(rows, one, two, three):
    row = lax.broadcasted_iota(jnp.int32, (rows, one.shape[1]), 0)
    return jnp.where(row == 0, one, jnp.where(row == 1, two, three))


def whole(x):
    return jnp.floor(x + 0.5)


def coded(level, mean, out, sl):
    power = jnp.ceil(jnp.log2(jnp.maximum(jnp.max(jnp.abs(mean), axis=0, keepdims=True), 1e-30)))
    steps = whole(mean * jnp.exp2(15.0 - power))
    out[:HEAD_DIM, sl] = jnp.clip(steps, -32767.0, 32767.0).astype(jnp.int32).astype(jnp.int16)
    eighths = whole(level * 8.0)
    rest = whole((level - eighths * 0.125) * 2.0**18)
    out[HEAD_DIM:, sl] = meta_rows(CODE, eighths, rest, power).astype(jnp.int32).astype(jnp.int16)


def code_part(top, total, numer, out, sl):
    held = jnp.maximum(total, 1e-30)
    coded(jnp.maximum(top + jnp.log2(held), FLOOR), numer * (1.0 / held), out, sl)


def decoded(msg, sl):
    x = msg[:, sl].astype(jnp.int32).astype(jnp.float32)
    level = x[HEAD_DIM : HEAD_DIM + 1] * 0.125 + x[HEAD_DIM + 1 : HEAD_DIM + 2] * 2.0**-18
    return level, x[:HEAD_DIM] * jnp.exp2(x[HEAD_DIM + 2 : HEAD_DIM + 3] - 15.0)


def joined(parts):
    top = functools.reduce(jnp.maximum, [p[0] for p in parts])
    total, numer = 0.0, 0.0
    for t, l, n in parts:
        by = jnp.exp2(t - top)
        total = total + by * l
        numer = numer + by * n
    return top, total, numer


def held_part(ref, sl):
    return ref[HEAD_DIM : HEAD_DIM + 1, sl], ref[HEAD_DIM + 1 : HEAD_DIM + 2, sl], ref[:HEAD_DIM, sl]


def sent_part(msg, sl):
    level, mean = decoded(msg, sl)
    return level, 1.0, mean


def part_kernel(offset, code, tokens, info, q_ref, fresh_ref, kv_ref, *rest):
    out, s_ref = rest[-2:]
    members, forks, carried, _ = q_ref.shape
    rows = carried - 2 * tokens
    both = 128 // rows
    cap = kv_ref.shape[1]
    me = info[0]
    unit = math.log2(math.e) / math.sqrt(HEAD_DIM)

    lane = lax.broadcasted_iota(jnp.int32, (1, 128), 1)
    place = lane // rows
    block = lax.rem(me + (offset + members), members)
    u = lax.broadcasted_iota(jnp.int32, (2 * tokens, 128), 0)
    seen = (u < tokens) & (me * tokens + u <= block * tokens + lax.rem(lane, tokens))
    empty = jnp.zeros((rows, HEAD_DIM), jnp.bfloat16)

    def several(g, steps):
        fork = [g * both + j for j in range(both)]
        live = jnp.full((1, 128), info[1 + fork[0]], jnp.int32)
        for j in range(1, both):
            live = jnp.where(place == j, info[1 + fork[j]], live)
        q = jnp.concatenate(
            [
                jnp.concatenate([q_ref[block, f, :rows] if k == j else empty for k in range(both)], axis=1)
                for j, f in enumerate(fork)
            ],
            axis=0,
        )
        fresh = jnp.concatenate([fresh_ref[f] for f in fork], axis=1)
        s = lax.dot_general(fresh, q, NT, preferred_element_type=jnp.float32)
        new = jnp.where(seen, s, -jnp.inf)
        top = jnp.max(new, axis=0, keepdims=True)
        for c in range(steps):
            at = c * STEP
            keys = jnp.concatenate([kv_ref[f, at : at + STEP, :HEAD_DIM] for f in fork], axis=1)
            s = lax.dot_general(keys, q, NT, preferred_element_type=jnp.float32)
            for lo in range(0, STEP, BLOCK):
                part = jnp.where(at + lo < live, s[lo : lo + BLOCK], -jnp.inf)
                s_ref[at + lo : at + lo + BLOCK] = part
                top = jnp.maximum(top, jnp.max(part, axis=0, keepdims=True))
        top = jnp.maximum(top, NEVER)
        w = jnp.exp2((new - top) * unit)
        total = jnp.sum(w, axis=0, keepdims=True)
        w = jnp.concatenate([w[tokens:], w[:tokens]], axis=0).astype(jnp.bfloat16)
        numer = lax.dot_general(fresh, w, TN, preferred_element_type=jnp.float32)
        for c in range(steps):
            at = c * STEP
            w = jnp.exp2((s_ref[at : at + STEP] - top) * unit)
            total = total + jnp.sum(w, axis=0, keepdims=True)
            values = jnp.concatenate([kv_ref[f, at : at + STEP, HEAD_DIM:] for f in fork], axis=1)
            numer = numer + lax.dot_general(
                values, w.astype(jnp.bfloat16), TN, preferred_element_type=jnp.float32
            )
        own = numer[:HEAD_DIM]
        for j in range(1, both):
            own = jnp.where(place == j, numer[j * HEAD_DIM : (j + 1) * HEAD_DIM], own)
        here = pl.ds(pl.multiple_of(g * 128, 128), 128)
        if code:
            code_part(top * unit, total, own, out, here)
        else:
            out[:HEAD_DIM, here] = own
            out[HEAD_DIM:, here] = meta_rows(META, top * unit, total, total)

    def group(g, carry):
        most = functools.reduce(jnp.maximum, [info[1 + g * both + j] for j in range(both)])
        for steps in range(cap // STEP + 1):
            pl.when((most > (steps - 1) * STEP) & (most <= steps * STEP))(
                functools.partial(several, g, steps)
            )
        return carry

    lax.fori_loop(0, forks // both, group, 0)


def part_of(blocks_q, info, cache, fresh, tokens, offset, *after, code=False):
    members, forks, carried, _ = blocks_q.shape
    rows = carried - 2 * tokens
    cap, width = cache.shape[1:]
    keys = cap + tokens
    height = HEAD_DIM + (CODE if code else META)
    vmem = pl.BlockSpec(memory_space=pltpu.VMEM)
    return pl.pallas_call(
        functools.partial(part_kernel, offset, code, tokens),
        in_specs=[pl.BlockSpec(memory_space=pltpu.SMEM)] + [vmem] * (3 + len(after)),
        out_specs=vmem,
        scratch_shapes=[pltpu.VMEM((cap, 128), jnp.float32)],
        out_shape=jax.ShapeDtypeStruct((height, forks * rows), jnp.int16 if code else jnp.float32),
        compiler_params=pltpu.CompilerParams(vmem_limit_bytes=16 * 2**20),
        cost_estimate=pl.CostEstimate(
            flops=4 * forks * rows * keys * HEAD_DIM,
            transcendentals=forks * rows * keys,
            bytes_accessed=2 * forks * keys * width,
        ),
        name="part",
    )(info, blocks_q, fresh, cache, *after)


def merge_kernel(msg, part, out):
    for at in range(0, msg.shape[1], 128):
        sl = slice(at, at + 128)
        top, total, numer = joined([sent_part(msg, sl), held_part(part, sl)])
        code_part(top, total, numer, out, sl)


def merge(msg, part):
    return pl.pallas_call(
        merge_kernel,
        out_shape=jax.ShapeDtypeStruct(msg.shape, msg.dtype),
        compiler_params=pltpu.CompilerParams(vmem_limit_bytes=8 * 2**20),
        name="merge",
    )(msg, part)


def finish_kernel(tokens, rows, info, span, own, right, left, out):
    me = info[0]
    forks = own.shape[1] // rows
    both = 128 // rows
    spot = lax.rem(lax.broadcasted_iota(jnp.int32, (rows, HEAD_DIM), 0), tokens) + me * tokens
    for g in range(forks // both):
        sl = slice(g * 128, (g + 1) * 128)
        _, total, numer = joined([held_part(own, sl), sent_part(right, sl), sent_part(left, sl)])
        turned = (numer / total).T
        for j in range(both):
            f = g * both + j
            value = turned[j * rows : (j + 1) * rows]
            out[f] = jnp.where(spot < span[f], value, 0.0).astype(jnp.bfloat16)


def finish(info, span, own, right, left, tokens, rows):
    forks = own.shape[1] // rows
    smem = pl.BlockSpec(memory_space=pltpu.SMEM)
    vmem = pl.BlockSpec(memory_space=pltpu.VMEM)
    return pl.pallas_call(
        functools.partial(finish_kernel, tokens, rows),
        in_specs=[smem, smem, vmem, vmem, vmem],
        out_specs=vmem,
        out_shape=jax.ShapeDtypeStruct((forks, rows, HEAD_DIM), jnp.bfloat16),
        compiler_params=pltpu.CompilerParams(vmem_limit_bytes=8 * 2**20),
        name="finish",
    )(info, span, own, right, left)


def own_kernel(tokens, info, span, owner, rows_ref, out):
    members, forks = rows_ref.shape[:2]
    me = info[0]
    row = lax.rem(lax.broadcasted_iota(jnp.int32, (2 * tokens, HEAD_DIM), 0), tokens)
    for i in range(members):
        picked = jnp.zeros((2 * tokens, HEAD_DIM), jnp.float32)
        for f in range(forks):
            mine = (owner[f] == me) & (row + i * tokens < span[f])
            picked = jnp.where(mine, rows_ref[i, f].astype(jnp.float32), picked)
        out[i * tokens : (i + 1) * tokens, :HEAD_DIM] = picked[:tokens]
        out[i * tokens : (i + 1) * tokens, HEAD_DIM:] = picked[tokens:]


def own_kv(info, span, owner, q, tokens, width):
    members, forks, carried, _ = q.shape
    smem = pl.BlockSpec(memory_space=pltpu.SMEM)
    at = carried // (2 * tokens) - 1
    return pl.pallas_call(
        functools.partial(own_kernel, tokens),
        grid=(1,),
        in_specs=[smem] * 3
        + [pl.BlockSpec((members, forks, 2 * tokens, HEAD_DIM), lambda g: (0, 0, at, 0))],
        out_specs=pl.BlockSpec((members * tokens, width), lambda g: (0, 0)),
        out_shape=jax.ShapeDtypeStruct((members * tokens, width), jnp.float32),
        compiler_params=pltpu.CompilerParams(vmem_limit_bytes=8 * 2**20),
        name="own_kv",
    )(info, span, owner, q).astype(jnp.bfloat16)


def body(queries, tool_key_value, cache, placed, blocks, span_len, owner):
    forks, tokens, width = tool_key_value.shape
    heads = queries.shape[2] // HEAD_DIM
    rows = heads * tokens
    me = lax.axis_index("inst")
    members = lax.axis_size("inst")
    half = members // 2
    live = placed[:, 0] * blocks[:, 0] * BLOCK
    info = jnp.concatenate([me.astype(jnp.int32)[None], live])
    own_q = queries.reshape(forks, tokens, heads, HEAD_DIM).transpose(0, 2, 1, 3)
    fresh = tool_key_value.reshape(forks, tokens, 2, HEAD_DIM).transpose(0, 2, 1, 3)
    own_q, fresh = own_q.reshape(forks, rows, HEAD_DIM), fresh.reshape(forks, 2 * tokens, HEAD_DIM)
    sent = jnp.concatenate([own_q, fresh], axis=1).astype(jnp.float32) * WIDE
    q = lax.all_gather(sent.astype(jnp.float16), "inst", axis=0)
    q = (q.astype(jnp.float32) * (1.0 / WIDE)).astype(jnp.bfloat16)

    part = functools.partial(part_of, q, info, cache, fresh, tokens)
    right, left = part(half - 1, code=True), part(-half, code=True)
    for k in range(half - 1, 0, -1):
        if k > 1:
            mine = part(k - 1, left)
            right = merge(passed_along(right, 1), mine)
            mine = part(-k, right)
        else:
            right = passed_along(right, 1)
            mine = part(-k, left)
        left = merge(passed_along(left, -1), mine)
    mine = part(0, left)
    left = passed_along(left, -1)
    owned = own_kv(info, span_len, owner, q, tokens, width).reshape(1, 1, members * tokens, width)
    attended = finish(info, span_len, mine, right, left, tokens, rows)
    attended = attended.reshape(forks, heads, tokens, HEAD_DIM).transpose(0, 2, 1, 3)
    return attended.reshape(forks, tokens, heads * HEAD_DIM), owned


def solution(mesh):
    return jax.shard_map(
        body,
        mesh=mesh,
        in_specs=(
            P(("groups", "rep"), "inst", "tp"),
            P(("groups", "rep"), "inst", "tp"),
            P(("groups", "rep"), "inst", "tp"),
            P(("groups", "rep"), "inst"),
            P(("groups", "rep"), "inst"),
            P(("groups", "rep")),
            P(("groups", "rep")),
        ),
        out_specs=(P(("groups", "rep"), "inst", "tp"), P(("groups", "inst"), "rep", None, "tp")),
        check_vma=False,
    )
```

time: 182 us -> 196 us (1.077)
  Pallas kernels: 30.3 us -> 47.5 us
  waiting for transfers between devices: 7.76 us -> 0.04 us
  starting transfers between devices: 50.7 us -> 54.6 us
    pallas_call x18 -> x29, Pallas kernels: 28.2 us -> 45.4 us  [the longest x16 43.2 us: part_of(): pl.pallas_call(functools.partial(part_kernel, offset, code, tokens), in_s...]
    ppermute x15, waiting for transfers between devices: 7.76 us -> 0.04 us  [passed_along(): return lax.ppermute(x, 'inst', [(i, (i + by) % size) for i in range(size)])]
    ppermute x15, starting transfers between devices: 50.7 us -> 54.6 us  [passed_along(): return lax.ppermute(x, 'inst', [(i, (i + by) % size) for i in range(size)])]
  transfers between devices with their start and end apart: 15 -> 15, of which waited for: 5 -> 0; matrix products, arithmetic and copies ran while one was open for 0% -> 0% of each run, Pallas kernels for 13% -> 22%
where the time goes in v3:
time: 196 us; the launch traced here: 195 us
  blocking collectives  87.7 us (45%)
  starting transfers between devices  54.6 us (28%)
  Pallas kernels  47.5 us (24%)
  other arithmetic  2.41 us (1%)
    all_gather x1, blocking collectives, body(): q = lax.all_gather(sent.astype(jnp.float16), 'inst', axis=0)  87.7 us
    ppermute x15, starting transfers between devices, passed_along(): return lax.ppermute(x, 'inst', [(i, (i + by) % size) for i in range(size)])  54.6 us
    pallas_call x16, Pallas kernels, part_of(): pl.pallas_call(functools.partial(part_kernel, offset, code, tokens), in_s...  43.2 us
  transfers between devices with their start and end apart: 15, of which 0 were waited for; matrix products, arithmetic and copies ran while one was open for 0% of the time, Pallas kernels for 22%

profile of v3, /device:TPU:80, one launch (start us, length us, event | category | flops | bytes accessed | tf_op | source)
XLA Modules:
  0.0 194.5 jit_solution(15773476532542052478)
XLA Ops:
  0.6 1.0 multiply_convert_fusion.1
  1.6 87.7 %all-gather.1 = f16[16,8,80,128]{3,2,1,0:T(8,128)(2,1)S(1)} all-gather(f16[1,8,80,128]{3,2,1,0:T(8,128)(2,1)S(1)} %multiply_convert_fusion.1), channel_id=1, replica_groups=mesh['groups'=2,'inst'=16,'tp'=8,'rep'=2] {'inst'}, dimensions={0}, use_global_device_ids=true | all-gather | bytes 2785280 | tf_op jit(solution)/shard_map/all_gather | solution.py:260
  89.3 0.7 multiply_convert_fusion.q_ref.rows_ref
  90.1 0.1 pad_add_fusion.info
  90.2 1.1 copy-done
  91.3 2.8 %part.17 = s16[136,512]{1,0:T(8,128)(2,1)S(1)} custom-call(s32[9]{0:T(128)S(1)} %pad_add_fusion.info, bf16[16,8,80,128]{3,2,1,0:T(8,128)(2,1)S(1)} %multiply_convert_fusion.q_ref.rows_ref, bf16[8,16,128]{2,1,0:T(8,128)(2,1)S(1)} %bitcast.23, bf16[8,768,256]{2,1,0:T(8,128)(2,1)S(1)} %copy-done), custom_call_target="tpu_custom_call" | custom-call | flops 203423744 | bytes 3178496 | tf_op jit(solution)/shard_map/part/pallas_call | solution.py:157
  94.1 2.0 %collective-permute-start.1 = (s16[136,512]{1,0:T(8,128)(2,1)S(1)}, s16[136,512]{1,0:T(8,128)(2,1)S(1)}, u32[]{:S(2)}, u32[]{:S(2)}) collective-permute-start(s16[136,512]{1,0:T(8,128)(2,1)S(1)} %part.17), channel_id=1, source_target_pairs={{0,16},{16,32},{32,48},{48,64},{64,80},{80,96},{96,112},{112,128},... | collective-permute-start | bytes 417800 | tf_op jit(solution)/shard_map/ppermute | solution.py:25
  96.1 2.9 %part.16.rest_0_ = s16[136,512]{1,0:T(8,128)(2,1)S(1)} custom-call(s32[9]{0:T(128)S(1)} %pad_add_fusion.info, bf16[16,8,80,128]{3,2,1,0:T(8,128)(2,1)S(1)} %multiply_convert_fusion.q_ref.rows_ref, bf16[8,16,128]{2,1,0:T(8,128)(2,1)S(1)} %bitcast.24, bf16[8,768,256]{2,1,0:T(8,128)(2,1)S(1)} %copy-done), custom_call_target="tpu_custom_call" | custom-call | flops 203423744 | bytes 3178496 | tf_op jit(solution)/shard_map/part/pallas_call | solution.py:157
  98.9 5.4 %collective-permute-start = (s16[136,512]{1,0:T(8,128)(2,1)S(1)}, s16[136,512]{1,0:T(8,128)(2,1)S(1)}, u32[]{:S(2)}, u32[]{:S(2)}) collective-permute-start(s16[136,512]{1,0:T(8,128)(2,1)S(1)} %part.16.rest_0_), channel_id=1, source_target_pairs={{0,240},{16,0},{32,16},{48,32},{64,48},{80,64},{96,80},{112,96},{1... | collective-permute-start | bytes 417800 | tf_op jit(solution)/shard_map/ppermute | solution.py:25
  104.4 2.7 %part.18 = f32[136,512]{1,0:T(8,128)S(1)} custom-call(s32[9]{0:T(128)S(1)} %pad_add_fusion.info, bf16[16,8,80,128]{3,2,1,0:T(8,128)(2,1)S(1)} %multiply_convert_fusion.q_ref.rows_ref, bf16[8,16,128]{2,1,0:T(8,128)(2,1)S(1)} %bitcast.25, bf16[8,768,256]{2,1,0:T(8,128)(2,1)S(1)} %copy-done, s16[136,512]{1,0:T(8,128)(2,1)S(1)} %part.16.rest_0_), custom_call_target="tpu_custom_call" | custom-call | flops 203423744 | bytes 3178496 | tf_op jit(solution)/shard_map/part/pallas_call | solution.py:157
  107.1 0.0 collective-permute-done.1.msg
  107.1 0.2 merge.13.rest_0_
  107.3 2.0 %collective-permute-start.3 = (s16[136,512]{1,0:T(8,128)(2,1)S(1)}, s16[136,512]{1,0:T(8,128)(2,1)S(1)}, u32[]{:S(2)}, u32[]{:S(2)}) collective-permute-start(s16[136,512]{1,0:T(8,128)(2,1)S(1)} %merge.13.rest_0_), channel_id=1, source_target_pairs={{0,16},{16,32},{32,48},{48,64},{64,80},{80,96},{96,112},{112,128},... | collective-permute-start | bytes 417800 | tf_op jit(solution)/shard_map/ppermute | solution.py:25
  109.2 2.7 %part.19 = f32[136,512]{1,0:T(8,128)S(1)} custom-call(s32[9]{0:T(128)S(1)} %pad_add_fusion.info, bf16[16,8,80,128]{3,2,1,0:T(8,128)(2,1)S(1)} %multiply_convert_fusion.q_ref.rows_ref, bf16[8,16,128]{2,1,0:T(8,128)(2,1)S(1)} %bitcast.26, bf16[8,768,256]{2,1,0:T(8,128)(2,1)S(1)} %copy-done, s16[136,512]{1,0:T(8,128)(2,1)S(1)} %merge.13.rest_0_), custom_call_target="tpu_custom_call" | custom-call | flops 203423744 | bytes 3178496 | tf_op jit(solution)/shard_map/part/pallas_call | solution.py:157
  111.9 0.0 collective-permute-done.msg
  111.9 0.2 merge.14.rest_0_
  112.1 5.5 %collective-permute-start.2 = (s16[136,512]{1,0:T(8,128)(2,1)S(1)}, s16[136,512]{1,0:T(8,128)(2,1)S(1)}, u32[]{:S(2)}, u32[]{:S(2)}) collective-permute-start(s16[136,512]{1,0:T(8,128)(2,1)S(1)} %merge.14.rest_0_), channel_id=1, source_target_pairs={{0,240},{16,0},{32,16},{48,32},{64,48},{80,64},{96,80},{112,96},{1... | collective-permute-start | bytes 417800 | tf_op jit(solution)/shard_map/ppermute | solution.py:25
  117.6 2.7 %part.20 = f32[136,512]{1,0:T(8,128)S(1)} custom-call(s32[9]{0:T(128)S(1)} %pad_add_fusion.info, bf16[16,8,80,128]{3,2,1,0:T(8,128)(2,1)S(1)} %multiply_convert_fusion.q_ref.rows_ref, bf16[8,16,128]{2,1,0:T(8,128)(2,1)S(1)} %bitcast.27, bf16[8,768,256]{2,1,0:T(8,128)(2,1)S(1)} %copy-done, s16[136,512]{1,0:T(8,128)(2,1)S(1)} %merge.14.rest_0_), custom_call_target="tpu_custom_call" | custom-call | flops 203423744 | bytes 3178496 | tf_op jit(solution)/shard_map/part/pallas_call | solution.py:157
  120.2 0.0 collective-permute-done.3.msg
  120.3 0.2 merge.15.rest_0_
  120.4 2.0 %collective-permute-start.5 = (s16[136,512]{1,0:T(8,128)(2,1)S(1)}, s16[136,512]{1,0:T(8,128)(2,1)S(1)}, u32[]{:S(2)}, u32[]{:S(2)}) collective-permute-start(s16[136,512]{1,0:T(8,128)(2,1)S(1)} %merge.15.rest_0_), channel_id=1, source_target_pairs={{0,16},{16,32},{32,48},{48,64},{64,80},{80,96},{96,112},{112,128},... | collective-permute-start | bytes 417800 | tf_op jit(solution)/shard_map/ppermute | solution.py:25
  122.4 2.7 %part.21 = f32[136,512]{1,0:T(8,128)S(1)} custom-call(s32[9]{0:T(128)S(1)} %pad_add_fusion.info, bf16[16,8,80,128]{3,2,1,0:T(8,128)(2,1)S(1)} %multiply_convert_fusion.q_ref.rows_ref, bf16[8,16,128]{2,1,0:T(8,128)(2,1)S(1)} %bitcast.28, bf16[8,768,256]{2,1,0:T(8,128)(2,1)S(1)} %copy-done, s16[136,512]{1,0:T(8,128)(2,1)S(1)} %merge.15.rest_0_), custom_call_target="tpu_custom_call" | custom-call | flops 203423744 | bytes 3178496 | tf_op jit(solution)/shard_map/part/pallas_call | solution.py:157
  125.1 0.2 merge.16.rest_0_
  125.3 5.5 %collective-permute-start.4 = (s16[136,512]{1,0:T(8,128)(2,1)S(1)}, s16[136,512]{1,0:T(8,128)(2,1)S(1)}, u32[]{:S(2)}, u32[]{:S(2)}) collective-permute-start(s16[136,512]{1,0:T(8,128)(2,1)S(1)} %merge.16.rest_0_), channel_id=1, source_target_pairs={{0,240},{16,0},{32,16},{48,32},{64,48},{80,64},{96,80},{112,96},{1... | collective-permute-start | bytes 417800 | tf_op jit(solution)/shard_map/ppermute | solution.py:25
  130.7 2.7 %part.22 = f32[136,512]{1,0:T(8,128)S(1)} custom-call(s32[9]{0:T(128)S(1)} %pad_add_fusion.info, bf16[16,8,80,128]{3,2,1,0:T(8,128)(2,1)S(1)} %multiply_convert_fusion.q_ref.rows_ref, bf16[8,16,128]{2,1,0:T(8,128)(2,1)S(1)} %bitcast.29, bf16[8,768,256]{2,1,0:T(8,128)(2,1)S(1)} %copy-done, s16[136,512]{1,0:T(8,128)(2,1)S(1)} %merge.16.rest_0_), custom_call_target="tpu_custom_call" | custom-call | flops 203423744 | bytes 3178496 | tf_op jit(solution)/shard_map/part/pallas_call | solution.py:157
  133.4 0.2 merge.17.rest_0_
  133.6 2.1 %collective-permute-start.7 = (s16[136,512]{1,0:T(8,128)(2,1)S(1)}, s16[136,512]{1,0:T(8,128)(2,1)S(1)}, u32[]{:S(2)}, u32[]{:S(2)}) collective-permute-start(s16[136,512]{1,0:T(8,128)(2,1)S(1)} %merge.17.rest_0_), channel_id=1, source_target_pairs={{0,16},{16,32},{32,48},{48,64},{64,80},{80,96},{96,112},{112,128},... | collective-permute-start | bytes 417800 | tf_op jit(solution)/shard_map/ppermute | solution.py:25
  135.7 2.7 %part.23 = f32[136,512]{1,0:T(8,128)S(1)} custom-call(s32[9]{0:T(128)S(1)} %pad_add_fusion.info, bf16[16,8,80,128]{3,2,1,0:T(8,128)(2,1)S(1)} %multiply_convert_fusion.q_ref.rows_ref, bf16[8,16,128]{2,1,0:T(8,128)(2,1)S(1)} %bitcast.30, bf16[8,768,256]{2,1,0:T(8,128)(2,1)S(1)} %copy-done, s16[136,512]{1,0:T(8,128)(2,1)S(1)} %merge.17.rest_0_), custom_call_target="tpu_custom_call" | custom-call | flops 203423744 | bytes 3178496 | tf_op jit(solution)/shard_map/part/pallas_call | solution.py:157
  138.4 0.0 collective-permute-done.4.msg
  138.4 0.2 merge.18.rest_0_
  138.6 5.4 %collective-permute-start.6 = (s16[136,512]{1,0:T(8,128)(2,1)S(1)}, s16[136,512]{1,0:T(8,128)(2,1)S(1)}, u32[]{:S(2)}, u32[]{:S(2)}) collective-permute-start(s16[136,512]{1,0:T(8,128)(2,1)S(1)} %merge.18.rest_0_), channel_id=1, source_target_pairs={{0,240},{16,0},{32,16},{48,32},{64,48},{80,64},{96,80},{112,96},{1... | collective-permute-start | bytes 417800 | tf_op jit(solution)/shard_map/ppermute | solution.py:25
  144.1 2.7 %part.24 = f32[136,512]{1,0:T(8,128)S(1)} custom-call(s32[9]{0:T(128)S(1)} %pad_add_fusion.info, bf16[16,8,80,128]{3,2,1,0:T(8,128)(2,1)S(1)} %multiply_convert_fusion.q_ref.rows_ref, bf16[8,16,128]{2,1,0:T(8,128)(2,1)S(1)} %bitcast.31, bf16[8,768,256]{2,1,0:T(8,128)(2,1)S(1)} %copy-done, s16[136,512]{1,0:T(8,128)(2,1)S(1)} %merge.18.rest_0_), custom_call_target="tpu_custom_call" | custom-call | flops 203423744 | bytes 3178496 | tf_op jit(solution)/shard_map/part/pallas_call | solution.py:157
  146.7 0.0 collective-permute-done.7.msg
  146.8 0.2 merge.19.rest_0_
  146.9 2.0 %collective-permute-start.9 = (s16[136,512]{1,0:T(8,128)(2,1)S(1)}, s16[136,512]{1,0:T(8,128)(2,1)S(1)}, u32[]{:S(2)}, u32[]{:S(2)}) collective-permute-start(s16[136,512]{1,0:T(8,128)(2,1)S(1)} %merge.19.rest_0_), channel_id=1, source_target_pairs={{0,16},{16,32},{32,48},{48,64},{64,80},{80,96},{96,112},{112,128},... | collective-permute-start | bytes 417800 | tf_op jit(solution)/shard_map/ppermute | solution.py:25
  148.9 2.7 %part.25 = f32[136,512]{1,0:T(8,128)S(1)} custom-call(s32[9]{0:T(128)S(1)} %pad_add_fusion.info, bf16[16,8,80,128]{3,2,1,0:T(8,128)(2,1)S(1)} %multiply_convert_fusion.q_ref.rows_ref, bf16[8,16,128]{2,1,0:T(8,128)(2,1)S(1)} %bitcast.32, bf16[8,768,256]{2,1,0:T(8,128)(2,1)S(1)} %copy-done, s16[136,512]{1,0:T(8,128)(2,1)S(1)} %merge.19.rest_0_), custom_call_target="tpu_custom_call" | custom-call | flops 203423744 | bytes 3178496 | tf_op jit(solution)/shard_map/part/pallas_call | solution.py:157
  151.6 0.0 collective-permute-done.6.msg
  151.6 0.2 merge.20.rest_0_
  151.8 5.5 %collective-permute-start.8 = (s16[136,512]{1,0:T(8,128)(2,1)S(1)}, s16[136,512]{1,0:T(8,128)(2,1)S(1)}, u32[]{:S(2)}, u32[]{:S(2)}) collective-permute-start(s16[136,512]{1,0:T(8,128)(2,1)S(1)} %merge.20.rest_0_), channel_id=1, source_target_pairs={{0,240},{16,0},{32,16},{48,32},{64,48},{80,64},{96,80},{112,96},{1... | collective-permute-start | bytes 417800 | tf_op jit(solution)/shard_map/ppermute | solution.py:25
  157.2 2.7 %part.26 = f32[136,512]{1,0:T(8,128)S(1)} custom-call(s32[9]{0:T(128)S(1)} %pad_add_fusion.info, bf16[16,8,80,128]{3,2,1,0:T(8,128)(2,1)S(1)} %multiply_convert_fusion.q_ref.rows_ref, bf16[8,16,128]{2,1,0:T(8,128)(2,1)S(1)} %bitcast.33, bf16[8,768,256]{2,1,0:T(8,128)(2,1)S(1)} %copy-done, s16[136,512]{1,0:T(8,128)(2,1)S(1)} %merge.20.rest_0_), custom_call_target="tpu_custom_call" | custom-call | flops 203423744 | bytes 3178496 | tf_op jit(solution)/shard_map/part/pallas_call | solution.py:157
  159.9 0.0 collective-permute-done.9.msg
  159.9 0.2 merge.21.rest_0_
  160.1 2.0 %collective-permute-start.11 = (s16[136,512]{1,0:T(8,128)(2,1)S(1)}, s16[136,512]{1,0:T(8,128)(2,1)S(1)}, u32[]{:S(2)}, u32[]{:S(2)}) collective-permute-start(s16[136,512]{1,0:T(8,128)(2,1)S(1)} %merge.21.rest_0_), channel_id=1, source_target_pairs={{0,16},{16,32},{32,48},{48,64},{64,80},{80,96},{96,112},{112,128},... | collective-permute-start | bytes 417800 | tf_op jit(solution)/shard_map/ppermute | solution.py:25
  162.1 2.7 %part.27 = f32[136,512]{1,0:T(8,128)S(1)} custom-call(s32[9]{0:T(128)S(1)} %pad_add_fusion.info, bf16[16,8,80,128]{3,2,1,0:T(8,128)(2,1)S(1)} %multiply_convert_fusion.q_ref.rows_ref, bf16[8,16,128]{2,1,0:T(8,128)(2,1)S(1)} %bitcast.34, bf16[8,768,256]{2,1,0:T(8,128)(2,1)S(1)} %copy-done, s16[136,512]{1,0:T(8,128)(2,1)S(1)} %merge.21.rest_0_), custom_call_target="tpu_custom_call" | custom-call | flops 203423744 | bytes 3178496 | tf_op jit(solution)/shard_map/part/pallas_call | solution.py:157
  164.7 0.0 collective-permute-done.8.msg
  164.7 0.2 merge.22.rest_0_
  164.9 5.5 %collective-permute-start.10 = (s16[136,512]{1,0:T(8,128)(2,1)S(1)}, s16[136,512]{1,0:T(8,128)(2,1)S(1)}, u32[]{:S(2)}, u32[]{:S(2)}) collective-permute-start(s16[136,512]{1,0:T(8,128)(2,1)S(1)} %merge.22.rest_0_), channel_id=1, source_target_pairs={{0,240},{16,0},{32,16},{48,32},{64,48},{80,64},{96,80},{112,96},{1... | collective-permute-start | bytes 417800 | tf_op jit(solution)/shard_map/ppermute | solution.py:25
  170.4 2.7 %part.28 = f32[136,512]{1,0:T(8,128)S(1)} custom-call(s32[9]{0:T(128)S(1)} %pad_add_fusion.info, bf16[16,8,80,128]{3,2,1,0:T(8,128)(2,1)S(1)} %multiply_convert_fusion.q_ref.rows_ref, bf16[8,16,128]{2,1,0:T(8,128)(2,1)S(1)} %bitcast.35, bf16[8,768,256]{2,1,0:T(8,128)(2,1)S(1)} %copy-done, s16[136,512]{1,0:T(8,128)(2,1)S(1)} %merge.22.rest_0_), custom_call_target="tpu_custom_call" | custom-call | flops 203423744 | bytes 3178496 | tf_op jit(solution)/shard_map/part/pallas_call | solution.py:157
  173.1 0.2 merge.23.rest_0_
  173.3 0.0 copy-start.2
  173.3 0.0 copy-start.3
  173.3 2.7 %part.29 = f32[136,512]{1,0:T(8,128)S(1)} custom-call(s32[9]{0:T(128)S(1)} %pad_add_fusion.info, bf16[16,8,80,128]{3,2,1,0:T(8,128)(2,1)S(1)} %multiply_convert_fusion.q_ref.rows_ref, bf16[8,16,128]{2,1,0:T(8,128)(2,1)S(1)} %bitcast.36, bf16[8,768,256]{2,1,0:T(8,128)(2,1)S(1)} %copy-done, s16[136,512]{1,0:T(8,128)(2,1)S(1)} %merge.23.rest_0_), custom_call_target="tpu_custom_call" | custom-call | flops 203423744 | bytes 3178496 | tf_op jit(solution)/shard_map/part/pallas_call | solution.py:157
  176.0 0.2 merge.24.rest_0_
  176.2 2.6 %collective-permute-start.12 = (s16[136,512]{1,0:T(8,128)(2,1)S(1)}, s16[136,512]{1,0:T(8,128)(2,1)S(1)}, u32[]{:S(2)}, u32[]{:S(2)}) collective-permute-start(s16[136,512]{1,0:T(8,128)(2,1)S(1)} %merge.24.rest_0_), channel_id=1, source_target_pairs={{0,240},{16,0},{32,16},{48,32},{64,48},{80,64},{96,80},{112,96},{1... | collective-permute-start | bytes 417800 | tf_op jit(solution)/shard_map/ppermute | solution.py:25
  178.8 0.7 own_kv.1
  179.5 3.3 %collective-permute-start.13 = (s16[136,512]{1,0:T(8,128)(2,1)S(1)}, s16[136,512]{1,0:T(8,128)(2,1)S(1)}, u32[]{:S(2)}, u32[]{:S(2)}) collective-permute-start(s16[136,512]{1,0:T(8,128)(2,1)S(1)} %merge.23.rest_0_), channel_id=1, source_target_pairs={{0,16},{16,32},{32,48},{48,64},{64,80},{80,96},{96,112},{112,128},... | collective-permute-start | bytes 417800 | tf_op jit(solution)/shard_map/ppermute | solution.py:25
  182.8 2.7 %part.30 = f32[136,512]{1,0:T(8,128)S(1)} custom-call(s32[9]{0:T(128)S(1)} %pad_add_fusion.info, bf16[16,8,80,128]{3,2,1,0:T(8,128)(2,1)S(1)} %multiply_convert_fusion.q_ref.rows_ref, bf16[8,16,128]{2,1,0:T(8,128)(2,1)S(1)} %bitcast.37, bf16[8,768,256]{2,1,0:T(8,128)(2,1)S(1)} %copy-done, s16[136,512]{1,0:T(8,128)(2,1)S(1)} %merge.24.rest_0_), custom_call_target="tpu_custom_call" | custom-call | flops 203423744 | bytes 3178496 | tf_op jit(solution)/shard_map/part/pallas_call | solution.py:157
  185.5 0.0 collective-permute-done.12.msg
  185.5 0.2 merge.25.rest_0_
  185.7 4.1 %collective-permute-start.14 = (s16[136,512]{1,0:T(8,128)(2,1)S(1)}, s16[136,512]{1,0:T(8,128)(2,1)S(1)}, u32[]{:S(2)}, u32[]{:S(2)}) collective-permute-start(s16[136,512]{1,0:T(8,128)(2,1)S(1)} %merge.25.rest_0_), channel_id=1, source_target_pairs={{0,240},{16,0},{32,16},{48,32},{64,48},{80,64},{96,80},{112,96},{1... | collective-permute-start | bytes 417800 | tf_op jit(solution)/shard_map/ppermute | solution.py:25
  189.8 0.6 convert_bitcast_fusion
  190.4 2.7 %part.31.own = f32[136,512]{1,0:T(8,128)S(1)} custom-call(s32[9]{0:T(128)S(1)} %pad_add_fusion.info, bf16[16,8,80,128]{3,2,1,0:T(8,128)(2,1)S(1)} %multiply_convert_fusion.q_ref.rows_ref, bf16[8,16,128]{2,1,0:T(8,128)(2,1)S(1)} %bitcast.38, bf16[8,768,256]{2,1,0:T(8,128)(2,1)S(1)} %copy-done, s16[136,512]{1,0:T(8,128)(2,1)S(1)} %merge.25.rest_0_), custom_call_target="tpu_custom_call" | custom-call | flops 203423744 | bytes 3178496 | tf_op jit(solution)/shard_map/part/pallas_call | solution.py:157
  193.1 0.0 collective-permute-done.14.left
  193.1 1.4 finish.1
  (15 shorter events, 0.0 us)
Async XLA Ops:
  89.3 0.7 copy-start.4
  89.3 0.7 copy-start.5
  89.3 1.9 copy-start
  89.3 1.9 copy-start.1
  94.1 13.0 %collective-permute-start.1 = (s16[136,512]{1,0:T(8,128)(2,1)S(1)}, s16[136,512]{1,0:T(8,128)(2,1)S(1)}, u32[]{:S(2)}, u32[]{:S(2)}) collective-permute-start(s16[136,512]{1,0:T(8,128)(2,1)S(1)} %part.17), channel_id=1, source_target_pairs={{0,16},{16,32},{32,48},{48,64},{64,80},{80,96},{96,112},{112,128},... | collective-permute-start | bytes 417800 | tf_op jit(solution)/shard_map/ppermute | solution.py:25
  98.9 13.0 %collective-permute-start = (s16[136,512]{1,0:T(8,128)(2,1)S(1)}, s16[136,512]{1,0:T(8,128)(2,1)S(1)}, u32[]{:S(2)}, u32[]{:S(2)}) collective-permute-start(s16[136,512]{1,0:T(8,128)(2,1)S(1)} %part.16.rest_0_), channel_id=1, source_target_pairs={{0,240},{16,0},{32,16},{48,32},{64,48},{80,64},{96,80},{112,96},{1... | collective-permute-start | bytes 417800 | tf_op jit(solution)/shard_map/ppermute | solution.py:25
  107.3 13.0 %collective-permute-start.3 = (s16[136,512]{1,0:T(8,128)(2,1)S(1)}, s16[136,512]{1,0:T(8,128)(2,1)S(1)}, u32[]{:S(2)}, u32[]{:S(2)}) collective-permute-start(s16[136,512]{1,0:T(8,128)(2,1)S(1)} %merge.13.rest_0_), channel_id=1, source_target_pairs={{0,16},{16,32},{32,48},{48,64},{64,80},{80,96},{96,112},{112,128},... | collective-permute-start | bytes 417800 | tf_op jit(solution)/shard_map/ppermute | solution.py:25
  112.1 13.0 %collective-permute-start.2 = (s16[136,512]{1,0:T(8,128)(2,1)S(1)}, s16[136,512]{1,0:T(8,128)(2,1)S(1)}, u32[]{:S(2)}, u32[]{:S(2)}) collective-permute-start(s16[136,512]{1,0:T(8,128)(2,1)S(1)} %merge.14.rest_0_), channel_id=1, source_target_pairs={{0,240},{16,0},{32,16},{48,32},{64,48},{80,64},{96,80},{112,96},{1... | collective-permute-start | bytes 417800 | tf_op jit(solution)/shard_map/ppermute | solution.py:25
  120.4 13.0 %collective-permute-start.5 = (s16[136,512]{1,0:T(8,128)(2,1)S(1)}, s16[136,512]{1,0:T(8,128)(2,1)S(1)}, u32[]{:S(2)}, u32[]{:S(2)}) collective-permute-start(s16[136,512]{1,0:T(8,128)(2,1)S(1)} %merge.15.rest_0_), channel_id=1, source_target_pairs={{0,16},{16,32},{32,48},{48,64},{64,80},{80,96},{96,112},{112,128},... | collective-permute-start | bytes 417800 | tf_op jit(solution)/shard_map/ppermute | solution.py:25
  125.3 13.2 %collective-permute-start.4 = (s16[136,512]{1,0:T(8,128)(2,1)S(1)}, s16[136,512]{1,0:T(8,128)(2,1)S(1)}, u32[]{:S(2)}, u32[]{:S(2)}) collective-permute-start(s16[136,512]{1,0:T(8,128)(2,1)S(1)} %merge.16.rest_0_), channel_id=1, source_target_pairs={{0,240},{16,0},{32,16},{48,32},{64,48},{80,64},{96,80},{112,96},{1... | collective-permute-start | bytes 417800 | tf_op jit(solution)/shard_map/ppermute | solution.py:25
  133.6 13.2 %collective-permute-start.7 = (s16[136,512]{1,0:T(8,128)(2,1)S(1)}, s16[136,512]{1,0:T(8,128)(2,1)S(1)}, u32[]{:S(2)}, u32[]{:S(2)}) collective-permute-start(s16[136,512]{1,0:T(8,128)(2,1)S(1)} %merge.17.rest_0_), channel_id=1, source_target_pairs={{0,16},{16,32},{32,48},{48,64},{64,80},{80,96},{96,112},{112,128},... | collective-permute-start | bytes 417800 | tf_op jit(solution)/shard_map/ppermute | solution.py:25
  138.6 13.0 %collective-permute-start.6 = (s16[136,512]{1,0:T(8,128)(2,1)S(1)}, s16[136,512]{1,0:T(8,128)(2,1)S(1)}, u32[]{:S(2)}, u32[]{:S(2)}) collective-permute-start(s16[136,512]{1,0:T(8,128)(2,1)S(1)} %merge.18.rest_0_), channel_id=1, source_target_pairs={{0,240},{16,0},{32,16},{48,32},{64,48},{80,64},{96,80},{112,96},{1... | collective-permute-start | bytes 417800 | tf_op jit(solution)/shard_map/ppermute | solution.py:25
  146.9 13.0 %collective-permute-start.9 = (s16[136,512]{1,0:T(8,128)(2,1)S(1)}, s16[136,512]{1,0:T(8,128)(2,1)S(1)}, u32[]{:S(2)}, u32[]{:S(2)}) collective-permute-start(s16[136,512]{1,0:T(8,128)(2,1)S(1)} %merge.19.rest_0_), channel_id=1, source_target_pairs={{0,16},{16,32},{32,48},{48,64},{64,80},{80,96},{96,112},{112,128},... | collective-permute-start | bytes 417800 | tf_op jit(solution)/shard_map/ppermute | solution.py:25
  151.8 13.0 %collective-permute-start.8 = (s16[136,512]{1,0:T(8,128)(2,1)S(1)}, s16[136,512]{1,0:T(8,128)(2,1)S(1)}, u32[]{:S(2)}, u32[]{:S(2)}) collective-permute-start(s16[136,512]{1,0:T(8,128)(2,1)S(1)} %merge.20.rest_0_), channel_id=1, source_target_pairs={{0,240},{16,0},{32,16},{48,32},{64,48},{80,64},{96,80},{112,96},{1... | collective-permute-start | bytes 417800 | tf_op jit(solution)/shard_map/ppermute | solution.py:25
  160.1 13.0 %collective-permute-start.11 = (s16[136,512]{1,0:T(8,128)(2,1)S(1)}, s16[136,512]{1,0:T(8,128)(2,1)S(1)}, u32[]{:S(2)}, u32[]{:S(2)}) collective-permute-start(s16[136,512]{1,0:T(8,128)(2,1)S(1)} %merge.21.rest_0_), channel_id=1, source_target_pairs={{0,16},{16,32},{32,48},{48,64},{64,80},{80,96},{96,112},{112,128},... | collective-permute-start | bytes 417800 | tf_op jit(solution)/shard_map/ppermute | solution.py:25
  164.9 11.1 %collective-permute-start.10 = (s16[136,512]{1,0:T(8,128)(2,1)S(1)}, s16[136,512]{1,0:T(8,128)(2,1)S(1)}, u32[]{:S(2)}, u32[]{:S(2)}) collective-permute-start(s16[136,512]{1,0:T(8,128)(2,1)S(1)} %merge.22.rest_0_), channel_id=1, source_target_pairs={{0,240},{16,0},{32,16},{48,32},{64,48},{80,64},{96,80},{112,96},{1... | collective-permute-start | bytes 417800 | tf_op jit(solution)/shard_map/ppermute | solution.py:25
  173.3 5.5 %copy-start.2 = (s32[8]{0:T(128)S(1)}, s32[8]{0:T(128)}, u32[]{:S(2)}) copy-start(s32[8]{0:T(128)} %span.3) | copy-start | bytes 100
  173.3 5.5 %copy-start.3 = (s32[8]{0:T(128)S(1)}, s32[8]{0:T(128)}, u32[]{:S(2)}) copy-start(s32[8]{0:T(128)} %owner.1) | copy-start | bytes 100
  176.2 9.3 %collective-permute-start.12 = (s16[136,512]{1,0:T(8,128)(2,1)S(1)}, s16[136,512]{1,0:T(8,128)(2,1)S(1)}, u32[]{:S(2)}, u32[]{:S(2)}) collective-permute-start(s16[136,512]{1,0:T(8,128)(2,1)S(1)} %merge.24.rest_0_), channel_id=1, source_target_pairs={{0,240},{16,0},{32,16},{48,32},{64,48},{80,64},{96,80},{112,96},{1... | collective-permute-start | bytes 417800 | tf_op jit(solution)/shard_map/ppermute | solution.py:25
  179.5 13.6 %collective-permute-start.13 = (s16[136,512]{1,0:T(8,128)(2,1)S(1)}, s16[136,512]{1,0:T(8,128)(2,1)S(1)}, u32[]{:S(2)}, u32[]{:S(2)}) collective-permute-start(s16[136,512]{1,0:T(8,128)(2,1)S(1)} %merge.23.rest_0_), channel_id=1, source_target_pairs={{0,16},{16,32},{32,48},{48,64},{64,80},{80,96},{96,112},{112,128},... | collective-permute-start | bytes 417800 | tf_op jit(solution)/shard_map/ppermute | solution.py:25
  185.7 7.4 %collective-permute-start.14 = (s16[136,512]{1,0:T(8,128)(2,1)S(1)}, s16[136,512]{1,0:T(8,128)(2,1)S(1)}, u32[]{:S(2)}, u32[]{:S(2)}) collective-permute-start(s16[136,512]{1,0:T(8,128)(2,1)S(1)} %merge.25.rest_0_), channel_id=1, source_target_pairs={{0,240},{16,0},{32,16},{48,32},{64,48},{80,64},{96,80},{112,96},{1... | collective-permute-start | bytes 417800 | tf_op jit(solution)/shard_map/ppermute | solution.py:25

commit v4 on v2

--- a/solution.py
+++ b/solution.py
@@ -12,7 +12,7 @@
 BLOCK = 128
 STEP = 256
 META = 8
-CODE = 16
+CODE = 8
 NEVER = -1e30
 WIDE = 4096.0
 FLOOR = -2000.0
@@ -73,126 +73,108 @@
     return level, 1.0, mean
 
 
-def part_kernel(offsets, codes, members, tokens, rows, info, *refs):
+def part_kernel(offsets, codes, tokens, info, q_ref, fresh_ref, kv_ref, *rest):
     n = len(offsets)
-    q_refs, fresh_ref, kv_ref = refs[:n], refs[n], refs[n + 1]
-    out_refs, s_ref, o_ref = refs[n + 2 : 2 * n + 2], refs[2 * n + 2], refs[2 * n + 3]
-    forks = kv_ref.shape[0]
+    outs, s_ref = rest[:n], rest[n]
+    members, forks, carried, _ = q_ref.shape
+    rows = carried - 2 * tokens
+    both = 128 // rows
     cap = kv_ref.shape[1]
     lanes = n * rows
-    g = pl.program_id(0)
     me = info[0]
     unit = math.log2(math.e) / math.sqrt(HEAD_DIM)
 
     lane = lax.broadcasted_iota(jnp.int32, (1, lanes), 1)
+    blocks = [lax.rem(me + (off + members), members) for off in offsets]
     first = jnp.zeros((1, lanes), jnp.int32)
-    for b, off in enumerate(offsets):
-        here = lax.rem(me + (off + members), members) * tokens
-        first = jnp.where((lane >= b * rows) & (lane < (b + 1) * rows), here, first)
+    for b, block in enumerate(blocks):
+        first = jnp.where((lane >= b * rows) & (lane < (b + 1) * rows), block * tokens, first)
     q_token = first + lax.rem(lane, tokens)
     u = lax.broadcasted_iota(jnp.int32, (2 * tokens, lanes), 0)
     seen = (u < tokens) & (me * tokens + u <= q_token)
 
-    def one(j, steps):
-        q = jnp.concatenate([r[j] for r in q_refs], axis=0)
-        fresh = fresh_ref[j]
-        live = info[1 + g * forks + j]
-        s_new = lax.dot_general(fresh, q, NT, preferred_element_type=jnp.float32)
-        s_new = jnp.where(seen, s_new, -jnp.inf)
-        top = jnp.max(s_new, axis=0, keepdims=True)
+    def several(g, steps):
+        fork = [g * both + j for j in range(both)]
+        live = [info[1 + f] for f in fork]
+        q = [jnp.concatenate([q_ref[i, f, :rows] for i in blocks], axis=0) for f in fork]
+        fresh = [fresh_ref[f] for f in fork]
+        new, top = [], []
+        for j in range(both):
+            s = lax.dot_general(fresh[j], q[j], NT, preferred_element_type=jnp.float32)
+            new.append(jnp.where(seen, s, -jnp.inf))
+            top.append(jnp.max(new[j], axis=0, keepdims=True))
         for c in range(steps):
-            at = c * STEP
-            s = lax.dot_general(
-                kv_ref[j, at : at + STEP, :HEAD_DIM], q, NT, preferred_element_type=jnp.float32
-            )
-            if c == steps - 1:
-                tail = jnp.where(at + BLOCK < live, s[BLOCK:], -jnp.inf)
-                s_ref[at : at + BLOCK] = s[:BLOCK]
-                s_ref[at + BLOCK : at + STEP] = tail
-                top = jnp.maximum(top, jnp.max(s[:BLOCK], axis=0, keepdims=True))
-                top = jnp.maximum(top, jnp.max(tail, axis=0, keepdims=True))
+            for j in range(both):
+                at = c * STEP
+                keys = kv_ref[fork[j], at : at + STEP, :HEAD_DIM]
+                s = lax.dot_general(keys, q[j], NT, preferred_element_type=jnp.float32)
+                for lo in range(0, STEP, BLOCK):
+                    part = jnp.where(at + lo < live[j], s[lo : lo + BLOCK], -jnp.inf)
+                    s_ref[j, at + lo : at + lo + BLOCK] = part
+                    top[j] = jnp.maximum(top[j], jnp.max(part, axis=0, keepdims=True))
+        top = [jnp.maximum(t, NEVER) for t in top]
+        total, numer = [], []
+        for j in range(both):
+            w = jnp.exp2((new[j] - top[j]) * unit)
+            total.append(jnp.sum(w, axis=0, keepdims=True))
+            w = jnp.concatenate([w[tokens:], w[:tokens]], axis=0).astype(jnp.bfloat16)
+            numer.append(lax.dot_general(fresh[j], w, TN, preferred_element_type=jnp.float32))
+        for c in range(steps):
+            for j in range(both):
+                at = c * STEP
+                w = jnp.exp2((s_ref[j, at : at + STEP] - top[j]) * unit)
+                total[j] = total[j] + jnp.sum(w, axis=0, keepdims=True)
+                values = kv_ref[fork[j], at : at + STEP, HEAD_DIM:]
+                numer[j] = numer[j] + lax.dot_general(
+                    values, w.astype(jnp.bfloat16), TN, preferred_element_type=jnp.float32
+                )
+        here = pl.ds(pl.multiple_of(g * 128, 128), 128)
+        for b in range(n):
+            mine = slice(b * rows, (b + 1) * rows)
+            t, l, o = (jnp.concatenate([x[:, mine] for x in xs], axis=1) for xs in (top, total, numer))
+            if codes[b]:
+                code_part(t * unit, l, o, outs[b], here)
             else:
-                s_ref[at : at + STEP] = s
-                top = jnp.maximum(top, jnp.max(s, axis=0, keepdims=True))
-        top = jnp.maximum(top, NEVER)
-        w = jnp.exp2((s_new - top) * unit)
-        total = jnp.sum(w, axis=0, keepdims=True)
-        w = jnp.concatenate([w[tokens:], w[:tokens]], axis=0)
-        numer = lax.dot_general(fresh, w.astype(jnp.bfloat16), TN, preferred_element_type=jnp.float32)
-        for c in range(steps):
-            at = c * STEP
-            w = jnp.exp2((s_ref[at : at + STEP] - top) * unit)
-            total = total + jnp.sum(w, axis=0, keepdims=True)
-            numer = numer + lax.dot_general(
-                kv_ref[j, at : at + STEP, HEAD_DIM:],
-                w.astype(jnp.bfloat16),
-                TN,
-                preferred_element_type=jnp.float32,
-            )
-        o_ref[j, :HEAD_DIM] = numer
-        row = lax.broadcasted_iota(jnp.int32, (META, lanes), 0)
-        o_ref[j, HEAD_DIM:] = jnp.where(row == 0, top * unit, total)
-
-    def fork(j, carry):
-        live = info[1 + g * forks + j]
+                outs[b][:HEAD_DIM, here] = o
+                outs[b][HEAD_DIM:, here] = meta_rows(META, t * unit, l, l)
+
+    def group(g, carry):
+        most = functools.reduce(jnp.maximum, [info[1 + g * both + j] for j in range(both)])
         for steps in range(cap // STEP + 1):
-            pl.when((live > (steps - 1) * STEP) & (live <= steps * STEP))(
-                functools.partial(one, j, steps)
+            pl.when((most > (steps - 1) * STEP) & (most <= steps * STEP))(
+                functools.partial(several, g, steps)
             )
         return carry
 
-    lax.fori_loop(0, forks, fork, 0)
-    for b in range(n):
-        o = jnp.concatenate([o_ref[j, :, b * rows : (b + 1) * rows] for j in range(forks)], axis=1)
-        if codes[b]:
-            code_part(o[HEAD_DIM : HEAD_DIM + 1], o[HEAD_DIM + 1 : HEAD_DIM + 2], o[:HEAD_DIM], out_refs[b], slice(None))
-        else:
-            out_refs[b][...] = o
+    lax.fori_loop(0, forks // both, group, 0)
 
 
 def parts_of(blocks_q, offsets, codes, info, cache, fresh, tokens):
     n = len(offsets)
     members, forks, carried, _ = blocks_q.shape
     rows = carried - 2 * tokens
-    both = 128 // rows
     cap, width = cache.shape[1:]
     keys = cap + tokens
     lanes = n * rows
     heights = [HEAD_DIM + (CODE if c else META) for c in codes]
+    vmem = pl.BlockSpec(memory_space=pltpu.VMEM)
     return pl.pallas_call(
-        functools.partial(part_kernel, offsets, codes, members, tokens, rows),
-        grid_spec=pltpu.PrefetchScalarGridSpec(
-            num_scalar_prefetch=1,
-            grid=(forks // both,),
-            in_specs=[
-                pl.BlockSpec(
-                    (None, both, rows, HEAD_DIM),
-                    lambda g, i, off=off: (lax.rem(i[0] + (off + members), members), g, 0, 0),
-                )
-                for off in offsets
-            ]
-            + [
-                pl.BlockSpec((both, 2 * tokens, HEAD_DIM), lambda g, i: (g, 0, 0)),
-                pl.BlockSpec((both, cap, width), lambda g, i: (g, 0, 0)),
-            ],
-            out_specs=[pl.BlockSpec((h, both * rows), lambda g, i: (0, g)) for h in heights],
-            scratch_shapes=[
-                pltpu.VMEM((cap, lanes), jnp.float32),
-                pltpu.VMEM((both, HEAD_DIM + META, lanes), jnp.float32),
-            ],
-        ),
+        functools.partial(part_kernel, offsets, codes, tokens),
+        in_specs=[pl.BlockSpec(memory_space=pltpu.SMEM), vmem, vmem, vmem],
+        out_specs=[vmem] * n,
+        scratch_shapes=[pltpu.VMEM((128 // rows, cap, lanes), jnp.float32)],
         out_shape=[
             jax.ShapeDtypeStruct((h, forks * rows), jnp.int16 if c else jnp.float32)
             for h, c in zip(heights, codes)
         ],
-        compiler_params=pltpu.CompilerParams(vmem_limit_bytes=8 * 2**20),
+        compiler_params=pltpu.CompilerParams(vmem_limit_bytes=16 * 2**20),
         cost_estimate=pl.CostEstimate(
             flops=4 * forks * lanes * keys * HEAD_DIM,
             transcendentals=forks * lanes * keys,
             bytes_accessed=2 * forks * keys * width,
         ),
         name="parts",
-    )(info, *[blocks_q] * n, fresh, cache)
+    )(info, blocks_q, fresh, cache)
 
 
 def merge_kernel(*refs):
@@ -312,7 +294,7 @@
     order = []
     for k in range(half, 0, -1):
         order += [-k, k - 1]
-    return [tuple(order[:2])] + [tuple(order[i : i + 4]) for i in range(2, len(order), 4)]
+    return [tuple(order[:2]), tuple(order[2:])]
 
 
 def solution(mesh):

time: 182 us -> 170 us (0.934)
  Pallas kernels: 30.3 us -> 17.1 us
  starting transfers between devices: 50.7 us -> 53.8 us
  waiting for transfers between devices: 7.76 us -> 5.02 us
    pallas_call x5 -> x2, Pallas kernels: 26 us -> 12.8 us  [parts_of(): pl.pallas_call(functools.partial(part_kernel, offsets, codes, tokens), in...]
    ppermute x15, starting transfers between devices: 50.7 us -> 53.8 us  [passed_along(): return lax.ppermute(x, 'inst', [(i, (i + by) % size) for i in range(size)])]
    ppermute x15, waiting for transfers between devices: 7.76 us -> 5.02 us  [passed_along(): return lax.ppermute(x, 'inst', [(i, (i + by) % size) for i in range(size)])]
  transfers between devices with their start and end apart: 15 -> 15, of which waited for: 5 -> 7; matrix products, arithmetic and copies ran while one was open for 0% -> 0% of each run, Pallas kernels for 13% -> 7%
where the time goes in v4:
time: 170 us; the launch traced here: 168 us
  blocking collectives  87.7 us (52%)
  starting transfers between devices  53.8 us (32%)
  Pallas kernels  17.1 us (10%)
  waiting for transfers between devices  5.02 us (3%)
  other arithmetic  2.41 us (1%)
    all_gather x1, blocking collectives, body(): q = lax.all_gather(sent.astype(jnp.float16), 'inst', axis=0)  87.7 us
    ppermute x15, starting transfers between devices, passed_along(): return lax.ppermute(x, 'inst', [(i, (i + by) % size) for i in range(size)])  53.8 us
    pallas_call x2, Pallas kernels, parts_of(): pl.pallas_call(functools.partial(part_kernel, offsets, codes, tokens), in...  12.8 us
    ppermute x15, waiting for transfers between devices, passed_along(): return lax.ppermute(x, 'inst', [(i, (i + by) % size) for i in range(size)])  5.02 us
  transfers between devices with their start and end apart: 15, of which 7 were waited for; matrix products, arithmetic and copies ran while one was open for 0% of the time, Pallas kernels for 7%

profile of v4, /device:TPU:80, one launch (start us, length us, event | category | flops | bytes accessed | tf_op | source)
XLA Modules:
  0.0 168.1 jit_solution(8528526947264073915)
XLA Ops:
  0.6 1.0 multiply_convert_fusion.1
  1.6 87.7 %all-gather.1 = f16[16,8,80,128]{3,2,1,0:T(8,128)(2,1)S(1)} all-gather(f16[1,8,80,128]{3,2,1,0:T(8,128)(2,1)S(1)} %multiply_convert_fusion.1), channel_id=1, replica_groups=mesh['groups'=2,'inst'=16,'tp'=8,'rep'=2] {'inst'}, dimensions={0}, use_global_device_ids=true | all-gather | bytes 2785280 | tf_op jit(solution)/shard_map/all_gather | solution.py:270
  89.3 0.0 copy-start.4
  89.3 0.0 copy-start.5
  89.3 0.0 copy-start
  89.3 0.0 copy-start.1
  89.3 0.7 multiply_convert_fusion.q_ref.rows_ref
  90.1 0.0 copy-done.4
  90.1 0.0 copy-done.5
  90.1 0.1 pad_add_fusion.info
  90.2 1.1 copy-done
  91.3 0.0 copy-done.1
  91.3 3.5 %parts.3 = (s16[136,512]{1,0:T(8,128)(2,1)S(1)}, s16[136,512]{1,0:T(8,128)(2,1)S(1)}) custom-call(s32[9]{0:T(128)S(1)} %pad_add_fusion.info, bf16[16,8,80,128]{3,2,1,0:T(8,128)(2,1)S(1)} %multiply_convert_fusion.q_ref.rows_ref, bf16[8,16,128]{2,1,0:T(8,128)(2,1)S(1)} %bitcast.23, bf16[8,768,256]{2,1,0:T(8,128)(2,1)S(1)} %copy-done), custom_call_target="tpu_custom_call" | custom-call | flops 406847488 | bytes 3178496 | tf_op jit(solution)/shard_map/parts/pallas_call | solution.py:161
  94.8 2.0 %collective-permute-start = (s16[136,512]{1,0:T(8,128)(2,1)S(1)}, s16[136,512]{1,0:T(8,128)(2,1)S(1)}, u32[]{:S(2)}, u32[]{:S(2)}) collective-permute-start(s16[136,512]{1,0:T(8,128)(2,1)S(1)} %get-tuple-element.19), channel_id=1, source_target_pairs={{0,16},{16,32},{32,48},{48,64},{64,80},{80,96},{96,112},{112,128},... | collective-permute-start | bytes 417800 | tf_op jit(solution)/shard_map/ppermute | solution.py:25
  96.8 5.2 %collective-permute-start.7 = (s16[136,512]{1,0:T(8,128)(2,1)S(1)}, s16[136,512]{1,0:T(8,128)(2,1)S(1)}, u32[]{:S(2)}, u32[]{:S(2)}) collective-permute-start(s16[136,512]{1,0:T(8,128)(2,1)S(1)} %get-tuple-element.26), channel_id=1, source_target_pairs={{0,240},{16,0},{32,16},{48,32},{64,48},{80,64},{96,80},{112,96},{1... | collective-permute-start | bytes 417800 | tf_op jit(solution)/shard_map/ppermute | solution.py:25
  101.9 9.3 %parts.2 = (f32[136,512]{1,0:T(8,128)S(1)}, f32[136,512]{1,0:T(8,128)S(1)}, f32[136,512]{1,0:T(8,128)S(1)}, f32[136,512]{1,0:T(8,128)S(1)}, f32[136,512]{1,0:T(8...) custom-call(s32[9]{0:T(128)S(1)} %pad_add_fusion.info, ...), custom_call_target="tpu_custom_call" | custom-call | flops 2847932416 | bytes 3178496 | tf_op jit(solution)/shard_map/parts/pallas_call | solution.py:161
  111.2 0.0 copy-start.2
  111.2 0.0 copy-start.3
  111.2 0.0 collective-permute-done.7.refs_0_
  111.2 0.2 merge.19
  111.4 2.0 %collective-permute-start.8 = (s16[136,512]{1,0:T(8,128)(2,1)S(1)}, s16[136,512]{1,0:T(8,128)(2,1)S(1)}, u32[]{:S(2)}, u32[]{:S(2)}) collective-permute-start(s16[136,512]{1,0:T(8,128)(2,1)S(1)} %merge.19), channel_id=1, source_target_pairs={{0,240},{16,0},{32,16},{48,32},{64,48},{80,64},{96,80},{112,96},{1... | collective-permute-start | bytes 417800 | tf_op jit(solution)/shard_map/ppermute | solution.py:25
  113.4 0.0 collective-permute-done.refs_0_
  113.4 0.2 merge.13
  113.6 4.0 %collective-permute-start.1 = (s16[136,512]{1,0:T(8,128)(2,1)S(1)}, s16[136,512]{1,0:T(8,128)(2,1)S(1)}, u32[]{:S(2)}, u32[]{:S(2)}) collective-permute-start(s16[136,512]{1,0:T(8,128)(2,1)S(1)} %merge.13), channel_id=1, source_target_pairs={{0,16},{16,32},{32,48},{48,64},{64,80},{80,96},{96,112},{112,128},... | collective-permute-start | bytes 417800 | tf_op jit(solution)/shard_map/ppermute | solution.py:25
  117.5 0.9 collective-permute-done.8.refs_0_
  118.4 0.2 merge.20
  118.6 3.7 %collective-permute-start.9 = (s16[136,512]{1,0:T(8,128)(2,1)S(1)}, s16[136,512]{1,0:T(8,128)(2,1)S(1)}, u32[]{:S(2)}, u32[]{:S(2)}) collective-permute-start(s16[136,512]{1,0:T(8,128)(2,1)S(1)} %merge.20), channel_id=1, source_target_pairs={{0,240},{16,0},{32,16},{48,32},{64,48},{80,64},{96,80},{112,96},{1... | collective-permute-start | bytes 417800 | tf_op jit(solution)/shard_map/ppermute | solution.py:25
  122.3 0.0 collective-permute-done.1.refs_0_
  122.3 0.2 merge.14
  122.5 2.2 %collective-permute-start.2 = (s16[136,512]{1,0:T(8,128)(2,1)S(1)}, s16[136,512]{1,0:T(8,128)(2,1)S(1)}, u32[]{:S(2)}, u32[]{:S(2)}) collective-permute-start(s16[136,512]{1,0:T(8,128)(2,1)S(1)} %merge.14), channel_id=1, source_target_pairs={{0,16},{16,32},{32,48},{48,64},{64,80},{80,96},{96,112},{112,128},... | collective-permute-start | bytes 417800 | tf_op jit(solution)/shard_map/ppermute | solution.py:25
  124.7 0.9 collective-permute-done.9.refs_0_
  125.6 0.2 merge.21
  125.7 5.0 %collective-permute-start.10 = (s16[136,512]{1,0:T(8,128)(2,1)S(1)}, s16[136,512]{1,0:T(8,128)(2,1)S(1)}, u32[]{:S(2)}, u32[]{:S(2)}) collective-permute-start(s16[136,512]{1,0:T(8,128)(2,1)S(1)} %merge.21), channel_id=1, source_target_pairs={{0,240},{16,0},{32,16},{48,32},{64,48},{80,64},{96,80},{112,96},{1... | collective-permute-start | bytes 417800 | tf_op jit(solution)/shard_map/ppermute | solution.py:25
  130.7 0.0 collective-permute-done.2.refs_0_
  130.7 0.2 merge.15
  130.9 2.0 %collective-permute-start.3 = (s16[136,512]{1,0:T(8,128)(2,1)S(1)}, s16[136,512]{1,0:T(8,128)(2,1)S(1)}, u32[]{:S(2)}, u32[]{:S(2)}) collective-permute-start(s16[136,512]{1,0:T(8,128)(2,1)S(1)} %merge.15), channel_id=1, source_target_pairs={{0,16},{16,32},{32,48},{48,64},{64,80},{80,96},{96,112},{112,128},... | collective-permute-start | bytes 417800 | tf_op jit(solution)/shard_map/ppermute | solution.py:25
  132.8 0.4 collective-permute-done.10.refs_0_
  133.3 0.2 merge.22
  133.4 5.6 %collective-permute-start.11 = (s16[136,512]{1,0:T(8,128)(2,1)S(1)}, s16[136,512]{1,0:T(8,128)(2,1)S(1)}, u32[]{:S(2)}, u32[]{:S(2)}) collective-permute-start(s16[136,512]{1,0:T(8,128)(2,1)S(1)} %merge.22), channel_id=1, source_target_pairs={{0,240},{16,0},{32,16},{48,32},{64,48},{80,64},{96,80},{112,96},{1... | collective-permute-start | bytes 417800 | tf_op jit(solution)/shard_map/ppermute | solution.py:25
  139.1 0.0 collective-permute-done.3.refs_0_
  139.1 0.2 merge.16
  139.2 2.0 %collective-permute-start.4 = (s16[136,512]{1,0:T(8,128)(2,1)S(1)}, s16[136,512]{1,0:T(8,128)(2,1)S(1)}, u32[]{:S(2)}, u32[]{:S(2)}) collective-permute-start(s16[136,512]{1,0:T(8,128)(2,1)S(1)} %merge.16), channel_id=1, source_target_pairs={{0,16},{16,32},{32,48},{48,64},{64,80},{80,96},{96,112},{112,128},... | collective-permute-start | bytes 417800 | tf_op jit(solution)/shard_map/ppermute | solution.py:25
  141.2 0.4 collective-permute-done.11.refs_0_
  141.6 0.2 merge.23
  141.8 5.6 %collective-permute-start.12 = (s16[136,512]{1,0:T(8,128)(2,1)S(1)}, s16[136,512]{1,0:T(8,128)(2,1)S(1)}, u32[]{:S(2)}, u32[]{:S(2)}) collective-permute-start(s16[136,512]{1,0:T(8,128)(2,1)S(1)} %merge.23), channel_id=1, source_target_pairs={{0,240},{16,0},{32,16},{48,32},{64,48},{80,64},{96,80},{112,96},{1... | collective-permute-start | bytes 417800 | tf_op jit(solution)/shard_map/ppermute | solution.py:25
  147.4 0.0 collective-permute-done.4.refs_0_
  147.4 0.2 merge.17
  147.6 2.0 %collective-permute-start.5 = (s16[136,512]{1,0:T(8,128)(2,1)S(1)}, s16[136,512]{1,0:T(8,128)(2,1)S(1)}, u32[]{:S(2)}, u32[]{:S(2)}) collective-permute-start(s16[136,512]{1,0:T(8,128)(2,1)S(1)} %merge.17), channel_id=1, source_target_pairs={{0,16},{16,32},{32,48},{48,64},{64,80},{80,96},{96,112},{112,128},... | collective-permute-start | bytes 417800 | tf_op jit(solution)/shard_map/ppermute | solution.py:25
  149.6 0.4 collective-permute-done.12.refs_0_
  150.0 0.2 merge.24
  150.2 5.6 %collective-permute-start.13 = (s16[136,512]{1,0:T(8,128)(2,1)S(1)}, s16[136,512]{1,0:T(8,128)(2,1)S(1)}, u32[]{:S(2)}, u32[]{:S(2)}) collective-permute-start(s16[136,512]{1,0:T(8,128)(2,1)S(1)} %merge.24), channel_id=1, source_target_pairs={{0,240},{16,0},{32,16},{48,32},{64,48},{80,64},{96,80},{112,96},{1... | collective-permute-start | bytes 417800 | tf_op jit(solution)/shard_map/ppermute | solution.py:25
  155.8 0.0 copy-done.2
  155.8 0.0 copy-done.3
  155.8 0.7 own_kv.1
  156.5 0.0 collective-permute-done.5.refs_0_
  156.5 0.2 merge.18
  156.7 2.0 %collective-permute-start.6 = (s16[136,512]{1,0:T(8,128)(2,1)S(1)}, s16[136,512]{1,0:T(8,128)(2,1)S(1)}, u32[]{:S(2)}, u32[]{:S(2)}) collective-permute-start(s16[136,512]{1,0:T(8,128)(2,1)S(1)} %merge.18), channel_id=1, source_target_pairs={{0,16},{16,32},{32,48},{48,64},{64,80},{80,96},{96,112},{112,128},... | collective-permute-start | bytes 417800 | tf_op jit(solution)/shard_map/ppermute | solution.py:25
  158.7 0.0 collective-permute-done.13.refs_0_
  158.7 0.2 merge.25
  158.9 5.3 %collective-permute-start.14 = (s16[136,512]{1,0:T(8,128)(2,1)S(1)}, s16[136,512]{1,0:T(8,128)(2,1)S(1)}, u32[]{:S(2)}, u32[]{:S(2)}) collective-permute-start(s16[136,512]{1,0:T(8,128)(2,1)S(1)} %merge.25), channel_id=1, source_target_pairs={{0,240},{16,0},{32,16},{48,32},{64,48},{80,64},{96,80},{112,96},{1... | collective-permute-start | bytes 417800 | tf_op jit(solution)/shard_map/ppermute | solution.py:25
  164.1 0.6 convert_bitcast_fusion
  164.8 0.1 collective-permute-done.6.right
  164.9 1.8 %collective-permute-done.14.left = s16[136,512]{1,0:T(8,128)(2,1)S(1)} collective-permute-done((s16[136,512]{1,0:T(8,128)(2,1)S(1)}, s16[136,512]{1,0:T(8,128)(2,1)S(1)}, u32[]{:S(2)}, u32[]{:S(2)}) %collective-permute-start.14) | collective-permute-done | bytes 139296 | tf_op jit(solution)/shard_map/ppermute | solution.py:25
  166.7 1.4 finish.1
  (1 shorter events, 0.0 us)
Async XLA Ops:
  89.3 0.7 copy-start.4
  89.3 0.7 copy-start.5
  89.3 1.9 %copy-start = (bf16[8,768,256]{2,1,0:T(8,128)(2,1)S(1)}, bf16[8,768,256]{2,1,0:T(8,128)(2,1)}, u32[]{:S(2)}) copy-start(bf16[8,768,256]{2,1,0:T(8,128)(2,1)} %kv_ref.3) | copy-start | bytes 9437188
  89.3 1.9 %copy-start.1 = (bf16[8,8,256]{2,1,0:T(8,128)(2,1)S(1)}, bf16[8,8,256]{2,1,0:T(8,128)(2,1)}, u32[]{:S(2)}) copy-start(bf16[8,8,256]{2,1,0:T(8,128)(2,1)} %param.8) | copy-start | bytes 98308
  94.8 18.6 %collective-permute-start = (s16[136,512]{1,0:T(8,128)(2,1)S(1)}, s16[136,512]{1,0:T(8,128)(2,1)S(1)}, u32[]{:S(2)}, u32[]{:S(2)}) collective-permute-start(s16[136,512]{1,0:T(8,128)(2,1)S(1)} %get-tuple-element.19), channel_id=1, source_target_pairs={{0,16},{16,32},{32,48},{48,64},{64,80},{80,96},{96,112},{112,128},... | collective-permute-start | bytes 417800 | tf_op jit(solution)/shard_map/ppermute | solution.py:25
  96.8 14.5 %collective-permute-start.7 = (s16[136,512]{1,0:T(8,128)(2,1)S(1)}, s16[136,512]{1,0:T(8,128)(2,1)S(1)}, u32[]{:S(2)}, u32[]{:S(2)}) collective-permute-start(s16[136,512]{1,0:T(8,128)(2,1)S(1)} %get-tuple-element.26), channel_id=1, source_target_pairs={{0,240},{16,0},{32,16},{48,32},{64,48},{80,64},{96,80},{112,96},{1... | collective-permute-start | bytes 417800 | tf_op jit(solution)/shard_map/ppermute | solution.py:25
  111.2 44.6 %copy-start.2 = (s32[8]{0:T(128)S(1)}, s32[8]{0:T(128)}, u32[]{:S(2)}) copy-start(s32[8]{0:T(128)} %span.3) | copy-start | bytes 100
  111.2 44.6 %copy-start.3 = (s32[8]{0:T(128)S(1)}, s32[8]{0:T(128)}, u32[]{:S(2)}) copy-start(s32[8]{0:T(128)} %owner.1) | copy-start | bytes 100
  111.4 7.0 %collective-permute-start.8 = (s16[136,512]{1,0:T(8,128)(2,1)S(1)}, s16[136,512]{1,0:T(8,128)(2,1)S(1)}, u32[]{:S(2)}, u32[]{:S(2)}) collective-permute-start(s16[136,512]{1,0:T(8,128)(2,1)S(1)} %merge.19), channel_id=1, source_target_pairs={{0,240},{16,0},{32,16},{48,32},{64,48},{80,64},{96,80},{112,96},{1... | collective-permute-start | bytes 417800 | tf_op jit(solution)/shard_map/ppermute | solution.py:25
  113.6 8.8 %collective-permute-start.1 = (s16[136,512]{1,0:T(8,128)(2,1)S(1)}, s16[136,512]{1,0:T(8,128)(2,1)S(1)}, u32[]{:S(2)}, u32[]{:S(2)}) collective-permute-start(s16[136,512]{1,0:T(8,128)(2,1)S(1)} %merge.13), channel_id=1, source_target_pairs={{0,16},{16,32},{32,48},{48,64},{64,80},{80,96},{96,112},{112,128},... | collective-permute-start | bytes 417800 | tf_op jit(solution)/shard_map/ppermute | solution.py:25
  118.6 7.0 %collective-permute-start.9 = (s16[136,512]{1,0:T(8,128)(2,1)S(1)}, s16[136,512]{1,0:T(8,128)(2,1)S(1)}, u32[]{:S(2)}, u32[]{:S(2)}) collective-permute-start(s16[136,512]{1,0:T(8,128)(2,1)S(1)} %merge.20), channel_id=1, source_target_pairs={{0,240},{16,0},{32,16},{48,32},{64,48},{80,64},{96,80},{112,96},{1... | collective-permute-start | bytes 417800 | tf_op jit(solution)/shard_map/ppermute | solution.py:25
  122.5 8.2 %collective-permute-start.2 = (s16[136,512]{1,0:T(8,128)(2,1)S(1)}, s16[136,512]{1,0:T(8,128)(2,1)S(1)}, u32[]{:S(2)}, u32[]{:S(2)}) collective-permute-start(s16[136,512]{1,0:T(8,128)(2,1)S(1)} %merge.14), channel_id=1, source_target_pairs={{0,16},{16,32},{32,48},{48,64},{64,80},{80,96},{96,112},{112,128},... | collective-permute-start | bytes 417800 | tf_op jit(solution)/shard_map/ppermute | solution.py:25
  125.7 7.5 %collective-permute-start.10 = (s16[136,512]{1,0:T(8,128)(2,1)S(1)}, s16[136,512]{1,0:T(8,128)(2,1)S(1)}, u32[]{:S(2)}, u32[]{:S(2)}) collective-permute-start(s16[136,512]{1,0:T(8,128)(2,1)S(1)} %merge.21), channel_id=1, source_target_pairs={{0,240},{16,0},{32,16},{48,32},{64,48},{80,64},{96,80},{112,96},{1... | collective-permute-start | bytes 417800 | tf_op jit(solution)/shard_map/ppermute | solution.py:25
  130.9 8.2 %collective-permute-start.3 = (s16[136,512]{1,0:T(8,128)(2,1)S(1)}, s16[136,512]{1,0:T(8,128)(2,1)S(1)}, u32[]{:S(2)}, u32[]{:S(2)}) collective-permute-start(s16[136,512]{1,0:T(8,128)(2,1)S(1)} %merge.15), channel_id=1, source_target_pairs={{0,16},{16,32},{32,48},{48,64},{64,80},{80,96},{96,112},{112,128},... | collective-permute-start | bytes 417800 | tf_op jit(solution)/shard_map/ppermute | solution.py:25
  133.4 8.2 %collective-permute-start.11 = (s16[136,512]{1,0:T(8,128)(2,1)S(1)}, s16[136,512]{1,0:T(8,128)(2,1)S(1)}, u32[]{:S(2)}, u32[]{:S(2)}) collective-permute-start(s16[136,512]{1,0:T(8,128)(2,1)S(1)} %merge.22), channel_id=1, source_target_pairs={{0,240},{16,0},{32,16},{48,32},{64,48},{80,64},{96,80},{112,96},{1... | collective-permute-start | bytes 417800 | tf_op jit(solution)/shard_map/ppermute | solution.py:25
  139.2 8.2 %collective-permute-start.4 = (s16[136,512]{1,0:T(8,128)(2,1)S(1)}, s16[136,512]{1,0:T(8,128)(2,1)S(1)}, u32[]{:S(2)}, u32[]{:S(2)}) collective-permute-start(s16[136,512]{1,0:T(8,128)(2,1)S(1)} %merge.16), channel_id=1, source_target_pairs={{0,16},{16,32},{32,48},{48,64},{64,80},{80,96},{96,112},{112,128},... | collective-permute-start | bytes 417800 | tf_op jit(solution)/shard_map/ppermute | solution.py:25
  141.8 8.2 %collective-permute-start.12 = (s16[136,512]{1,0:T(8,128)(2,1)S(1)}, s16[136,512]{1,0:T(8,128)(2,1)S(1)}, u32[]{:S(2)}, u32[]{:S(2)}) collective-permute-start(s16[136,512]{1,0:T(8,128)(2,1)S(1)} %merge.23), channel_id=1, source_target_pairs={{0,240},{16,0},{32,16},{48,32},{64,48},{80,64},{96,80},{112,96},{1... | collective-permute-start | bytes 417800 | tf_op jit(solution)/shard_map/ppermute | solution.py:25
  147.6 8.9 %collective-permute-start.5 = (s16[136,512]{1,0:T(8,128)(2,1)S(1)}, s16[136,512]{1,0:T(8,128)(2,1)S(1)}, u32[]{:S(2)}, u32[]{:S(2)}) collective-permute-start(s16[136,512]{1,0:T(8,128)(2,1)S(1)} %merge.17), channel_id=1, source_target_pairs={{0,16},{16,32},{32,48},{48,64},{64,80},{80,96},{96,112},{112,128},... | collective-permute-start | bytes 417800 | tf_op jit(solution)/shard_map/ppermute | solution.py:25
  150.2 8.5 %collective-permute-start.13 = (s16[136,512]{1,0:T(8,128)(2,1)S(1)}, s16[136,512]{1,0:T(8,128)(2,1)S(1)}, u32[]{:S(2)}, u32[]{:S(2)}) collective-permute-start(s16[136,512]{1,0:T(8,128)(2,1)S(1)} %merge.24), channel_id=1, source_target_pairs={{0,240},{16,0},{32,16},{48,32},{64,48},{80,64},{96,80},{112,96},{1... | collective-permute-start | bytes 417800 | tf_op jit(solution)/shard_map/ppermute | solution.py:25
  156.7 8.2 %collective-permute-start.6 = (s16[136,512]{1,0:T(8,128)(2,1)S(1)}, s16[136,512]{1,0:T(8,128)(2,1)S(1)}, u32[]{:S(2)}, u32[]{:S(2)}) collective-permute-start(s16[136,512]{1,0:T(8,128)(2,1)S(1)} %merge.18), channel_id=1, source_target_pairs={{0,16},{16,32},{32,48},{48,64},{64,80},{80,96},{96,112},{112,128},... | collective-permute-start | bytes 417800 | tf_op jit(solution)/shard_map/ppermute | solution.py:25
  158.9 7.9 %collective-permute-start.14 = (s16[136,512]{1,0:T(8,128)(2,1)S(1)}, s16[136,512]{1,0:T(8,128)(2,1)S(1)}, u32[]{:S(2)}, u32[]{:S(2)}) collective-permute-start(s16[136,512]{1,0:T(8,128)(2,1)S(1)} %merge.25), channel_id=1, source_target_pairs={{0,240},{16,0},{32,16},{48,32},{64,48},{80,64},{96,80},{112,96},{1... | collective-permute-start | bytes 417800 | tf_op jit(solution)/shard_map/ppermute | solution.py:25

commit v5 on v4

--- a/solution.py
+++ b/solution.py
@@ -294,7 +294,7 @@
     order = []
     for k in range(half, 0, -1):
         order += [-k, k - 1]
-    return [tuple(order[:2]), tuple(order[2:])]
+    return [tuple(order)]
 
 
 def solution(mesh):

time: 170 us -> 170 us (level)
  Pallas kernels: 17.1 us -> 13.2 us
    pallas_call x2 -> x1, Pallas kernels: 12.8 us -> 8.88 us  [parts_of(): pl.pallas_call(functools.partial(part_kernel, offsets, codes, tokens), in...]
  transfers between devices with their start and end apart: 15 -> 15, of which waited for: 7 -> 12; matrix products, arithmetic and copies ran while one was open for 0% -> 0% of each run, Pallas kernels for 7% -> 2%
where the time goes in v5:
time: 170 us; the launch traced here: 167 us
  blocking collectives  87.7 us (52%)
  starting transfers between devices  54.9 us (32%)
  Pallas kernels  13.2 us (8%)
  waiting for transfers between devices  6.7 us (4%)
  other arithmetic  2.41 us (1%)
    all_gather x1, blocking collectives, body(): q = lax.all_gather(sent.astype(jnp.float16), 'inst', axis=0)  87.7 us
    ppermute x15, starting transfers between devices, passed_along(): return lax.ppermute(x, 'inst', [(i, (i + by) % size) for i in range(size)])  54.9 us
    pallas_call x1, Pallas kernels, parts_of(): pl.pallas_call(functools.partial(part_kernel, offsets, codes, tokens), in...  8.88 us
    ppermute x15, waiting for transfers between devices, passed_along(): return lax.ppermute(x, 'inst', [(i, (i + by) % size) for i in range(size)])  6.7 us
  transfers between devices with their start and end apart: 15, of which 12 were waited for; matrix products, arithmetic and copies ran while one was open for 0% of the time, Pallas kernels for 2%

profile of v5, /device:TPU:80, one launch (start us, length us, event | category | flops | bytes accessed | tf_op | source)
XLA Modules:
  0.0 167.0 jit_solution(6221822144269326397)
XLA Ops:
  0.6 1.0 multiply_convert_fusion.1
  1.6 87.7 %all-gather.1 = f16[16,8,80,128]{3,2,1,0:T(8,128)(2,1)S(1)} all-gather(f16[1,8,80,128]{3,2,1,0:T(8,128)(2,1)S(1)} %multiply_convert_fusion.1), channel_id=1, replica_groups=mesh['groups'=2,'inst'=16,'tp'=8,'rep'=2] {'inst'}, dimensions={0}, use_global_device_ids=true | all-gather | bytes 2785280 | tf_op jit(solution)/shard_map/all_gather | solution.py:270
  89.3 0.0 copy-start.4
  89.3 0.0 copy-start.5
  89.3 0.0 copy-start
  89.3 0.0 copy-start.3
  89.3 0.7 multiply_convert_fusion.q_ref.rows_ref
  90.1 0.0 copy-done.4
  90.1 0.0 copy-done.5
  90.1 0.1 pad_add_fusion.info
  90.2 0.0 copy-done
  90.2 1.1 copy-done.3
  91.3 8.9 %parts.1 = (s16[136,512]{1,0:T(8,128)(2,1)S(1)}, s16[136,512]{1,0:T(8,128)(2,1)S(1)}, f32[136,512]{1,0:T(8,128)S(1)}, f32[136,512]{1,0:T(8,128)S(1)}, f32[136,51...) custom-call(s32[9]{0:T(128)S(1)} %pad_add_fusion.info, ...), custom_call_target="tpu_custom_call" | custom-call | flops 3254779904 | bytes 3178496 | tf_op jit(solution)/shard_map/parts/pallas_call | solution.py:161
  100.2 0.0 copy-start.1
  100.2 0.0 copy-start.2
  100.2 2.4 %collective-permute-start.7 = (s16[136,512]{1,0:T(8,128)(2,1)S(1)}, s16[136,512]{1,0:T(8,128)(2,1)S(1)}, u32[]{:S(2)}, u32[]{:S(2)}) collective-permute-start(s16[136,512]{1,0:T(8,128)(2,1)S(1)} %get-tuple-element.26), channel_id=1, source_target_pairs={{0,240},{16,0},{32,16},{48,32},{64,48},{80,64},{96,80},{112,96},{1... | collective-permute-start | bytes 417800 | tf_op jit(solution)/shard_map/ppermute | solution.py:25
  102.6 3.5 %collective-permute-start = (s16[136,512]{1,0:T(8,128)(2,1)S(1)}, s16[136,512]{1,0:T(8,128)(2,1)S(1)}, u32[]{:S(2)}, u32[]{:S(2)}) collective-permute-start(s16[136,512]{1,0:T(8,128)(2,1)S(1)} %get-tuple-element.19), channel_id=1, source_target_pairs={{0,16},{16,32},{32,48},{48,64},{64,80},{80,96},{96,112},{112,128},... | collective-permute-start | bytes 417800 | tf_op jit(solution)/shard_map/ppermute | solution.py:25
  106.1 1.1 collective-permute-done.7.refs_0_
  107.2 0.2 merge.19
  107.3 3.6 %collective-permute-start.8 = (s16[136,512]{1,0:T(8,128)(2,1)S(1)}, s16[136,512]{1,0:T(8,128)(2,1)S(1)}, u32[]{:S(2)}, u32[]{:S(2)}) collective-permute-start(s16[136,512]{1,0:T(8,128)(2,1)S(1)} %merge.19), channel_id=1, source_target_pairs={{0,240},{16,0},{32,16},{48,32},{64,48},{80,64},{96,80},{112,96},{1... | collective-permute-start | bytes 417800 | tf_op jit(solution)/shard_map/ppermute | solution.py:25
  111.0 0.0 collective-permute-done.refs_0_
  111.0 0.2 merge.13
  111.2 2.3 %collective-permute-start.1 = (s16[136,512]{1,0:T(8,128)(2,1)S(1)}, s16[136,512]{1,0:T(8,128)(2,1)S(1)}, u32[]{:S(2)}, u32[]{:S(2)}) collective-permute-start(s16[136,512]{1,0:T(8,128)(2,1)S(1)} %merge.13), channel_id=1, source_target_pairs={{0,16},{16,32},{32,48},{48,64},{64,80},{80,96},{96,112},{112,128},... | collective-permute-start | bytes 417800 | tf_op jit(solution)/shard_map/ppermute | solution.py:25
  113.5 1.3 collective-permute-done.8.refs_0_
  114.8 0.2 merge.20
  114.9 5.6 %collective-permute-start.9 = (s16[136,512]{1,0:T(8,128)(2,1)S(1)}, s16[136,512]{1,0:T(8,128)(2,1)S(1)}, u32[]{:S(2)}, u32[]{:S(2)}) collective-permute-start(s16[136,512]{1,0:T(8,128)(2,1)S(1)} %merge.20), channel_id=1, source_target_pairs={{0,240},{16,0},{32,16},{48,32},{64,48},{80,64},{96,80},{112,96},{1... | collective-permute-start | bytes 417800 | tf_op jit(solution)/shard_map/ppermute | solution.py:25
  120.6 0.2 collective-permute-done.1.refs_0_
  120.8 0.2 merge.14
  121.0 2.0 %collective-permute-start.2 = (s16[136,512]{1,0:T(8,128)(2,1)S(1)}, s16[136,512]{1,0:T(8,128)(2,1)S(1)}, u32[]{:S(2)}, u32[]{:S(2)}) collective-permute-start(s16[136,512]{1,0:T(8,128)(2,1)S(1)} %merge.14), channel_id=1, source_target_pairs={{0,16},{16,32},{32,48},{48,64},{64,80},{80,96},{96,112},{112,128},... | collective-permute-start | bytes 417800 | tf_op jit(solution)/shard_map/ppermute | solution.py:25
  122.9 0.9 collective-permute-done.9.refs_0_
  123.8 0.2 merge.21
  123.9 5.6 %collective-permute-start.10 = (s16[136,512]{1,0:T(8,128)(2,1)S(1)}, s16[136,512]{1,0:T(8,128)(2,1)S(1)}, u32[]{:S(2)}, u32[]{:S(2)}) collective-permute-start(s16[136,512]{1,0:T(8,128)(2,1)S(1)} %merge.21), channel_id=1, source_target_pairs={{0,240},{16,0},{32,16},{48,32},{64,48},{80,64},{96,80},{112,96},{1... | collective-permute-start | bytes 417800 | tf_op jit(solution)/shard_map/ppermute | solution.py:25
  129.6 0.2 collective-permute-done.2.refs_0_
  129.8 0.2 merge.15
  130.0 2.0 %collective-permute-start.3 = (s16[136,512]{1,0:T(8,128)(2,1)S(1)}, s16[136,512]{1,0:T(8,128)(2,1)S(1)}, u32[]{:S(2)}, u32[]{:S(2)}) collective-permute-start(s16[136,512]{1,0:T(8,128)(2,1)S(1)} %merge.15), channel_id=1, source_target_pairs={{0,16},{16,32},{32,48},{48,64},{64,80},{80,96},{96,112},{112,128},... | collective-permute-start | bytes 417800 | tf_op jit(solution)/shard_map/ppermute | solution.py:25
  131.9 0.2 collective-permute-done.10.refs_0_
  132.2 0.2 merge.22
  132.3 5.6 %collective-permute-start.11 = (s16[136,512]{1,0:T(8,128)(2,1)S(1)}, s16[136,512]{1,0:T(8,128)(2,1)S(1)}, u32[]{:S(2)}, u32[]{:S(2)}) collective-permute-start(s16[136,512]{1,0:T(8,128)(2,1)S(1)} %merge.22), channel_id=1, source_target_pairs={{0,240},{16,0},{32,16},{48,32},{64,48},{80,64},{96,80},{112,96},{1... | collective-permute-start | bytes 417800 | tf_op jit(solution)/shard_map/ppermute | solution.py:25
  138.0 0.2 collective-permute-done.3.refs_0_
  138.2 0.2 merge.16
  138.3 2.0 %collective-permute-start.4 = (s16[136,512]{1,0:T(8,128)(2,1)S(1)}, s16[136,512]{1,0:T(8,128)(2,1)S(1)}, u32[]{:S(2)}, u32[]{:S(2)}) collective-permute-start(s16[136,512]{1,0:T(8,128)(2,1)S(1)} %merge.16), channel_id=1, source_target_pairs={{0,16},{16,32},{32,48},{48,64},{64,80},{80,96},{96,112},{112,128},... | collective-permute-start | bytes 417800 | tf_op jit(solution)/shard_map/ppermute | solution.py:25
  140.3 0.2 collective-permute-done.11.refs_0_
  140.5 0.2 merge.23
  140.7 5.6 %collective-permute-start.12 = (s16[136,512]{1,0:T(8,128)(2,1)S(1)}, s16[136,512]{1,0:T(8,128)(2,1)S(1)}, u32[]{:S(2)}, u32[]{:S(2)}) collective-permute-start(s16[136,512]{1,0:T(8,128)(2,1)S(1)} %merge.23), channel_id=1, source_target_pairs={{0,240},{16,0},{32,16},{48,32},{64,48},{80,64},{96,80},{112,96},{1... | collective-permute-start | bytes 417800 | tf_op jit(solution)/shard_map/ppermute | solution.py:25
  146.3 0.2 collective-permute-done.4.refs_0_
  146.5 0.2 merge.17
  146.7 2.0 %collective-permute-start.5 = (s16[136,512]{1,0:T(8,128)(2,1)S(1)}, s16[136,512]{1,0:T(8,128)(2,1)S(1)}, u32[]{:S(2)}, u32[]{:S(2)}) collective-permute-start(s16[136,512]{1,0:T(8,128)(2,1)S(1)} %merge.17), channel_id=1, source_target_pairs={{0,16},{16,32},{32,48},{48,64},{64,80},{80,96},{96,112},{112,128},... | collective-permute-start | bytes 417800 | tf_op jit(solution)/shard_map/ppermute | solution.py:25
  148.7 0.2 collective-permute-done.12.refs_0_
  148.9 0.2 merge.24
  149.1 5.6 %collective-permute-start.13 = (s16[136,512]{1,0:T(8,128)(2,1)S(1)}, s16[136,512]{1,0:T(8,128)(2,1)S(1)}, u32[]{:S(2)}, u32[]{:S(2)}) collective-permute-start(s16[136,512]{1,0:T(8,128)(2,1)S(1)} %merge.24), channel_id=1, source_target_pairs={{0,240},{16,0},{32,16},{48,32},{64,48},{80,64},{96,80},{112,96},{1... | collective-permute-start | bytes 417800 | tf_op jit(solution)/shard_map/ppermute | solution.py:25
  154.7 0.0 copy-done.1
  154.7 0.0 copy-done.2
  154.7 0.7 own_kv.1
  155.4 0.0 collective-permute-done.5.refs_0_
  155.4 0.2 merge.18
  155.6 2.0 %collective-permute-start.6 = (s16[136,512]{1,0:T(8,128)(2,1)S(1)}, s16[136,512]{1,0:T(8,128)(2,1)S(1)}, u32[]{:S(2)}, u32[]{:S(2)}) collective-permute-start(s16[136,512]{1,0:T(8,128)(2,1)S(1)} %merge.18), channel_id=1, source_target_pairs={{0,16},{16,32},{32,48},{48,64},{64,80},{80,96},{96,112},{112,128},... | collective-permute-start | bytes 417800 | tf_op jit(solution)/shard_map/ppermute | solution.py:25
  157.6 0.0 collective-permute-done.13.refs_0_
  157.6 0.2 merge.25
  157.8 5.3 %collective-permute-start.14 = (s16[136,512]{1,0:T(8,128)(2,1)S(1)}, s16[136,512]{1,0:T(8,128)(2,1)S(1)}, u32[]{:S(2)}, u32[]{:S(2)}) collective-permute-start(s16[136,512]{1,0:T(8,128)(2,1)S(1)} %merge.25), channel_id=1, source_target_pairs={{0,240},{16,0},{32,16},{48,32},{64,48},{80,64},{96,80},{112,96},{1... | collective-permute-start | bytes 417800 | tf_op jit(solution)/shard_map/ppermute | solution.py:25
  163.1 0.6 convert_bitcast_fusion
  163.7 0.1 collective-permute-done.6.right
  163.8 1.8 %collective-permute-done.14.left = s16[136,512]{1,0:T(8,128)(2,1)S(1)} collective-permute-done((s16[136,512]{1,0:T(8,128)(2,1)S(1)}, s16[136,512]{1,0:T(8,128)(2,1)S(1)}, u32[]{:S(2)}, u32[]{:S(2)}) %collective-permute-start.14) | collective-permute-done | bytes 139296 | tf_op jit(solution)/shard_map/ppermute | solution.py:25
  165.6 1.4 finish.1
  (1 shorter events, 0.0 us)
Async XLA Ops:
  89.3 0.7 copy-start.4
  89.3 0.7 copy-start.5
  89.3 0.8 copy-start
  89.3 1.9 %copy-start.3 = (bf16[8,768,256]{2,1,0:T(8,128)(2,1)S(1)}, bf16[8,768,256]{2,1,0:T(8,128)(2,1)}, u32[]{:S(2)}) copy-start(bf16[8,768,256]{2,1,0:T(8,128)(2,1)} %kv_ref.1) | copy-start | bytes 9437188
  100.2 54.5 %copy-start.1 = (s32[8]{0:T(128)S(1)}, s32[8]{0:T(128)}, u32[]{:S(2)}) copy-start(s32[8]{0:T(128)} %span.3) | copy-start | bytes 100
  100.2 54.5 %copy-start.2 = (s32[8]{0:T(128)S(1)}, s32[8]{0:T(128)}, u32[]{:S(2)}) copy-start(s32[8]{0:T(128)} %owner.1) | copy-start | bytes 100
  100.2 7.0 %collective-permute-start.7 = (s16[136,512]{1,0:T(8,128)(2,1)S(1)}, s16[136,512]{1,0:T(8,128)(2,1)S(1)}, u32[]{:S(2)}, u32[]{:S(2)}) collective-permute-start(s16[136,512]{1,0:T(8,128)(2,1)S(1)} %get-tuple-element.26), channel_id=1, source_target_pairs={{0,240},{16,0},{32,16},{48,32},{64,48},{80,64},{96,80},{112,96},{1... | collective-permute-start | bytes 417800 | tf_op jit(solution)/shard_map/ppermute | solution.py:25
  102.6 8.4 %collective-permute-start = (s16[136,512]{1,0:T(8,128)(2,1)S(1)}, s16[136,512]{1,0:T(8,128)(2,1)S(1)}, u32[]{:S(2)}, u32[]{:S(2)}) collective-permute-start(s16[136,512]{1,0:T(8,128)(2,1)S(1)} %get-tuple-element.19), channel_id=1, source_target_pairs={{0,16},{16,32},{32,48},{48,64},{64,80},{80,96},{96,112},{112,128},... | collective-permute-start | bytes 417800 | tf_op jit(solution)/shard_map/ppermute | solution.py:25
  107.3 7.4 %collective-permute-start.8 = (s16[136,512]{1,0:T(8,128)(2,1)S(1)}, s16[136,512]{1,0:T(8,128)(2,1)S(1)}, u32[]{:S(2)}, u32[]{:S(2)}) collective-permute-start(s16[136,512]{1,0:T(8,128)(2,1)S(1)} %merge.19), channel_id=1, source_target_pairs={{0,240},{16,0},{32,16},{48,32},{64,48},{80,64},{96,80},{112,96},{1... | collective-permute-start | bytes 417800 | tf_op jit(solution)/shard_map/ppermute | solution.py:25
  111.2 9.6 %collective-permute-start.1 = (s16[136,512]{1,0:T(8,128)(2,1)S(1)}, s16[136,512]{1,0:T(8,128)(2,1)S(1)}, u32[]{:S(2)}, u32[]{:S(2)}) collective-permute-start(s16[136,512]{1,0:T(8,128)(2,1)S(1)} %merge.13), channel_id=1, source_target_pairs={{0,16},{16,32},{32,48},{48,64},{64,80},{80,96},{96,112},{112,128},... | collective-permute-start | bytes 417800 | tf_op jit(solution)/shard_map/ppermute | solution.py:25
  114.9 8.8 %collective-permute-start.9 = (s16[136,512]{1,0:T(8,128)(2,1)S(1)}, s16[136,512]{1,0:T(8,128)(2,1)S(1)}, u32[]{:S(2)}, u32[]{:S(2)}) collective-permute-start(s16[136,512]{1,0:T(8,128)(2,1)S(1)} %merge.20), channel_id=1, source_target_pairs={{0,240},{16,0},{32,16},{48,32},{64,48},{80,64},{96,80},{112,96},{1... | collective-permute-start | bytes 417800 | tf_op jit(solution)/shard_map/ppermute | solution.py:25
  121.0 8.8 %collective-permute-start.2 = (s16[136,512]{1,0:T(8,128)(2,1)S(1)}, s16[136,512]{1,0:T(8,128)(2,1)S(1)}, u32[]{:S(2)}, u32[]{:S(2)}) collective-permute-start(s16[136,512]{1,0:T(8,128)(2,1)S(1)} %merge.14), channel_id=1, source_target_pairs={{0,16},{16,32},{32,48},{48,64},{64,80},{80,96},{96,112},{112,128},... | collective-permute-start | bytes 417800 | tf_op jit(solution)/shard_map/ppermute | solution.py:25
  123.9 8.2 %collective-permute-start.10 = (s16[136,512]{1,0:T(8,128)(2,1)S(1)}, s16[136,512]{1,0:T(8,128)(2,1)S(1)}, u32[]{:S(2)}, u32[]{:S(2)}) collective-permute-start(s16[136,512]{1,0:T(8,128)(2,1)S(1)} %merge.21), channel_id=1, source_target_pairs={{0,240},{16,0},{32,16},{48,32},{64,48},{80,64},{96,80},{112,96},{1... | collective-permute-start | bytes 417800 | tf_op jit(solution)/shard_map/ppermute | solution.py:25
  130.0 8.2 %collective-permute-start.3 = (s16[136,512]{1,0:T(8,128)(2,1)S(1)}, s16[136,512]{1,0:T(8,128)(2,1)S(1)}, u32[]{:S(2)}, u32[]{:S(2)}) collective-permute-start(s16[136,512]{1,0:T(8,128)(2,1)S(1)} %merge.15), channel_id=1, source_target_pairs={{0,16},{16,32},{32,48},{48,64},{64,80},{80,96},{96,112},{112,128},... | collective-permute-start | bytes 417800 | tf_op jit(solution)/shard_map/ppermute | solution.py:25
  132.3 8.2 %collective-permute-start.11 = (s16[136,512]{1,0:T(8,128)(2,1)S(1)}, s16[136,512]{1,0:T(8,128)(2,1)S(1)}, u32[]{:S(2)}, u32[]{:S(2)}) collective-permute-start(s16[136,512]{1,0:T(8,128)(2,1)S(1)} %merge.22), channel_id=1, source_target_pairs={{0,240},{16,0},{32,16},{48,32},{64,48},{80,64},{96,80},{112,96},{1... | collective-permute-start | bytes 417800 | tf_op jit(solution)/shard_map/ppermute | solution.py:25
  138.3 8.2 %collective-permute-start.4 = (s16[136,512]{1,0:T(8,128)(2,1)S(1)}, s16[136,512]{1,0:T(8,128)(2,1)S(1)}, u32[]{:S(2)}, u32[]{:S(2)}) collective-permute-start(s16[136,512]{1,0:T(8,128)(2,1)S(1)} %merge.16), channel_id=1, source_target_pairs={{0,16},{16,32},{32,48},{48,64},{64,80},{80,96},{96,112},{112,128},... | collective-permute-start | bytes 417800 | tf_op jit(solution)/shard_map/ppermute | solution.py:25
  140.7 8.2 %collective-permute-start.12 = (s16[136,512]{1,0:T(8,128)(2,1)S(1)}, s16[136,512]{1,0:T(8,128)(2,1)S(1)}, u32[]{:S(2)}, u32[]{:S(2)}) collective-permute-start(s16[136,512]{1,0:T(8,128)(2,1)S(1)} %merge.23), channel_id=1, source_target_pairs={{0,240},{16,0},{32,16},{48,32},{64,48},{80,64},{96,80},{112,96},{1... | collective-permute-start | bytes 417800 | tf_op jit(solution)/shard_map/ppermute | solution.py:25
  146.7 8.7 %collective-permute-start.5 = (s16[136,512]{1,0:T(8,128)(2,1)S(1)}, s16[136,512]{1,0:T(8,128)(2,1)S(1)}, u32[]{:S(2)}, u32[]{:S(2)}) collective-permute-start(s16[136,512]{1,0:T(8,128)(2,1)S(1)} %merge.17), channel_id=1, source_target_pairs={{0,16},{16,32},{32,48},{48,64},{64,80},{80,96},{96,112},{112,128},... | collective-permute-start | bytes 417800 | tf_op jit(solution)/shard_map/ppermute | solution.py:25
  149.1 8.5 %collective-permute-start.13 = (s16[136,512]{1,0:T(8,128)(2,1)S(1)}, s16[136,512]{1,0:T(8,128)(2,1)S(1)}, u32[]{:S(2)}, u32[]{:S(2)}) collective-permute-start(s16[136,512]{1,0:T(8,128)(2,1)S(1)} %merge.24), channel_id=1, source_target_pairs={{0,240},{16,0},{32,16},{48,32},{64,48},{80,64},{96,80},{112,96},{1... | collective-permute-start | bytes 417800 | tf_op jit(solution)/shard_map/ppermute | solution.py:25
  155.6 8.2 %collective-permute-start.6 = (s16[136,512]{1,0:T(8,128)(2,1)S(1)}, s16[136,512]{1,0:T(8,128)(2,1)S(1)}, u32[]{:S(2)}, u32[]{:S(2)}) collective-permute-start(s16[136,512]{1,0:T(8,128)(2,1)S(1)} %merge.18), channel_id=1, source_target_pairs={{0,16},{16,32},{32,48},{48,64},{64,80},{80,96},{96,112},{112,128},... | collective-permute-start | bytes 417800 | tf_op jit(solution)/shard_map/ppermute | solution.py:25
  157.8 7.9 %collective-permute-start.14 = (s16[136,512]{1,0:T(8,128)(2,1)S(1)}, s16[136,512]{1,0:T(8,128)(2,1)S(1)}, u32[]{:S(2)}, u32[]{:S(2)}) collective-permute-start(s16[136,512]{1,0:T(8,128)(2,1)S(1)} %merge.25), channel_id=1, source_target_pairs={{0,240},{16,0},{32,16},{48,32},{64,48},{80,64},{96,80},{112,96},{1... | collective-permute-start | bytes 417800 | tf_op jit(solution)/shard_map/ppermute | solution.py:25
